TPU v7x, 32 devices: a whole 2x2x4 slice. The times are simulated.
32 devices in a mesh: dp: 2 (over x), sp: 4 (over z), tp: 4 (over y, core).
Axes of the slice: x: 2, y: 2, z: 4, core: 2. Of those that a mesh axis runs over, the one named last changes fastest.
Arguments:
- x_in: bfloat16 [32768, 4096], P(('dp', 'sp', 'tp')), parts along dimension 0
- seg_ids: int32 [32768], P(('dp', 'sp', 'tp')), parts along dimension 0
- w_zx: bfloat16 [4096, 2, 8192], P(None, None, 'tp')
- w_bc: bfloat16 [4096, 2, 1024], P(None, None, 'tp')
- w_dt: bfloat16 [4096, 128], P(None, 'tp')
- conv_x: bfloat16 [4, 8192], P(None, 'tp')
- conv_bc: bfloat16 [4, 2, 1024], P(None, None, 'tp')
- bias_x: bfloat16 [8192], P('tp')
- bias_bc: bfloat16 [2, 1024], P(None, 'tp')
- a_log: float32 [128], P('tp')
- dt_bias: float32 [128], P('tp')
- d_skip: float32 [128], P('tp')
- norm_w: bfloat16 [8192], P('tp')
- w_out: bfloat16 [8192, 4096], P('tp')
Outputs:
- output: bfloat16 [32768, 4096], P(('dp', 'sp', 'tp')), parts along dimension 0
There are 2 independent parts. A program takes and returns all parts, laid end to end along the dimension named above; an argument that names none is the same for every part.
All inputs are finite; a program needn't handle non-finite values.
Results may differ from a plain program's by a relative error of at most 0.00663.
Values are sent between devices in bfloat16 or wider.
A program may use at most 1 GiB of HBM per device.

v0:
```python
import math
import jax
import jax.numpy as jnp
from jax import lax
from jax.sharding import PartitionSpec as P

SSD_TILE = 256
CONV_WIDTH = 4
STATE_DIM = 128
NORM_EPS = 1e-5


def causal_conv(pre_rows, tail_rows, seg_rows, seg_tail, conv_w, conv_b):
    row_count = pre_rows.shape[0]
    padded = jnp.concatenate([tail_rows, pre_rows], axis=0)
    seg_pad = jnp.concatenate([seg_tail, seg_rows], axis=0)
    conv_acc = conv_b.astype(jnp.float32)
    for tap_idx in range(CONV_WIDTH):
        keep_tap = (seg_pad[tap_idx:tap_idx + row_count] == seg_rows)[:, None]
        tap_term = padded[tap_idx:tap_idx + row_count].astype(jnp.float32) * conv_w[tap_idx].astype(jnp.float32)
        conv_acc = conv_acc + jnp.where(keep_tap, tap_term, 0.0)
    return jax.nn.silu(conv_acc).astype(jnp.bfloat16)


def ssd_tile(state, tile_in, skip_gain):
    x_ssm, b_ssm, c_ssm, dt_val, log_a, seg_rows, seg_prev = tile_in
    row_count = x_ssm.shape[0]
    last_row = row_count - 1
    cum_log = jnp.cumsum(log_a, axis=0)
    causal = jnp.arange(row_count)[:, None] >= jnp.arange(row_count)[None, :]
    same_doc = ((seg_rows[:, None] == seg_rows[None, :]) & causal)[:, :, None, None]
    decay = jnp.where(same_doc, jnp.exp(jnp.where(same_doc, cum_log[:, None] - cum_log[None, :], 0.0)), 0.0)
    scores = jnp.einsum('tgn,sgn->tsg', c_ssm, b_ssm, preferred_element_type=jnp.float32)
    mix_mat = scores[..., None] * decay * dt_val[None]
    y_ssm = jnp.einsum('tsgr,sgrp->tgrp', mix_mat, x_ssm, preferred_element_type=jnp.float32)
    keep_in = (seg_rows == seg_prev)[:, None, None]
    in_fac = jnp.where(keep_in, jnp.exp(cum_log), 0.0)
    y_ssm = y_ssm + jnp.einsum('tgn,grpn->tgrp', c_ssm, state, preferred_element_type=jnp.float32) * in_fac[..., None]
    y_ssm = y_ssm + skip_gain[None, :, :, None] * x_ssm.astype(jnp.float32)
    keep_end = (seg_rows == seg_rows[last_row])[:, None, None]
    end_w = jnp.where(keep_end, jnp.exp(cum_log[last_row][None] - cum_log), 0.0) * dt_val
    carry_fac = jnp.where(seg_rows[last_row] == seg_prev, jnp.exp(cum_log[last_row]), 0.0)
    new_state = carry_fac[:, :, None, None] * state + jnp.einsum('sgrp,sgn->grpn', x_ssm * end_w[..., None], b_ssm, preferred_element_type=jnp.float32)
    return new_state, y_ssm


def block_ssd(x_ssm, b_ssm, c_ssm, dt_val, log_a, seg_rows, seg_prev, skip_gain):
    row_count, groups, per_group, head_dim = x_ssm.shape
    tile_size = math.gcd(row_count, SSD_TILE)
    n_tiles = row_count // tile_size
    seg_shift = jnp.concatenate([seg_prev[None], seg_rows[:-1]])
    tile_prev = seg_shift.reshape(n_tiles, tile_size)[:, 0]
    tiles_in = (x_ssm.reshape(n_tiles, tile_size, groups, per_group, head_dim), b_ssm.reshape(n_tiles, tile_size, groups, STATE_DIM), c_ssm.reshape(n_tiles, tile_size, groups, STATE_DIM), dt_val.reshape(n_tiles, tile_size, groups, per_group), log_a.reshape(n_tiles, tile_size, groups, per_group), seg_rows.reshape(n_tiles, tile_size), tile_prev)

    def body(state, step_in):
        return ssd_tile(state, step_in, skip_gain)

    init_state = jnp.zeros((groups, per_group, head_dim, STATE_DIM), jnp.float32)
    end_state, y_tiles = lax.scan(body, init_state, tiles_in)
    return end_state, y_tiles.reshape(row_count, groups, per_group, head_dim)


def gate_norm(y_ssm, z_gate, norm_w):
    row_count, groups, per_group, head_dim = y_ssm.shape
    group_size = per_group * head_dim
    gated = y_ssm.reshape(row_count, groups, group_size) * jax.nn.silu(z_gate.astype(jnp.float32)).reshape(row_count, groups, group_size)
    normed = gated * lax.rsqrt(jnp.mean(gated * gated, axis=-1, keepdims=True) + NORM_EPS)
    return (normed.reshape(row_count, groups * group_size) * norm_w.astype(jnp.float32)).astype(jnp.bfloat16)


def chain_state(end_state, block_decay, seq_axis, n_blocks):
    dev_index = lax.axis_index(seq_axis)
    to_next = [(src_dev, src_dev + 1) for src_dev in range(n_blocks - 1)]
    state_in = lax.ppermute(end_state, seq_axis, to_next)
    decay_in = jnp.where(dev_index == 0, 1.0, lax.ppermute(block_decay, seq_axis, to_next))
    for step_idx in range((n_blocks - 1).bit_length()):
        hop_span = 2 ** step_idx
        hop_perm = [(src_dev, src_dev + hop_span) for src_dev in range(n_blocks - hop_span)]
        prev_state = lax.ppermute(state_in, seq_axis, hop_perm)
        prev_decay = lax.ppermute(decay_in, seq_axis, hop_perm)
        has_prev = dev_index >= hop_span
        state_in = jnp.where(has_prev, decay_in[:, :, None, None] * prev_state + state_in, state_in)
        decay_in = jnp.where(has_prev, decay_in * prev_decay, decay_in)
    return state_in


def local_layer(x_blk, seg_blk, weights, seq_axis, n_blocks):
    w_zx, w_bc, w_dt, conv_x, conv_bc, bias_x, bias_bc, a_log, dt_bias, d_skip, norm_w, w_out = weights
    row_count = x_blk.shape[0]
    inner_dim = w_zx.shape[2]
    group_width = w_bc.shape[2]
    heads = w_dt.shape[1]
    groups = group_width // STATE_DIM
    per_group = heads // groups
    head_dim = inner_dim // heads
    halo_len = CONV_WIDTH - 1
    zx_proj = jnp.einsum('ld,dkc->lkc', x_blk, w_zx, preferred_element_type=jnp.float32).astype(jnp.bfloat16)
    bc_pre = jnp.einsum('ld,dkc->lkc', x_blk, w_bc, preferred_element_type=jnp.float32).astype(jnp.bfloat16).reshape(row_count, 2 * group_width)
    dt_raw = jnp.dot(x_blk, w_dt, preferred_element_type=jnp.float32).astype(jnp.bfloat16)
    x_pre = zx_proj[:, 1]
    to_next = [(src_dev, src_dev + 1) for src_dev in range(n_blocks - 1)]
    tail_x = lax.ppermute(x_pre[row_count - halo_len:], seq_axis, to_next)
    tail_bc = lax.ppermute(bc_pre[row_count - halo_len:], seq_axis, to_next)
    tail_seg = lax.ppermute(seg_blk[row_count - halo_len:], seq_axis, to_next)
    x_act = causal_conv(x_pre, tail_x, seg_blk, tail_seg, conv_x, bias_x)
    bc_act = causal_conv(bc_pre, tail_bc, seg_blk, tail_seg, conv_bc.reshape(CONV_WIDTH, 2 * group_width), bias_bc.reshape(2 * group_width))
    x_ssm = x_act.reshape(row_count, groups, per_group, head_dim)
    b_ssm = bc_act[:, :group_width].reshape(row_count, groups, STATE_DIM)
    c_ssm = bc_act[:, group_width:].reshape(row_count, groups, STATE_DIM)
    dt_val = jax.nn.softplus(dt_raw.astype(jnp.float32) + dt_bias).reshape(row_count, groups, per_group)
    log_a = -jnp.exp(a_log).reshape(groups, per_group) * dt_val
    seg_prev = tail_seg[halo_len - 1]
    end_state, y_local = block_ssd(x_ssm, b_ssm, c_ssm, dt_val, log_a, seg_blk, seg_prev, d_skip.reshape(groups, per_group))
    cum_blk = jnp.cumsum(log_a, axis=0)
    block_decay = jnp.where(seg_blk[row_count - 1] == seg_prev, jnp.exp(cum_blk[row_count - 1]), 0.0)
    state_in = chain_state(end_state, block_decay, seq_axis, n_blocks)
    keep_blk = (seg_blk == seg_prev)[:, None, None]
    corr_fac = jnp.where(keep_blk, jnp.exp(cum_blk), 0.0)
    y_ssm = y_local + jnp.einsum('tgn,grpn->tgrp', c_ssm, state_in, preferred_element_type=jnp.float32) * corr_fac[..., None]
    y_norm = gate_norm(y_ssm, zx_proj[:, 0], norm_w)
    return jnp.dot(y_norm, w_out, preferred_element_type=jnp.float32)


def solution(mesh):
    seq_blocks = mesh.shape['sp']
    token_spec = P(('dp', 'sp', 'tp'), None)
    seg_spec = P(('dp', 'sp', 'tp'))
    weight_specs = (P(None, None, 'tp'), P(None, None, 'tp'), P(None, 'tp'), P(None, 'tp'), P(None, None, 'tp'), P('tp'), P(None, 'tp'), P('tp'), P('tp'), P('tp'), P('tp'), P('tp', None))

    def body(x_loc, seg_loc, w_zx, w_bc, w_dt, conv_x, conv_bc, bias_x, bias_bc, a_log, dt_bias, d_skip, norm_w, w_out):
        x_blk = lax.all_gather(x_loc, 'tp', axis=0, tiled=True)
        seg_blk = lax.all_gather(seg_loc, 'tp', axis=0, tiled=True)
        weights = (w_zx, w_bc, w_dt, conv_x, conv_bc, bias_x, bias_bc, a_log, dt_bias, d_skip, norm_w, w_out)
        out_part = local_layer(x_blk, seg_blk, weights, 'sp', seq_blocks)
        out_loc = lax.psum_scatter(out_part, 'tp', scatter_dimension=0, tiled=True)
        return (x_loc.astype(jnp.float32) + out_loc).astype(jnp.bfloat16)

    return jax.shard_map(body, mesh=mesh, in_specs=(token_spec, seg_spec) + weight_specs, out_specs=token_spec, check_vma=False)
```

profile of v0, /device:TPU:0, one launch (start us, length us, event | category | flops | bytes accessed | tf_op | source)
XLA Modules:
  0.0 2503.4 jit_solution(1615190604969459717)
XLA Ops:
  29.6 184.2 %all-gather.2.cloned.1.call-done = bf16[4096,4096]{1,0:T(8,128)(2,1)} async-done(((bf16[1024,4096]{1,0:T(8,128)(2,1)}), bf16[4096,4096]{1,0:T(8,128)(2,1)}) %all-gather.2.cloned.1.call-update) | async-done | bytes 33554448 | tf_op jit(solution)/shard_map/all_gather | solution.py:131
  213.8 152.5 %fusion.57 = bf16[4096,2,2048]{2,0,1:T(8,128)(2,1)} fusion(bf16[4096,2,2048]{2,1,0:T(2,128)(2,1)} %param.18, bf16[4096,4096]{1,0:T(8,128)(2,1)} %all-gather.2.cloned.1.call-done), kind=kOutput, calls=%fused_computation.79 | convolution fusion | flops 137455730688 | bytes 100663296 | tf_op jit(solution)/shard_map/ld,dkc->lkc/dot_general | solution.py:97
  479.5 43.1 %multiply_convert_fusion = bf16[4096,2048]{1,0:T(8,128)(2,1)} fusion(bf16[4096,2048]{1,0:T(8,128)(2,1)} %get-tuple-element.173, bf16[3,2048]{1,0:T(4,128)(2,1)S(1)} %collective-permute-done.1, f32[2048]{0:T(1024)S(1)} %bitcast.247, f32[2048]{0:T(1024)S(1)} %bitcast.248, f32[2048]{0:T(1024)S(1)} %bitcast.246, f32[2048]{0:T(1024)S(1)} %bitcast.245, ...), kind=kLoop, calls=%fused_computation.75 | loop fusion | flops 243269632 | bytes 33619968 | tf_op jit(solution)/shard_map/convert_element_type | solution.py:22
  522.5 47.8 %reshape.226 = bf16[16,256,2,16,64]{4,3,2,1,0:T(8,128)(2,1)} reshape(bf16[4096,2048]{1,0:T(8,128)(2,1)} %multiply_convert_fusion) | data formatting | bytes 33554432 | tf_op jit(solution)/shard_map/reshape;reshape | solution.py:53
  570.3 37.6 %copy.93 = bf16[16,256,2,16,64]{1,4,3,2,0:T(8,128)(2,1)} copy(bf16[16,256,2,16,64]{4,3,2,1,0:T(8,128)(2,1)} %reshape.226) | data formatting | bytes 33554432
  608.0 1082.0 %while.13 = (s32[]{:T(128)}, f32[2,16,64,128]{3,2,1,0:T(8,128)S(1)}, f32[16,256,2,16,64]{1,0,4,3,2:T(8,128)}, s32[16,256]{1,0:T(8,128)}, s32[16]{0:T(128)S(1)}, ...) while((s32[]{:T(128)}, ...), condition=%wide.region_3.4_spmd.clone, body=%wide.region_0.3_spmd.clone.sunk | while | flops 586916480 | bytes 24262512 | solution.py:59
  628.1 47.6 %dynamic_update_slice.6 = f32[16,256,2,16,64]{1,0,4,3,2:T(8,128)} dynamic-update-slice(f32[16,256,2,16,64]{1,0,4,3,2:T(8,128)} %get-tuple-element.286, f32[1,256,2,16,64]{1,0,4,3,2:T(1,128)S(1)} %copy.160, s32[]{:T(128)S(6)} %copy.165, s32[]{:T(128)} %constant.33.clone.1..sunk, s32[]{:T(128)} %constant.33.clone.1..sunk, s32[]{:T(128)} %constant.33.clone.1..sunk, s32[]{:T(128)} %constant.33.clone.1..sunk) | dynamic-update-slice | bytes 4194308 | tf_op jit(solution)/shard_map/while/body/jit(dynamic_update_index_in_dim)/dynamic_update_slice | solution.py:59
  695.8 47.6 %dynamic_update_slice.6 = f32[16,256,2,16,64]{1,0,4,3,2:T(8,128)} dynamic-update-slice(f32[16,256,2,16,64]{1,0,4,3,2:T(8,128)} %get-tuple-element.286, f32[1,256,2,16,64]{1,0,4,3,2:T(1,128)S(1)} %copy.160, s32[]{:T(128)S(6)} %copy.165, s32[]{:T(128)} %constant.33.clone.1..sunk, s32[]{:T(128)} %constant.33.clone.1..sunk, s32[]{:T(128)} %constant.33.clone.1..sunk, s32[]{:T(128)} %constant.33.clone.1..sunk) | dynamic-update-slice | bytes 4194308 | tf_op jit(solution)/shard_map/while/body/jit(dynamic_update_index_in_dim)/dynamic_update_slice | solution.py:59
  763.4 47.6 %dynamic_update_slice.6 = f32[16,256,2,16,64]{1,0,4,3,2:T(8,128)} dynamic-update-slice(f32[16,256,2,16,64]{1,0,4,3,2:T(8,128)} %get-tuple-element.286, f32[1,256,2,16,64]{1,0,4,3,2:T(1,128)S(1)} %copy.160, s32[]{:T(128)S(6)} %copy.165, s32[]{:T(128)} %constant.33.clone.1..sunk, s32[]{:T(128)} %constant.33.clone.1..sunk, s32[]{:T(128)} %constant.33.clone.1..sunk, s32[]{:T(128)} %constant.33.clone.1..sunk) | dynamic-update-slice | bytes 4194308 | tf_op jit(solution)/shard_map/while/body/jit(dynamic_update_index_in_dim)/dynamic_update_slice | solution.py:59
  831.0 47.6 %dynamic_update_slice.6 = f32[16,256,2,16,64]{1,0,4,3,2:T(8,128)} dynamic-update-slice(f32[16,256,2,16,64]{1,0,4,3,2:T(8,128)} %get-tuple-element.286, f32[1,256,2,16,64]{1,0,4,3,2:T(1,128)S(1)} %copy.160, s32[]{:T(128)S(6)} %copy.165, s32[]{:T(128)} %constant.33.clone.1..sunk, s32[]{:T(128)} %constant.33.clone.1..sunk, s32[]{:T(128)} %constant.33.clone.1..sunk, s32[]{:T(128)} %constant.33.clone.1..sunk) | dynamic-update-slice | bytes 4194308 | tf_op jit(solution)/shard_map/while/body/jit(dynamic_update_index_in_dim)/dynamic_update_slice | solution.py:59
  898.6 47.6 %dynamic_update_slice.6 = f32[16,256,2,16,64]{1,0,4,3,2:T(8,128)} dynamic-update-slice(f32[16,256,2,16,64]{1,0,4,3,2:T(8,128)} %get-tuple-element.286, f32[1,256,2,16,64]{1,0,4,3,2:T(1,128)S(1)} %copy.160, s32[]{:T(128)S(6)} %copy.165, s32[]{:T(128)} %constant.33.clone.1..sunk, s32[]{:T(128)} %constant.33.clone.1..sunk, s32[]{:T(128)} %constant.33.clone.1..sunk, s32[]{:T(128)} %constant.33.clone.1..sunk) | dynamic-update-slice | bytes 4194308 | tf_op jit(solution)/shard_map/while/body/jit(dynamic_update_index_in_dim)/dynamic_update_slice | solution.py:59
  966.3 47.6 %dynamic_update_slice.6 = f32[16,256,2,16,64]{1,0,4,3,2:T(8,128)} dynamic-update-slice(f32[16,256,2,16,64]{1,0,4,3,2:T(8,128)} %get-tuple-element.286, f32[1,256,2,16,64]{1,0,4,3,2:T(1,128)S(1)} %copy.160, s32[]{:T(128)S(6)} %copy.165, s32[]{:T(128)} %constant.33.clone.1..sunk, s32[]{:T(128)} %constant.33.clone.1..sunk, s32[]{:T(128)} %constant.33.clone.1..sunk, s32[]{:T(128)} %constant.33.clone.1..sunk) | dynamic-update-slice | bytes 4194308 | tf_op jit(solution)/shard_map/while/body/jit(dynamic_update_index_in_dim)/dynamic_update_slice | solution.py:59
  1033.9 47.6 %dynamic_update_slice.6 = f32[16,256,2,16,64]{1,0,4,3,2:T(8,128)} dynamic-update-slice(f32[16,256,2,16,64]{1,0,4,3,2:T(8,128)} %get-tuple-element.286, f32[1,256,2,16,64]{1,0,4,3,2:T(1,128)S(1)} %copy.160, s32[]{:T(128)S(6)} %copy.165, s32[]{:T(128)} %constant.33.clone.1..sunk, s32[]{:T(128)} %constant.33.clone.1..sunk, s32[]{:T(128)} %constant.33.clone.1..sunk, s32[]{:T(128)} %constant.33.clone.1..sunk) | dynamic-update-slice | bytes 4194308 | tf_op jit(solution)/shard_map/while/body/jit(dynamic_update_index_in_dim)/dynamic_update_slice | solution.py:59
  1101.5 47.6 %dynamic_update_slice.6 = f32[16,256,2,16,64]{1,0,4,3,2:T(8,128)} dynamic-update-slice(f32[16,256,2,16,64]{1,0,4,3,2:T(8,128)} %get-tuple-element.286, f32[1,256,2,16,64]{1,0,4,3,2:T(1,128)S(1)} %copy.160, s32[]{:T(128)S(6)} %copy.165, s32[]{:T(128)} %constant.33.clone.1..sunk, s32[]{:T(128)} %constant.33.clone.1..sunk, s32[]{:T(128)} %constant.33.clone.1..sunk, s32[]{:T(128)} %constant.33.clone.1..sunk) | dynamic-update-slice | bytes 4194308 | tf_op jit(solution)/shard_map/while/body/jit(dynamic_update_index_in_dim)/dynamic_update_slice | solution.py:59
  1169.1 47.5 %dynamic_update_slice.6 = f32[16,256,2,16,64]{1,0,4,3,2:T(8,128)} dynamic-update-slice(f32[16,256,2,16,64]{1,0,4,3,2:T(8,128)} %get-tuple-element.286, f32[1,256,2,16,64]{1,0,4,3,2:T(1,128)S(1)} %copy.160, s32[]{:T(128)S(6)} %copy.165, s32[]{:T(128)} %constant.33.clone.1..sunk, s32[]{:T(128)} %constant.33.clone.1..sunk, s32[]{:T(128)} %constant.33.clone.1..sunk, s32[]{:T(128)} %constant.33.clone.1..sunk) | dynamic-update-slice | bytes 4194308 | tf_op jit(solution)/shard_map/while/body/jit(dynamic_update_index_in_dim)/dynamic_update_slice | solution.py:59
  1236.7 47.5 %dynamic_update_slice.6 = f32[16,256,2,16,64]{1,0,4,3,2:T(8,128)} dynamic-update-slice(f32[16,256,2,16,64]{1,0,4,3,2:T(8,128)} %get-tuple-element.286, f32[1,256,2,16,64]{1,0,4,3,2:T(1,128)S(1)} %copy.160, s32[]{:T(128)S(6)} %copy.165, s32[]{:T(128)} %constant.33.clone.1..sunk, s32[]{:T(128)} %constant.33.clone.1..sunk, s32[]{:T(128)} %constant.33.clone.1..sunk, s32[]{:T(128)} %constant.33.clone.1..sunk) | dynamic-update-slice | bytes 4194308 | tf_op jit(solution)/shard_map/while/body/jit(dynamic_update_index_in_dim)/dynamic_update_slice | solution.py:59
  1304.2 47.5 %dynamic_update_slice.6 = f32[16,256,2,16,64]{1,0,4,3,2:T(8,128)} dynamic-update-slice(f32[16,256,2,16,64]{1,0,4,3,2:T(8,128)} %get-tuple-element.286, f32[1,256,2,16,64]{1,0,4,3,2:T(1,128)S(1)} %copy.160, s32[]{:T(128)S(6)} %copy.165, s32[]{:T(128)} %constant.33.clone.1..sunk, s32[]{:T(128)} %constant.33.clone.1..sunk, s32[]{:T(128)} %constant.33.clone.1..sunk, s32[]{:T(128)} %constant.33.clone.1..sunk) | dynamic-update-slice | bytes 4194308 | tf_op jit(solution)/shard_map/while/body/jit(dynamic_update_index_in_dim)/dynamic_update_slice | solution.py:59
  1371.9 47.5 %dynamic_update_slice.6 = f32[16,256,2,16,64]{1,0,4,3,2:T(8,128)} dynamic-update-slice(f32[16,256,2,16,64]{1,0,4,3,2:T(8,128)} %get-tuple-element.286, f32[1,256,2,16,64]{1,0,4,3,2:T(1,128)S(1)} %copy.160, s32[]{:T(128)S(6)} %copy.165, s32[]{:T(128)} %constant.33.clone.1..sunk, s32[]{:T(128)} %constant.33.clone.1..sunk, s32[]{:T(128)} %constant.33.clone.1..sunk, s32[]{:T(128)} %constant.33.clone.1..sunk) | dynamic-update-slice | bytes 4194308 | tf_op jit(solution)/shard_map/while/body/jit(dynamic_update_index_in_dim)/dynamic_update_slice | solution.py:59
  1439.4 47.5 %dynamic_update_slice.6 = f32[16,256,2,16,64]{1,0,4,3,2:T(8,128)} dynamic-update-slice(f32[16,256,2,16,64]{1,0,4,3,2:T(8,128)} %get-tuple-element.286, f32[1,256,2,16,64]{1,0,4,3,2:T(1,128)S(1)} %copy.160, s32[]{:T(128)S(6)} %copy.165, s32[]{:T(128)} %constant.33.clone.1..sunk, s32[]{:T(128)} %constant.33.clone.1..sunk, s32[]{:T(128)} %constant.33.clone.1..sunk, s32[]{:T(128)} %constant.33.clone.1..sunk) | dynamic-update-slice | bytes 4194308 | tf_op jit(solution)/shard_map/while/body/jit(dynamic_update_index_in_dim)/dynamic_update_slice | solution.py:59
  1507.1 47.5 %dynamic_update_slice.6 = f32[16,256,2,16,64]{1,0,4,3,2:T(8,128)} dynamic-update-slice(f32[16,256,2,16,64]{1,0,4,3,2:T(8,128)} %get-tuple-element.286, f32[1,256,2,16,64]{1,0,4,3,2:T(1,128)S(1)} %copy.160, s32[]{:T(128)S(6)} %copy.165, s32[]{:T(128)} %constant.33.clone.1..sunk, s32[]{:T(128)} %constant.33.clone.1..sunk, s32[]{:T(128)} %constant.33.clone.1..sunk, s32[]{:T(128)} %constant.33.clone.1..sunk) | dynamic-update-slice | bytes 4194308 | tf_op jit(solution)/shard_map/while/body/jit(dynamic_update_index_in_dim)/dynamic_update_slice | solution.py:59
  1574.8 47.5 %dynamic_update_slice.6 = f32[16,256,2,16,64]{1,0,4,3,2:T(8,128)} dynamic-update-slice(f32[16,256,2,16,64]{1,0,4,3,2:T(8,128)} %get-tuple-element.286, f32[1,256,2,16,64]{1,0,4,3,2:T(1,128)S(1)} %copy.160, s32[]{:T(128)S(6)} %copy.165, s32[]{:T(128)} %constant.33.clone.1..sunk, s32[]{:T(128)} %constant.33.clone.1..sunk, s32[]{:T(128)} %constant.33.clone.1..sunk, s32[]{:T(128)} %constant.33.clone.1..sunk) | dynamic-update-slice | bytes 4194308 | tf_op jit(solution)/shard_map/while/body/jit(dynamic_update_index_in_dim)/dynamic_update_slice | solution.py:59
  1642.4 47.5 %dynamic_update_slice.6 = f32[16,256,2,16,64]{1,0,4,3,2:T(8,128)} dynamic-update-slice(f32[16,256,2,16,64]{1,0,4,3,2:T(8,128)} %get-tuple-element.286, f32[1,256,2,16,64]{1,0,4,3,2:T(1,128)S(1)} %copy.160, s32[]{:T(128)S(6)} %copy.165, s32[]{:T(128)} %constant.33.clone.1..sunk, s32[]{:T(128)} %constant.33.clone.1..sunk, s32[]{:T(128)} %constant.33.clone.1..sunk, s32[]{:T(128)} %constant.33.clone.1..sunk) | dynamic-update-slice | bytes 4194308 | tf_op jit(solution)/shard_map/while/body/jit(dynamic_update_index_in_dim)/dynamic_update_slice | solution.py:59
  1951.3 89.2 %fusion.64 = f32[4096,4096]{1,0:T(8,128)} fusion(bf16[2048,4096]{1,0:T(8,128)(2,1)} %param.29, f32[4096,2048]{1,0:T(8,128)} %bitcast.226, f32[4096,2048]{1,0:T(8,128)} %copy.104, f32[2048]{0:T(1024)S(1)} %convert_element_type.163, bf16[4096,2,2048]{2,0,1:T(8,128)(2,1)} %fusion.57), kind=kOutput, calls=%fused_computation.82 | convolution fusion | flops 68794974208 | bytes 167780352 | tf_op jit(solution)/shard_map/dot_general | solution.py:121
  2040.6 443.5 %reduce-scatter.4.cloned.1.call-done = f32[1024,4096]{1,0:T(8,128)} async-done(((f32[4096,4096]{1,0:T(8,128)}), f32[1024,4096]{1,0:T(8,128)}) %reduce-scatter.4.cloned.1.call-update) | async-done | bytes 16777232
  (505 shorter events, 706.5 us)
Async XLA Ops:
  6.5 390.1 %copy-start = (bf16[4096,32]{0,1:T(8,128)(2,1)S(1)}, bf16[4096,32]{0,1:T(8,128)(2,1)}, u32[]{:S(2)}) copy-start(bf16[4096,32]{0,1:T(8,128)(2,1)} %param.20) | copy-start | bytes 786436
  6.5 207.3 %all-gather.2.cloned.1.call-start = ((), (), s32[]{:S(2)}) async-start(), calls=%async_computation.1 | async-start | bytes 41943040 | tf_op jit(solution)/shard_map/all_gather | solution.py:131
  7.3 2476.8 %reduce-scatter.4.cloned.1.call-start = ((), (), s32[]{:S(2)}) async-start(), calls=%async_computation.2 | async-start | bytes 83886080
  13.5 352.8 %copy-start.6 = (s32[4096]{0:T(1024)}, s32[4096]{0:T(1024)S(1)}, u32[]{:S(2)}) copy-start(s32[4096]{0:T(1024)S(1)} %all_gather.6) | copy-start | bytes 49156
  13.6 12.7 collective-permute-start
  413.6 39.3 %copy-start.7 = (pred[4096]{0:T(1024)(128)(4,1)S(1)}, pred[4096]{0:T(1024)(128)(4,1)}, u32[]{:S(2)}) copy-start(pred[4096]{0:T(1024)(128)(4,1)} %get-tuple-element.178) | copy-start | bytes 12292
  413.6 39.3 %copy-start.8 = (pred[4096]{0:T(1024)(128)(4,1)S(1)}, pred[4096]{0:T(1024)(128)(4,1)}, u32[]{:S(2)}) copy-start(pred[4096]{0:T(1024)(128)(4,1)} %get-tuple-element.179) | copy-start | bytes 12292
  413.6 39.3 %copy-start.9 = (pred[4096]{0:T(1024)(128)(4,1)S(1)}, pred[4096]{0:T(1024)(128)(4,1)}, u32[]{:S(2)}) copy-start(pred[4096]{0:T(1024)(128)(4,1)} %get-tuple-element.180) | copy-start | bytes 12292
  413.6 39.3 %copy-start.17 = (f32[1,2,2,128]{3,1,2,0:T(2,128)S(1)}, f32[1,2,2,128]{3,1,2,0:T(2,128)}, u32[]{:S(2)}) copy-start(f32[1,2,2,128]{3,1,2,0:T(2,128)} %copy.124) | copy-start | bytes 6148
  413.7 39.3 %copy-start.18 = (f32[1,2,2,128]{3,1,2,0:T(2,128)S(1)}, f32[1,2,2,128]{3,1,2,0:T(2,128)}, u32[]{:S(2)}) copy-start(f32[1,2,2,128]{3,1,2,0:T(2,128)} %copy.125) | copy-start | bytes 6148
  413.7 39.3 %copy-start.19 = (f32[1,2,2,128]{3,1,2,0:T(2,128)S(1)}, f32[1,2,2,128]{3,1,2,0:T(2,128)}, u32[]{:S(2)}) copy-start(f32[1,2,2,128]{3,1,2,0:T(2,128)} %copy.126) | copy-start | bytes 6148
  413.7 39.3 %copy-start.20 = (f32[1,2,2,128]{3,1,2,0:T(2,128)S(1)}, f32[1,2,2,128]{3,1,2,0:T(2,128)}, u32[]{:S(2)}) copy-start(f32[1,2,2,128]{3,1,2,0:T(2,128)} %copy.128) | copy-start | bytes 6148
  413.7 39.3 %copy-start.21 = (f32[1,2,2,128]{3,1,2,0:T(2,128)S(1)}, f32[1,2,2,128]{3,1,2,0:T(2,128)}, u32[]{:S(2)}) copy-start(f32[1,2,2,128]{3,1,2,0:T(2,128)} %copy.127) | copy-start | bytes 6148
  438.0 14.7 collective-permute-start.2
  441.4 38.0 %collective-permute-start.1 = (bf16[3,2048]{1,0:T(4,128)(2,1)S(1)}, bf16[3,2048]{1,0:T(4,128)(2,1)S(1)}, u32[]{:S(2)}, u32[]{:S(2)}) collective-permute-start(bf16[3,2048]{1,0:T(4,128)(2,1)S(1)} %slice_bitcast_fusion.1), channel_id=1, source_target_pairs={{0,4},{4,8},{8,12},{1,5},{5,9},{9,13},{2,6},{6,10},{10,14},{3,7},{... | collective-permute-start | bytes 36872 | tf_op jit(solution)/shard_map/ppermute | solution.py:102
  570.3 37.6 %copy-start.26 = (f32[32]{0:T(128)S(1)}, f32[32]{0:T(128)}, u32[]{:S(2)}) copy-start(f32[32]{0:T(128)} %param.27) | copy-start | bytes 388
  607.9 1129.6 %copy-start.22 = (bf16[2048]{0:T(1024)(128)(2,1)S(1)}, bf16[2048]{0:T(1024)(128)(2,1)}, u32[]{:S(2)}) copy-start(bf16[2048]{0:T(1024)(128)(2,1)} %param.28) | copy-start | bytes 12292
  608.0 1140.0 %copy-start.15 = (pred[4096]{0:T(1024)(128)(4,1)S(1)}, pred[4096]{0:T(1024)(128)(4,1)}, u32[]{:S(2)}) copy-start(pred[4096]{0:T(1024)(128)(4,1)} %get-tuple-element.181) | copy-start | bytes 12292
  1689.9 25.6 %collective-permute-start.5 = (f32[2,16,64,128]{3,2,1,0:T(8,128)S(1)}, f32[2,16,64,128]{3,2,1,0:T(8,128)S(1)}, u32[]{:S(2)}, u32[]{:S(2)}) collective-permute-start(f32[2,16,64,128]{3,2,1,0:T(8,128)S(1)} %get-tuple-element.64), channel_id=1, source_target_pairs={{0,4},{4,8},{8,12},{1,5},{5,9},{9,13},{2,6},{6,10},{10,14},{3,7},{... | collective-permute-start | bytes 3145736 | tf_op jit(solution)/shard_map/ppermute | solution.py:74
  1715.5 25.8 %collective-permute-start.6 = (f32[2,16,64,128]{3,2,1,0:T(8,128)S(1)}, f32[2,16,64,128]{3,2,1,0:T(8,128)S(1)}, u32[]{:S(2)}, u32[]{:S(2)}) collective-permute-start(f32[2,16,64,128]{3,2,1,0:T(8,128)S(1)} %collective-permute-done.5), channel_id=1, source_target_pairs={{0,4},{4,8},{8,12},{1,5},{5,9},{9,13},{2,6},{6,10},{10,14},{3,7},{... | collective-permute-start | bytes 3145736 | tf_op jit(solution)/shard_map/ppermute | solution.py:79
  1735.3 6.0 collective-permute-start.3
  1742.5 97.6 %collective-permute-start.7 = (f32[2,16,64,128]{3,2,1,0:T(8,128)}, f32[2,16,64,128]{3,2,1,0:T(8,128)}, u32[]{:S(2)}, u32[]{:S(2)}) collective-permute-start(f32[2,16,64,128]{3,2,1,0:T(8,128)} %add_select_fusion.1), channel_id=1, source_target_pairs={{0,8},{4,12},{1,9},{5,13},{2,10},{6,14},{3,11},{7,15},{16,24},{20,... | collective-permute-start | bytes 3145736 | tf_op jit(solution)/shard_map/ppermute | solution.py:79
  1770.1 33.9 %collective-permute-start.4 = (f32[2,16]{1,0:T(2,128)S(1)}, f32[2,16]{1,0:T(2,128)S(1)}, u32[]{:S(2)}, u32[]{:S(2)}) collective-permute-start(f32[2,16]{1,0:T(2,128)S(1)} %broadcast_select_fusion), channel_id=1, source_target_pairs={{0,4},{4,8},{8,12},{1,5},{5,9},{9,13},{2,6},{6,10},{10,14},{3,7},{... | collective-permute-start | bytes 392 | tf_op jit(solution)/shard_map/ppermute | solution.py:80
  2040.6 455.5 %copy-start.1 = (bf16[4096,32]{0,1:T(8,128)(2,1)S(1)}, bf16[4096,32]{0,1:T(8,128)(2,1)}, u32[]{:S(2)}) copy-start(bf16[4096,32]{0,1:T(8,128)(2,1)} %param.20) | copy-start | bytes 786436
  (13 other events, 346.1 us)
Sparse Core Ops, SparseCore 0:
  8.9 204.8 all-gather.1
  2040.7 443.3 reduce-scatter.3
where the time goes:
time: 2540 us; the launch traced here: 2500 us
  local copies, waits for them, and re-layouts  1120 us (44%)
  waiting for transfers between devices  652 us (26%)
  matrix products  459 us (18%)
  other arithmetic  195 us (8%)
  starting transfers between devices  28.7 us (1%)
    dynamic_update_slice x32, local copies, waits for them, and re-layouts, block_ssd(): end_state, y_tiles = lax.scan(body, init_state, tiles_in)  795 us
    unnamed x3, waiting for transfers between devices  444 us
    all_gather x1, waiting for transfers between devices, body(): x_blk = lax.all_gather(x_loc, 'tp', axis=0, tiled=True)  184 us
    dot_general x1, matrix products, local_layer(): jnp.einsum('ld,dkc->lkc', x_blk, w_zx, preferred_element_type=jnp.float32)  152 us
    dot_general x1, matrix products, local_layer(): return jnp.dot(y_norm, w_out, preferred_element_type=jnp.float32)  89.2 us
    unnamed x67, local copies, waits for them, and re-layouts  81.3 us
    dot_general x16, matrix products, ssd_tile(): jnp.einsum('tsgr,sgrp->tgrp', mix_mat, x_ssm, preferred_element_type=jnp....  71.5 us
    convert_element_type x2, other arithmetic, causal_conv(): return jax.nn.silu(conv_acc).astype(jnp.bfloat16)  58.8 us
  transfers between devices with their start and end apart: 10, of which 4 were waited for; matrix products, arithmetic and copies ran while one was open for 6% of the time, Pallas kernels for 0%

commit v1 on v0

v1 whole, which is shorter than its diff:
```python
import functools
import jax
import jax.numpy as jnp
from jax import lax
from jax.sharding import PartitionSpec as P
from jax.experimental import pallas as pl
from jax.experimental.pallas import tpu as pltpu

T = 128
XW = 2048
NB = 512
GW = 1024
D = 4096
TOK = 1024
HEADS, HEAD = 32, 64
XT = 512
MT = 256
HALO = 16
SUB = 8
MH = MT + HALO
LOG2E = 1.4426950408889634
NORM_EPS = 1e-5
MIB = 2**20
f32, bf16 = jnp.float32, jnp.bfloat16
MESH = pl.DeviceIdType.MESH
ONE = pl.Buffered(1)


def silu(v):
    h = 0.5 * v
    return h + h * jnp.tanh(h)


def lane_bcast(cols, h):
    return jnp.broadcast_to(cols[:, h:h + 1], (cols.shape[0], T))


def pair_bcast(cols, p):
    lanes = lax.broadcasted_iota(jnp.int32, (cols.shape[0], T), 1)
    return jnp.where(lanes < HEAD, lane_bcast(cols, 2 * p), lane_bcast(cols, 2 * p + 1))


def row(ref, r):
    return ref[r:r + 1, :]


def mac(a, b, ca=1, cb=0, **kw):
    return lax.dot_general(a, b, (((ca,), (cb,)), ((), ())), preferred_element_type=f32, **kw)


def rows_from(start, size):
    return pl.ds(start if isinstance(start, int) else pl.multiple_of(start, 16), size)


def front_kernel(pre, *refs, nx, per, hrows):
    xs_, hs_, auxs = refs[:nx], refs[nx:2 * nx], refs[2 * nx:3 * nx]
    (wx_ref, wb_ref, wdt_ref, cin_ref, cw_ref, cwb_ref, hp_ref,
     xa_ref, bca_ref, dc_ref, cout_ref, xbuf, pbuf, bbuf, xw, bt, cum_all, wgt, abuf, sem) = refs[3 * nx:]
    n = pl.program_id(0)
    last_n = XW // XT
    nm = nx * per
    rows = lax.broadcasted_iota(jnp.int32, (T, T), 0)
    cols = lax.broadcasted_iota(jnp.int32, (T, T), 1)
    tiles = [slice(t * T, (t + 1) * T) for t in range(MT // T)]

    def copies(m):
        i, s = divmod(m, per)
        if s:
            return [pltpu.make_async_copy(xs_[i].at[rows_from(s * MT - HALO, MH)], xbuf.at[m], sem.at[m])]
        return [pltpu.make_async_copy(hs_[i].at[rows_from(hrows[i](pre), HALO)], xbuf.at[m, pl.ds(0, HALO)], sem.at[m]),
                pltpu.make_async_copy(xs_[i].at[pl.ds(0, MT)], xbuf.at[m, pl.ds(HALO, MT)], sem.at[m])]

    def left(i):
        return slice(nm * MT + SUB * (i + 1), nm * MT + SUB * (i + 2))

    def heads_first(v):
        return pltpu.roll(v, lax.rem(T - (XT // HEAD) * (n - 1), T), 1)

    def at(m, ts):
        return pl.ds(pl.multiple_of(m * MT + ts.start, T), T)

    def conv(read, lo, w, keep):
        cs = slice(lo, lo + T)
        acc = read(0, cs) * row(w, 3)[:, cs] + row(w, 4)[:, cs]
        for k in range(3):
            acc = acc + (read(3 - k, cs) * w[k:k + 1, cs]) * keep[k]
        return silu(acc).astype(bf16)

    def taps(m, ts):
        return [lane_bcast(abuf[m, ts, :], 2 - k) for k in range(3)]

    def x_dot(m):
        pbuf[lax.rem(n, 2), m] = jnp.dot(xbuf[m], wx_ref[...], preferred_element_type=f32).astype(bf16).astype(f32)

    def setup(m, i, s):
        for ts in tiles:
            r0 = HALO + ts.start
            keep = taps(m, ts)
            for c in range(NB // T):
                act = conv(lambda d, cs: bbuf[r0 - d:r0 - d + T, cs], c * T, cwb_ref, keep)
                bca_ref[at(m, ts), c * T:(c + 1) * T] = act
                if c < 2:
                    bt[i, c, :, at(s, ts)] = act.T
            raw = bbuf[r0:r0 + T, NB:NB + T] + row(hp_ref, 0)
            dtv = jnp.maximum(raw, 0.0) + jnp.log1p(jnp.exp(-jnp.abs(raw)))
            log_a = -jnp.exp(row(hp_ref, 1)) * dtv * LOG2E
            cum = mac((rows >= cols).astype(f32), log_a, precision=lax.Precision.HIGHEST)
            dc_ref[at(m, ts), :] = jnp.where(cols < HEADS, cum, pltpu.roll(dtv, HEADS, 1))
            before = jnp.where((s == 0) & (ts.start == 0), 0.0, row(cum_all, nm * MT))
            cum = cum + before
            cum_all[at(m, ts), :] = cum
            cum_all[nm * MT:nm * MT + SUB, :] = jnp.broadcast_to(cum[T - 1:T, :], (8, T))
            wgt[at(m, ts), :] = dtv

    def weigh(i):
        lo, end = i * per * MT, (i + 1) * per * MT
        doc = abuf[end // MT - 1, MT - 1:MT, 5:6]
        last = row(cum_all, end - 1)
        keep_in = abuf[lo // MT, 0:1, 0:1] * (abuf[lo // MT, 0:1, 5:6] == doc).astype(f32)
        carry = jnp.broadcast_to(jnp.exp2(last) * keep_in, (8, T))
        for r in range(lo, end, T):
            keep = jnp.broadcast_to((abuf[r // MT, r % MT:r % MT + T, 5:6] == doc).astype(f32), (T, T))
            wgt[r:r + T, :] = jnp.exp2(last - cum_all[r:r + T, :]) * wgt[r:r + T, :] * keep
        cum_all[left(i), :] = carry

    def x_conv(m):
        slot = lax.rem(n + 1, 2)
        for ts in tiles:
            r0 = HALO + ts.start
            keep = taps(m, ts)
            wg = heads_first(wgt[at(m, ts), :])
            for p in range(XT // T):
                cs = slice(p * T, (p + 1) * T)
                xa = conv(lambda d, cs: pbuf[slot, m, r0 - d:r0 - d + T, cs], p * T, cw_ref, keep)
                xa_ref[at(m, ts), cs] = xa
                xw[at(m, ts), cs] = (xa.astype(f32) * pair_bcast(wg, p)).astype(bf16)

    def end_state():
        g = (n - 1) // (GW // XT)
        for i in range(nx):
            upd = jnp.dot(bt[i, g], xw[i * per * MT:(i + 1) * per * MT, :], preferred_element_type=f32)
            cr = heads_first(cum_all[left(i), :])
            for p in range(XT // T):
                cs = slice(p * T, (p + 1) * T)
                carry = pair_bcast(cr, p)
                cout_ref[i, 0:T, cs] = cin_ref[i, 0:T, cs] * jnp.broadcast_to(carry[0:1], (T, T)) + upd[:, cs]
                cout_ref[i, T:T + 8, cs] = cin_ref[i, T:T + 8, cs] * carry

    @pl.when(n == 0)
    def _():
        for m in range(nm):
            for c in copies(m):
                c.start()
        bbuf[:, NB:] = jnp.zeros((MH, T), f32)
        for m in range(nm):
            i, s = divmod(m, per)
            abuf[m] = auxs[i][s * MT:(s + 1) * MT, :]

        @pl.loop(0, nm)
        def _(m):
            for k in range(nm):
                @pl.when(m == k)
                def _():
                    for c in copies(k):
                        c.wait()
            bbuf[:, 0:NB] = jnp.dot(xbuf[m], wb_ref[...], preferred_element_type=f32).astype(bf16).astype(f32)
            bbuf[:, NB:NB + HEADS] = jnp.dot(xbuf[m], wdt_ref[...], preferred_element_type=f32).astype(bf16).astype(f32)
            x_dot(m)
            setup(m, m // per, lax.rem(m, per))

        for i in range(nx):
            weigh(i)

    @pl.when((n > 0) & (n < last_n))
    def _():
        @pl.loop(0, nm)
        def _(m):
            x_dot(m)
            x_conv(m)

    @pl.when(n == last_n)
    def _():
        @pl.loop(0, nm)
        def _(m):
            x_conv(m)

    @pl.when(n > 0)
    def _():
        end_state()


def front_call(pre, aux, amaps, xs, halos, hrows, weights, cin, consts, *, per):
    nx = len(xs)
    nm = nx * per
    n = nm * MT
    nt = XW // XT
    w2, wb, wdt = weights
    hbm = pl.BlockSpec(memory_space=pl.ANY)
    prev = lambda j: jnp.maximum(j - 1, 0)
    whole = lambda *shape, mode=ONE: pl.BlockSpec(shape, lambda j, b: (0,) * len(shape), pipeline_mode=mode)
    cols = lambda k: pl.BlockSpec((k, XT), lambda j, b: (0, prev(j)))
    state = pl.BlockSpec((nx, T + 8, XT), lambda j, b: (0, 0, prev(j)))
    in_specs = [hbm] * (2 * nx) + [pl.BlockSpec((per * MT, T), lambda j, b, f=f: (f(b), 0), pipeline_mode=ONE) for f in amaps] + [
        pl.BlockSpec((D, XT), lambda j, b: (0, nt + jnp.minimum(j, nt - 1))), whole(D, NB), whole(D, HEADS),
        state, cols(8), whole(8, NB), whole(8, T)]
    gs = pltpu.PrefetchScalarGridSpec(
        num_scalar_prefetch=1, grid=(nt + 1,), in_specs=in_specs,
        out_specs=[cols(n), whole(n, NB, mode=None), whole(n, T, mode=None), state],
        scratch_shapes=[pltpu.VMEM((nm, MH, D), bf16), pltpu.VMEM((2, nm, MH, XT), f32), pltpu.VMEM((MH, NB + T), f32),
                        pltpu.VMEM((n, XT), bf16), pltpu.VMEM((nx, 2, T, per * MT), bf16),
                        pltpu.VMEM((n + 8 * (nx + 1), T), f32), pltpu.VMEM((n, T), f32), pltpu.VMEM((nm, MT, T), f32),
                        pltpu.SemaphoreType.DMA((nm,))],
    )
    return pl.pallas_call(
        functools.partial(front_kernel, nx=nx, per=per, hrows=hrows), grid_spec=gs,
        out_shape=[jax.ShapeDtypeStruct((n, XW), bf16), jax.ShapeDtypeStruct((n, NB), bf16),
                   jax.ShapeDtypeStruct((n, T), f32), jax.ShapeDtypeStruct((nx, T + 8, XW), f32)],
        compiler_params=pltpu.CompilerParams(dimension_semantics=("arbitrary",), vmem_limit_bytes=62 * MIB),
        cost_estimate=pl.CostEstimate(flops=n * 25_000_000, bytes_accessed=n * 10000, transcendentals=n * 4096),
        name="front",
    )(pre, *xs, *halos, *[aux] * nx, w2, wb, wdt, cin, *consts)


def mixz_kernel(pre, *refs, nx):
    xs_, auxs = refs[:nx], refs[nx:2 * nx]
    (xa_ref, bg_ref, cg_ref, dc_ref, wz_ref, cin_ref, hp_ref, yn_ref, cout_ref, xv, av, zbuf, ybuf, xw, state) = refs[2 * nx:]
    g, i, tile = pl.program_id(0), pl.program_id(1), pl.program_id(2)
    n_tiles = pl.num_programs(2)

    @pl.when(tile == 0)
    def _():
        state[...] = cin_ref[0]

    for k in range(nx):
        @pl.when(i == k)
        def _():
            xv[...] = xs_[k][...]
            av[...] = auxs[k][...]

    zbuf[...] = jnp.dot(xv[...], wz_ref[...], preferred_element_type=f32).astype(bf16).astype(f32)
    rows = lax.broadcasted_iota(jnp.int32, (T, T), 0)
    cols = lax.broadcasted_iota(jnp.int32, (T, T), 1)
    lo_half = cols < 64
    zero = jnp.zeros((T, T), bf16)
    for t in range(MT // T):
        rs = slice(t * T, (t + 1) * T)
        aux = av[rs, :]
        auxt = aux.T
        mask = (rows >= cols) & (lane_bcast(aux, 5) == jnp.broadcast_to(auxt[5:6, :], (T, T)))
        k_in = lane_bcast(aux, 3)
        k_end = lane_bcast(aux, 4)
        dc = pltpu.roll(dc_ref[rs, :], lax.rem(T - 16 * g, T), 1)
        dct = dc.T
        rel = dct[:HEADS // 2, :] - jnp.log2(dct[HEADS:HEADS + HEADS // 2, :])
        bg, cg = bg_ref[rs, :], cg_ref[rs, :]
        sm = jnp.where(mask, mac(cg, bg, 1, 1), 0.0)
        ybuf[...] = mac(cg, state[...].astype(bf16))
        sq = jnp.zeros((T, T), f32)
        for p in range(GW // T):
            cs = slice(p * T, (p + 1) * T)
            xa = xa_ref[rs, cs]
            xaf = xa.astype(f32)
            c0, c1 = lane_bcast(dc, 2 * p), lane_bcast(dc, 2 * p + 1)
            mixes = []
            for hh, cb in ((2 * p, c0), (2 * p + 1, c1)):
                diff = jnp.minimum(cb - jnp.broadcast_to(rel[hh:hh + 1, :], (T, T)), 126.0)
                mixes.append((sm * jnp.exp2(diff)).astype(bf16))
            lhs = jnp.concatenate(mixes, axis=1)
            rhs = jnp.concatenate([jnp.where(lo_half, xa, zero), jnp.where(lo_half, zero, xa)], axis=0)
            y = mac(lhs, rhs)
            cump = jnp.where(lo_half, c0, c1)
            dtp = pair_bcast(dc, HEADS // 2 + p)
            last = cump[T - 1:T, :]
            xw[:, cs] = (xaf * (jnp.exp2(last - cump) * dtp * k_end)).astype(bf16)
            y = y + ybuf[:, cs] * (jnp.exp2(cump) * k_in) + hp_ref[0:1, cs] * xaf
            v = y * silu(zbuf[rs, cs])
            ybuf[:, cs] = v
            sq = sq + v * v
            state[:, cs] = state[:, cs] * (jnp.exp2(last) * k_in[T - 1:T, :])
        ms = jnp.sum(sq, axis=1, keepdims=True) * (1.0 / GW)
        r = jnp.broadcast_to(lax.rsqrt(ms + NORM_EPS), (T, T))
        for p in range(GW // T):
            cs = slice(p * T, (p + 1) * T)
            yn_ref[rs, cs] = (ybuf[:, cs] * r * hp_ref[1:2, cs]).astype(bf16)
        state[...] = state[...] + mac(bg, xw[...], 0, 0)

    @pl.when(tile == n_tiles - 1)
    def _():
        cout_ref[0] = state[...]


def mixz_call(pre, aux, amaps, xs, arrs, w2, cin, hp, *, per, cofs):
    nx = len(xs)
    n = nx * per * MT
    xa, bca, dc = arrs
    piece = lambda k: (lambda g, i, t: jnp.clip((i - k) * per + t, 0, per - 1))
    rows = lambda w, c: pl.BlockSpec((MT, w), lambda g, i, t, b: (i * per + t, c(g)))
    state = lambda ofs: pl.BlockSpec((1, T, GW), lambda g, i, t, b: (ofs + i, 0, g))
    cols = lambda k: pl.BlockSpec((k, GW), lambda g, i, t, b: (0, g))
    in_specs = [pl.BlockSpec((MT, D), lambda g, i, t, b, k=k: (piece(k)(g, i, t), 0)) for k in range(nx)]
    in_specs += [pl.BlockSpec((MT, T), lambda g, i, t, b, k=k: (amaps[k](b) * per + piece(k)(g, i, t), 0)) for k in range(nx)]
    same = lambda g: g
    in_specs += [rows(GW, same), rows(T, same), rows(T, lambda g: 2 + g), rows(T, lambda g: 0), cols(D), state(cofs), cols(8)]
    gs = pltpu.PrefetchScalarGridSpec(
        num_scalar_prefetch=1, grid=(2, nx, per), in_specs=in_specs, out_specs=[rows(GW, same), state(0)],
        scratch_shapes=[pltpu.VMEM((MT, D), bf16), pltpu.VMEM((MT, T), f32), pltpu.VMEM((MT, GW), f32), pltpu.VMEM((T, GW), f32),
                        pltpu.VMEM((T, GW), bf16), pltpu.VMEM((T, GW), f32)],
    )
    return pl.pallas_call(
        functools.partial(mixz_kernel, nx=nx), grid_spec=gs,
        out_shape=[jax.ShapeDtypeStruct((n, XW), bf16), jax.ShapeDtypeStruct((nx, T, XW), f32)],
        compiler_params=pltpu.CompilerParams(dimension_semantics=("arbitrary",) * 3, vmem_limit_bytes=60 * MIB),
        cost_estimate=pl.CostEstimate(flops=n * 20_000_000, bytes_accessed=n * 14000, transcendentals=n * 10000),
        name="mixz",
    )(pre, *xs, *[aux] * nx, xa, bca, bca, dc, w2, cin, hp)


def seq_slot(me, s):
    c = (me % 2 + s % 2) % 2
    y = (me // 2 + s // 2) % 2
    return 2 * y + c


def count(flag):
    return jnp.where(flag, 1, 0)


def ahead_kernel(n_blocks, seg_ref, tail_ref, segs_ref, tails_ref, send_sem, recv_sem):
    me, blk = lax.axis_index('tp'), lax.axis_index('sp')
    barrier = pltpu.get_barrier_semaphore()
    others = [{'tp': seq_slot(me, s)} for s in (1, 2, 3)]
    before = {'sp': jnp.maximum(blk - 1, 0), 'tp': 3}
    after = [{'sp': jnp.minimum(blk + 1, n_blocks - 1), 'tp': q} for q in range(4)]
    sends_on = (me == 3) & (blk < n_blocks - 1)
    for dev in others:
        pl.semaphore_signal(barrier, inc=1, device_id=dev, device_id_type=MESH)

    @pl.when(blk > 0)
    def _():
        pl.semaphore_signal(barrier, inc=1, device_id=before, device_id_type=MESH)

    @pl.when(sends_on)
    def _():
        for dev in after:
            pl.semaphore_signal(barrier, inc=1, device_id=dev, device_id_type=MESH)

    pl.semaphore_wait(barrier, 3 + count(blk > 0) + 4 * count(sends_on))

    def copies(dev, entry, k, rk):
        return [pltpu.make_async_remote_copy(src_ref=seg_ref, dst_ref=segs_ref.at[entry], send_sem=send_sem.at[k, 0],
                                             recv_sem=recv_sem.at[rk, 0], device_id=dev, device_id_type=MESH),
                pltpu.make_async_remote_copy(src_ref=tail_ref, dst_ref=tails_ref.at[entry], send_sem=send_sem.at[k, 1],
                                             recv_sem=recv_sem.at[rk, 1], device_id=dev, device_id_type=MESH)]

    inner = [copies(dev, me + 1, k, k) for k, dev in enumerate(others)]
    outer = [copies(dev, 0, 3 + q, 3) for q, dev in enumerate(after)]
    for cs in inner:
        for c in cs:
            c.start()

    @pl.when(sends_on)
    def _():
        for cs in outer:
            for c in cs:
                c.start()

    segs_ref[me + 1] = seg_ref[...]
    tails_ref[me + 1] = tail_ref[...]

    @pl.when(blk == 0)
    def _():
        segs_ref[0] = jnp.zeros_like(seg_ref)
        tails_ref[0] = jnp.zeros_like(tail_ref)

    for cs in inner:
        for c in cs:
            c.wait_send()
            c.wait_recv()

    @pl.when(sends_on)
    def _():
        for cs in outer:
            for c in cs:
                c.wait_send()

    @pl.when(blk > 0)
    def _():
        for c in outer[0]:
            c.wait_recv()


def ahead_call(seg, x, n_blocks):
    rows = x.shape[0]
    vmem = pl.BlockSpec(memory_space=pltpu.VMEM)
    return pl.pallas_call(
        functools.partial(ahead_kernel, n_blocks),
        grid=(1,),
        in_specs=[vmem, pl.BlockSpec((HALO, D), lambda i: (rows // HALO - 1, 0))],
        out_specs=[vmem, vmem],
        out_shape=[jax.ShapeDtypeStruct((5, rows // T, T), jnp.int32), jax.ShapeDtypeStruct((5, HALO, D), bf16)],
        scratch_shapes=[pltpu.SemaphoreType.DMA((7, 2)), pltpu.SemaphoreType.DMA((4, 2))],
        compiler_params=pltpu.CompilerParams(collective_id=0, has_side_effects=True, vmem_limit_bytes=16 * MIB),
        name="ahead",
    )(seg.reshape(rows // T, T), x)


CW = 256


def chain_kernel(n_blocks, e01_ref, e2_ref, e3_ref, out_ref, ebuf, sbuf, obuf, lsem, send_sem, recv_sem):
    me, blk = lax.axis_index('tp'), lax.axis_index('sp')
    srcs = [e01_ref.at[0], e01_ref.at[1], e2_ref.at[0], e3_ref.at[0]]
    loads = [pltpu.make_async_copy(src, ebuf.at[seq_slot(me, s)], lsem.at[s]) for s, src in enumerate(srcs)]
    for c in loads:
        c.start()
    barrier = pltpu.get_barrier_semaphore()
    before = {'sp': jnp.maximum(blk - 1, 0)}
    after = {'sp': jnp.minimum(blk + 1, n_blocks - 1)}

    @pl.when(blk > 0)
    def _():
        pl.semaphore_signal(barrier, inc=1, device_id=before, device_id_type=MESH)

    @pl.when(blk < n_blocks - 1)
    def _():
        pl.semaphore_signal(barrier, inc=1, device_id=after, device_id_type=MESH)

    pl.semaphore_wait(barrier, count(blk > 0) + count(blk < n_blocks - 1))

    for c in loads:
        c.wait()

    def through(q, s, cs):
        return ebuf[q, :T, cs] + ebuf[q, T:T + 1, cs] * s

    for q in (1, 2, 3):
        ebuf[q, :T, :] = through(q, ebuf[q - 1, :T, :], slice(None))
        ebuf[q, T:, :] = ebuf[q, T:, :] * ebuf[q - 1, T:, :]

    @pl.when(blk == 0)
    def _():
        sbuf[...] = jnp.zeros_like(sbuf)

    n = XW // CW

    def send(j):
        return pltpu.make_async_remote_copy(src_ref=obuf.at[j], dst_ref=sbuf.at[j], send_sem=send_sem.at[j],
                                            recv_sem=recv_sem.at[j], device_id=after, device_id_type=MESH)

    for j in range(n):
        cs = slice(j * CW, (j + 1) * CW)

        @pl.when(blk > 0)
        def _():
            send(j).wait_recv()

        @pl.when(blk < n_blocks - 1)
        def _():
            obuf[j] = through(3, sbuf[j], cs)
            send(j).start()

    for j in range(n):
        cs = slice(j * CW, (j + 1) * CW)
        for q in range(4):
            v = through(q - 1, sbuf[j], cs) if q else sbuf[j]
            out_ref[seq_slot(me, q), :, cs] = v

    @pl.when(blk < n_blocks - 1)
    def _():
        for j in range(n):
            send(j).wait_send()


def chain_call(e01, e2, e3, n_blocks):
    hbm = pl.BlockSpec(memory_space=pl.ANY)
    n = XW // CW
    return pl.pallas_call(
        functools.partial(chain_kernel, n_blocks),
        in_specs=[hbm] * 3,
        out_specs=pl.BlockSpec(memory_space=pltpu.VMEM),
        out_shape=jax.ShapeDtypeStruct((4, T, XW), f32),
        scratch_shapes=[pltpu.VMEM((4, T + SUB, XW), f32), pltpu.VMEM((n, T, CW), f32), pltpu.VMEM((n, T, CW), f32),
                        pltpu.SemaphoreType.DMA((4,)), pltpu.SemaphoreType.DMA((n,)), pltpu.SemaphoreType.DMA((n,))],
        compiler_params=pltpu.CompilerParams(collective_id=1, has_side_effects=True, vmem_limit_bytes=40 * MIB),
        name="chain",
    )(e01, e2, e3)


NT = 512


def out_kernel(y_ref, yr_ref, w_ref, wr0_ref, wr1_ref, *refs):
    h = XW // 2
    acc = (jnp.dot(y_ref[...], w_ref[...], preferred_element_type=f32)
           + jnp.dot(yr_ref[:, 0:h], wr0_ref[...], preferred_element_type=f32)
           + jnp.dot(yr_ref[:, h:], wr1_ref[...], preferred_element_type=f32))
    if len(refs) > 1:
        x_ref, other_ref = refs[:2]
        acc = x_ref[...].astype(f32) + (acc + other_ref[...])
    refs[-1][...] = acc.astype(refs[-1].dtype)


def out_call(run, part, y, yr, w, wr, x=None, other=None, into=None):
    rows = yr.shape[0]
    h = XW // 2
    at = lambda r: (lambda j: (r, j))
    cols = at(0)
    ins = [y, yr, w, *wr]
    specs = [pl.BlockSpec((rows, XW), lambda j: (run * (TOK // rows) + part, 0), pipeline_mode=ONE),
             pl.BlockSpec((rows, XW), lambda j: (0, 0), pipeline_mode=ONE),
             pl.BlockSpec((XW, NT), cols), pl.BlockSpec((h, NT), cols), pl.BlockSpec((h, NT), cols)]
    alias = {}
    if x is not None:
        ins += [x, other]
        specs += [pl.BlockSpec((rows, NT), at(part)), pl.BlockSpec((rows, NT), cols)]
    if into is not None:
        alias = {len(ins): 0}
        ins.append(into)
        specs.append(pl.BlockSpec(memory_space=pl.ANY))
    return pl.pallas_call(
        out_kernel,
        grid=(D // NT,), in_specs=specs,
        out_specs=pl.BlockSpec((rows, NT), cols if x is None else at(part)),
        out_shape=jax.ShapeDtypeStruct((rows, D), f32) if x is None else jax.ShapeDtypeStruct(x.shape, bf16),
        input_output_aliases=alias,
        compiler_params=pltpu.CompilerParams(dimension_semantics=("arbitrary",), vmem_limit_bytes=56 * MIB),
        cost_estimate=pl.CostEstimate(flops=rows * 33_000_000, bytes_accessed=rows * 100000, transcendentals=0),
        name="out_proj",
    )(*ins)


def send(v, perm):
    return lax.ppermute(v, 'tp', perm)


def after(v, *deps):
    return lax.optimization_barrier((v,) + deps)[0]


NCH = 2
CORE_SWAP = [(i, i ^ 1) for i in range(4)]
CHIP_SWAP = [(i, i ^ 2) for i in range(4)]


def token_aux(seg_ext):
    seg = seg_ext[3:]
    n = seg.shape[0]
    tile_prev = jnp.repeat(seg_ext[2:n + 2:T], T)
    tile_last = jnp.repeat(seg[T - 1::T], T)
    cols = [seg == seg_ext[3 - k:n + 3 - k] for k in (1, 2, 3)] + [seg == tile_prev, seg == tile_last, seg - seg_ext[0]]
    lane = lax.broadcasted_iota(jnp.int32, (n, T), 1)
    out = jnp.zeros((n, T), f32)
    for i, c in enumerate(cols):
        out = jnp.where(lane == i, c.astype(f32)[:, None], out)
    return out


def solution(mesh):
    n_blocks = mesh.shape['sp']
    token_spec = seg_spec = P(('dp', 'sp', 'tp'))
    weight_specs = tuple(P(*['tp' if i == dim else None for i in range(dim + 1)]) for dim in (2, 2, 1, 1, 2, 0, 1, 0, 0, 0, 0, 0))

    def body(x_loc, seg_loc, w_zx, w_bc, w_dt, conv_x, conv_bc, bias_x, bias_bc, a_log, dt_bias, d_skip, norm_w, w_out):
        rows, d = x_loc.shape
        me, blk = lax.axis_index('tp'), lax.axis_index('sp')
        ch = rows // NCH
        per, kper = rows // MT, ch // MT
        segs, tails = ahead_call(seg_loc, x_loc, n_blocks)
        x_snd, segs = lax.optimization_barrier((x_loc, segs))
        x_par = send(x_snd, CORE_SWAP)
        parts = [x_snd[:ch]]
        parts.append(after(x_snd, parts[0])[ch:])
        x_dir = [send(v, CHIP_SWAP) for v in parts]
        place = lax.axis_index('dp') * n_blocks + blk
        half = w_out.shape[0] // 2
        step = half // (mesh.shape['dp'] * n_blocks)
        w_half = [send(after(lax.dynamic_slice(w_out, (h * half + place * step, 0), (step, d)), segs), CHIP_SWAP) for h in range(2)]

        def w_gather(h, dep):
            return lax.all_gather(after(w_half[h], dep), ('dp', 'sp'), axis=0, tiled=True)

        aux = token_aux(jnp.concatenate([segs[0].reshape(-1)[-3:], segs[1:].reshape(-1)]))
        tails = tails.reshape(-1, d)
        w2, wb = w_zx.reshape(d, 2 * XW), w_bc.reshape(d, NB)
        pad = lambda v: jnp.pad(v.astype(f32), ((0, SUB - v.shape[0]), (0, 0)))
        cw = pad(jnp.concatenate([conv_x, bias_x[None]], axis=0))
        cwb = pad(jnp.concatenate([conv_bc.reshape(4, NB), bias_bc.reshape(1, NB)], axis=0))
        hp1 = jnp.pad(jnp.stack([dt_bias, a_log]), ((0, 6), (0, T - HEADS)))
        hp2 = pad(jnp.stack([jnp.repeat(d_skip, HEAD), norm_w.astype(f32)]))
        init = jnp.broadcast_to((jnp.arange(T + SUB) >= T).astype(f32)[None, :, None], (2, T + SUB, XW))
        pre = jnp.stack([seq_slot(me, s) for s in range(4)]).astype(jnp.int32)
        weights = (w2, wb, w_dt)
        consts = (cw, cwb, hp1)

        def front(slots, part, xs, halos, hrows, carry, per):
            return front_call(pre, aux, [lambda b, s=s: b[s] * (rows // (per * MT)) + part for s in slots], xs, halos, hrows,
                              weights, carry, consts, per=per)

        tail_row = lambda s: (lambda b: b[s] * HALO)
        *own, ends = front((0, 1), 0, [x_loc, x_par], [tails] * 2, [tail_row(0), tail_row(1)], init, per)
        w_rem = [w_gather(0, ends)]
        x_dir[0] = after(x_dir[0], ends)
        rem, carry, x_fwd = [[], []], [init[:1], after(init[:1], ends)], []
        for k in range(NCH):
            x_fwd.append(send(x_dir[k], CORE_SWAP))
            for r, xs in ((0, x_dir), (1, x_fwd)):
                halo = (tails, tail_row(2 + r)) if k == 0 else (xs[k - 1], lambda b: ch - HALO)
                c = after(carry[r], carry[0]) if r else after(carry[0], carry[1])
                *arrs, carry[r] = front((2 + r,), k, [xs[k]], [halo[0]], [halo[1]], c, kper)
                rem[r].append(arrs)
            if k + 1 < NCH:
                x_dir[k + 1] = after(x_dir[k + 1], carry[1])
        starts = chain_call(ends, carry[0], carry[1], n_blocks)
        w_rem.append(w_gather(1, starts))

        def mix(slots, part, xs, arrs, start, cofs, per):
            return mixz_call(pre, aux, [lambda b, s=s: b[s] * (rows // (per * MT)) + part for s in slots], xs, arrs, w2, start, hp2,
                             per=per, cofs=cofs)

        y_in = [[], []]
        last = starts
        for r, xs in ((1, x_fwd), (0, x_dir)):
            c, cofs = after(starts, last), 2 + r
            for k in range(NCH):
                yn, c = mix((2 + r,), k, [xs[k]], rem[r][k], c, cofs, kper)
                last, cofs = c, 0
                y_in[r].append(send(yn, CHIP_SWAP))
        y_own, _ = mix((0, 1), 0, [x_loc, x_par], own, after(starts, last), 0, per)
        other = []
        for k in range(NCH):
            part = out_call(1, k, y_own, y_in[1][k], w_out, w_rem)
            other.append(send(part, CORE_SWAP))
        y = None
        for k in range(NCH):
            y = out_call(0, k, y_own, y_in[0][k], w_out, w_rem, x_loc, other[k], y)
        return y

    return jax.shard_map(body, mesh=mesh, in_specs=(token_spec, seg_spec) + weight_specs, out_specs=token_spec, check_vma=False)
```

time: 2540 us -> 708 us (0.28)
  the two profiles are of different devices: /device:TPU:0 before, /device:TPU:28 now
where the time goes in v1:
time: 708 us; the launch traced here: 699 us
  Pallas kernels  516 us (73%)
  waiting for transfers between devices  92.9 us (13%)
  local copies, waits for them, and re-layouts  56.1 us (8%)
  between operations  14 us (2%)
  starting transfers between devices  10.8 us (2%)
  other arithmetic  9.27 us (1%)
    pallas_call x5, Pallas kernels, front_call(): pl.pallas_call(functools.partial(front_kernel, nx=nx, per=per, hrows=hrow...  211 us
    pallas_call x5, Pallas kernels, mixz_call(): pl.pallas_call(functools.partial(mixz_kernel, nx=nx), grid_spec=gs, out_s...  158 us
    pallas_call x4, Pallas kernels, out_call(): pl.pallas_call(out_kernel, grid=(D // NT,), in_specs=specs, out_specs=pl....  101 us
    ppermute x13, waiting for transfers between devices, send(): return lax.ppermute(v, 'tp', perm)  92.8 us
    unnamed x41, local copies, waits for them, and re-layouts  40.2 us
    pallas_call x1, Pallas kernels, chain_call(): pl.pallas_call(functools.partial(chain_kernel, n_blocks), in_specs=[hbm]...  36.2 us
  transfers between devices with their start and end apart: 15, of which 4 were waited for; matrix products, arithmetic and copies ran while one was open for 8% of the time, Pallas kernels for 69%

profile of v1, /device:TPU:28, one launch (start us, length us, event | category | flops | bytes accessed | tf_op | source)
XLA Modules:
  0.0 699.3 jit_solution(17953535384784917588)
XLA Ops:
  7.2 10.8 %ahead.1 = (s32[5,8,128]{2,1,0:T(8,128)S(1)}, bf16[5,16,4096]{2,1,0:T(8,128)(2,1)S(1)}) custom-call(s32[8,128]{1,0:T(8,128)S(1)} %bitcast.37, bf16[1024,4096]{1,0:T(8,128)(2,1)} %refs_0_.7), custom_call_target="tpu_custom_call" | custom-call | tf_op jit(solution)/shard_map/ahead/pallas_call | solution.py:395
  29.7 23.2 %copy.21 = bf16[512,8,2,2048]{3,1,2,0:T(8,128)(2,1)} copy(bf16[512,8,2,2048]{3,2,1,0:T(2,128)(2,1)} %bitcast.57) | data formatting | bytes 67108864
  52.9 5.1 copy.22
  62.8 5.3 select_select_fusion.refs_4_.refs_5_.refs_2_.refs_3_.refs_1_
  69.6 92.0 %front.5 = (bf16[2048,2048]{1,0:T(8,128)(2,1)}, bf16[2048,512]{1,0:T(8,128)(2,1)}, f32[2048,128]{1,0:T(8,128)}, f32[2,136,2048]{2,1,0:T(8,128)}) custom-call(s32[4]{0:T(128)} %pad_add_fusion.1.pre, bf16[1024,4096]{1,0:T(8,128)(2,1)} %refs_0_.7, bf16[1024,4096]{1,0:T(8,128)(2,1)} %collective-permute-done.refs_1_, bf16[80,4096]{1,0:T(8,128)(2,1)} %bitcast.38, ...), custom_call_target="tpu_custom_call" | custom-call | flops 51200000000 | bytes 20480000 | tf_op jit(solution)/shard_map/front/pallas_call | solution.py:214
  161.7 4.7 slice.50
  169.6 30.3 %front.6 = (bf16[512,2048]{1,0:T(8,128)(2,1)}, bf16[512,512]{1,0:T(8,128)(2,1)}, f32[512,128]{1,0:T(8,128)}, f32[1,136,2048]{2,1,0:T(8,128)}) custom-call(s32[4]{0:T(128)} %pad_add_fusion.1.pre, bf16[512,4096]{1,0:T(8,128)(2,1)} %collective-permute-done.2.refs_0_.refs_1_, bf16[80,4096]{1,0:T(8,128)(2,1)} %bitcast.40, ...), custom_call_target="tpu_custom_call" | custom-call | flops 12800000000 | bytes 5120000 | tf_op jit(solution)/shard_map/front/pallas_call | solution.py:214
  200.0 29.3 %front.7 = (bf16[512,2048]{1,0:T(8,128)(2,1)}, bf16[512,512]{1,0:T(8,128)(2,1)}, f32[512,128]{1,0:T(8,128)}, f32[1,136,2048]{2,1,0:T(8,128)}) custom-call(s32[4]{0:T(128)} %pad_add_fusion.1.pre, bf16[512,4096]{1,0:T(8,128)(2,1)} %collective-permute-done.3.refs_0_.refs_1_, bf16[80,4096]{1,0:T(8,128)(2,1)} %bitcast.41, ...), custom_call_target="tpu_custom_call" | custom-call | flops 12800000000 | bytes 5120000 | tf_op jit(solution)/shard_map/front/pallas_call | solution.py:214
  229.3 30.7 %collective-permute-done.1.refs_0_ = bf16[512,4096]{1,0:T(8,128)(2,1)} collective-permute-done((bf16[512,4096]{1,0:T(8,128)(2,1)}, bf16[512,4096]{1,0:T(8,128)(2,1)}, u32[]{:S(2)}, u32[]{:S(2)}) %collective-permute-start.1) | collective-permute-done | bytes 4194336 | tf_op jit(solution)/shard_map/ppermute | solution.py:533
  261.7 29.8 %front.8 = (bf16[512,2048]{1,0:T(8,128)(2,1)}, bf16[512,512]{1,0:T(8,128)(2,1)}, f32[512,128]{1,0:T(8,128)}, f32[1,136,2048]{2,1,0:T(8,128)}) custom-call(s32[4]{0:T(128)} %pad_add_fusion.1.pre, bf16[512,4096]{1,0:T(8,128)(2,1)} %collective-permute-done.1.refs_0_, bf16[512,4096]{1,0:T(8,128)(2,1)} %collective-permute-done.2.refs_0_.refs_1_, ...), custom_call_target="tpu_custom_call" | custom-call | flops 12800000000 | bytes 5120000 | tf_op jit(solution)/shard_map/front/pallas_call | solution.py:214
  291.6 29.5 %front.9 = (bf16[512,2048]{1,0:T(8,128)(2,1)}, bf16[512,512]{1,0:T(8,128)(2,1)}, f32[512,128]{1,0:T(8,128)}, f32[1,136,2048]{2,1,0:T(8,128)}) custom-call(s32[4]{0:T(128)} %pad_add_fusion.1.pre, bf16[512,4096]{1,0:T(8,128)(2,1)} %collective-permute-done.4.refs_0_, bf16[512,4096]{1,0:T(8,128)(2,1)} %collective-permute-done.3.refs_0_.refs_1_, ...), custom_call_target="tpu_custom_call" | custom-call | flops 12800000000 | bytes 5120000 | tf_op jit(solution)/shard_map/front/pallas_call | solution.py:214
  324.0 36.2 %chain.1.refs_9_.refs_7_ = f32[4,128,2048]{2,1,0:T(8,128)S(1)} custom-call(f32[2,136,2048]{2,1,0:T(8,128)S(1)} %copy-done.1, f32[1,136,2048]{2,1,0:T(8,128)S(1)} %copy-done.2, f32[1,136,2048]{2,1,0:T(8,128)S(1)} %copy-done.3), custom_call_target="tpu_custom_call" | custom-call | tf_op jit(solution)/shard_map/chain/pallas_call | solution.py:477
  363.1 22.3 %mixz.8 = (bf16[512,2048]{1,0:T(8,128)(2,1)}, f32[1,128,2048]{2,1,0:T(8,128)}) custom-call(s32[4]{0:T(128)} %pad_add_fusion.1.pre, bf16[512,4096]{1,0:T(8,128)(2,1)} %collective-permute-done.3.refs_0_.refs_1_, f32[4096,128]{1,0:T(8,128)} %select_select_fusion.refs_4_.refs_5_.refs_2_.refs_3_.refs_1_, bf16[512,2048]{1,0:T(8,128)(2,1)} %get-tuple-element.85.refs_2_, ...), custom_call_target="tpu_custom_call" | custom-call | flops 10240000000 | bytes 7168000 | tf_op jit(solution)/shard_map/mixz/pallas_call | solution.py:309
  385.4 22.1 %mixz.9 = (bf16[512,2048]{1,0:T(8,128)(2,1)}, f32[1,128,2048]{2,1,0:T(8,128)}) custom-call(s32[4]{0:T(128)} %pad_add_fusion.1.pre, bf16[512,4096]{1,0:T(8,128)(2,1)} %collective-permute-done.4.refs_0_, f32[4096,128]{1,0:T(8,128)} %select_select_fusion.refs_4_.refs_5_.refs_2_.refs_3_.refs_1_, bf16[512,2048]{1,0:T(8,128)(2,1)} %get-tuple-element.82.refs_2_, ...), custom_call_target="tpu_custom_call" | custom-call | flops 10240000000 | bytes 7168000 | tf_op jit(solution)/shard_map/mixz/pallas_call | solution.py:309
  409.6 69.9 %mixz.5 = (bf16[2048,2048]{1,0:T(8,128)(2,1)}, f32[2,128,2048]{2,1,0:T(8,128)}) custom-call(s32[4]{0:T(128)} %pad_add_fusion.1.pre, bf16[1024,4096]{1,0:T(8,128)(2,1)} %refs_0_.7, bf16[1024,4096]{1,0:T(8,128)(2,1)} %collective-permute-done.refs_1_, f32[4096,128]{1,0:T(8,128)} %select_select_fusion.refs_4_.refs_5_.refs_2_.refs_3_.refs_1_, ...), custom_call_target="tpu_custom_call" | custom-call | flops 40960000000 | bytes 28672000 | tf_op jit(solution)/shard_map/mixz/pallas_call | solution.py:309
  479.5 20.4 %collective-permute-done.11.yr_ref = bf16[512,2048]{1,0:T(8,128)(2,1)} collective-permute-done((bf16[512,2048]{1,0:T(8,128)(2,1)}, bf16[512,2048]{1,0:T(8,128)(2,1)}, u32[]{:S(2)}, u32[]{:S(2)}) %collective-permute-start.11) | collective-permute-done | bytes 2097184 | tf_op jit(solution)/shard_map/ppermute | solution.py:533
  499.9 24.6 %out_proj.5 = f32[512,4096]{1,0:T(8,128)} custom-call(bf16[2048,2048]{1,0:T(8,128)(2,1)} %get-tuple-element.69.y_ref, bf16[512,2048]{1,0:T(8,128)(2,1)} %collective-permute-done.11.yr_ref, bf16[2048,4096]{1,0:T(8,128)(2,1)} %w_ref.7, bf16[1024,4096]{1,0:T(8,128)(2,1)} %all-gather.3.cloned.1.call-done.wr0_ref, ...), custom_call_target="tpu_custom_call" | custom-call | flops 16896000000 | bytes 51200000 | tf_op jit(solution)/shard_map/out_proj/pallas_call | solution.py:520
  525.8 24.4 %out_proj.4 = f32[512,4096]{1,0:T(8,128)} custom-call(bf16[2048,2048]{1,0:T(8,128)(2,1)} %get-tuple-element.69.y_ref, bf16[512,2048]{1,0:T(8,128)(2,1)} %copy-done.17, bf16[2048,4096]{1,0:T(8,128)(2,1)} %w_ref.7, bf16[1024,4096]{1,0:T(8,128)(2,1)} %all-gather.3.cloned.1.call-done.wr0_ref, bf16[1024,4096]{1,0:T(8,128)(2,1)} %all-gather.5.cloned.1.call-done.wr1_ref), custom_call_target="tpu_custom_call" | custom-call | flops 16896000000 | bytes 51200000 | tf_op jit(solution)/shard_map/out_proj/pallas_call | solution.py:520
  550.7 21.7 %mixz.6 = (bf16[512,2048]{1,0:T(8,128)(2,1)}, f32[1,128,2048]{2,1,0:T(8,128)}) custom-call(s32[4]{0:T(128)} %pad_add_fusion.1.pre, bf16[512,4096]{1,0:T(8,128)(2,1)} %collective-permute-done.2.refs_0_.refs_1_, f32[4096,128]{1,0:T(8,128)} %select_select_fusion.refs_4_.refs_5_.refs_2_.refs_3_.refs_1_, bf16[512,2048]{1,0:T(8,128)(2,1)} %get-tuple-element.73.refs_2_, ...), custom_call_target="tpu_custom_call" | custom-call | flops 10240000000 | bytes 7168000 | tf_op jit(solution)/shard_map/mixz/pallas_call | solution.py:309
  572.9 21.8 %mixz.7 = (bf16[512,2048]{1,0:T(8,128)(2,1)}, f32[1,128,2048]{2,1,0:T(8,128)}) custom-call(s32[4]{0:T(128)} %pad_add_fusion.1.pre, bf16[512,4096]{1,0:T(8,128)(2,1)} %collective-permute-done.1.refs_0_, f32[4096,128]{1,0:T(8,128)} %select_select_fusion.refs_4_.refs_5_.refs_2_.refs_3_.refs_1_, bf16[512,2048]{1,0:T(8,128)(2,1)} %get-tuple-element.70.refs_2_, ...), custom_call_target="tpu_custom_call" | custom-call | flops 10240000000 | bytes 7168000 | tf_op jit(solution)/shard_map/mixz/pallas_call | solution.py:309
  596.2 24.9 %collective-permute-done.10.yr_ref = bf16[512,2048]{1,0:T(8,128)(2,1)S(1)} collective-permute-done((bf16[512,2048]{1,0:T(8,128)(2,1)}, bf16[512,2048]{1,0:T(8,128)(2,1)S(1)}, u32[]{:S(2)}, u32[]{:S(2)}) %collective-permute-start.10) | collective-permute-done | bytes 2097184 | tf_op jit(solution)/shard_map/ppermute | solution.py:533
  622.5 25.8 %out_proj.6.refs_2_ = bf16[1024,4096]{1,0:T(8,128)(2,1)} custom-call(bf16[2048,2048]{1,0:T(8,128)(2,1)} %get-tuple-element.69.y_ref, bf16[512,2048]{1,0:T(8,128)(2,1)} %copy-done.6, bf16[2048,4096]{1,0:T(8,128)(2,1)} %w_ref.7, bf16[1024,4096]{1,0:T(8,128)(2,1)} %all-gather.3.cloned.1.call-done.wr0_ref, ...), custom_call_target="tpu_custom_call" | custom-call | flops 16896000000 | bytes 51200000 | tf_op jit(solution)/shard_map/out_proj/pallas_call | solution.py:520
  648.3 16.8 %collective-permute-done.5.yr_ref = bf16[512,2048]{1,0:T(8,128)(2,1)S(1)} collective-permute-done((bf16[512,2048]{1,0:T(8,128)(2,1)}, bf16[512,2048]{1,0:T(8,128)(2,1)S(1)}, u32[]{:S(2)}, u32[]{:S(2)}) %collective-permute-start.5) | collective-permute-done | bytes 2097184 | tf_op jit(solution)/shard_map/ppermute | solution.py:533
  666.4 25.8 %out_proj.7 = bf16[1024,4096]{1,0:T(8,128)(2,1)} custom-call(bf16[2048,2048]{1,0:T(8,128)(2,1)} %get-tuple-element.69.y_ref, bf16[512,2048]{1,0:T(8,128)(2,1)} %copy-done.7, bf16[2048,4096]{1,0:T(8,128)(2,1)} %w_ref.7, bf16[1024,4096]{1,0:T(8,128)(2,1)} %all-gather.3.cloned.1.call-done.wr0_ref, ...), custom_call_target="tpu_custom_call", output_to_operand_aliasing={{}: (7, {})} | custom-call | flops 16896000000 | bytes 51200000 | tf_op jit(solution)/shard_map/out_proj/pallas_call | solution.py:520
  (94 shorter events, 38.0 us)
Async XLA Ops:
  6.5 493.3 %all-gather.3.cloned.1.call-start = ((), (), s32[]{:S(2)}) async-start(), calls=%async_computation | async-start | bytes 9437184 | tf_op jit(solution)/shard_map/all_gather | solution.py:580
  19.0 49.1 %collective-permute-start = (bf16[1024,4096]{1,0:T(8,128)(2,1)}, bf16[1024,4096]{1,0:T(8,128)(2,1)}, u32[]{:S(2)}, u32[]{:S(2)}) collective-permute-start(bf16[1024,4096]{1,0:T(8,128)(2,1)} %refs_0_.7), channel_id=1, source_target_pairs={{0,1},{1,0},{2,3},{3,2},{4,5},{5,4},{6,7},{7,6},{8,9},{9,8},{10,11... | collective-permute-start | bytes 25165832 | tf_op jit(solution)/shard_map/ppermute | solution.py:533
  23.6 138.0 %collective-permute-start.2 = (bf16[512,4096]{1,0:T(8,128)(2,1)}, bf16[512,4096]{1,0:T(8,128)(2,1)}, u32[]{:S(2)}, u32[]{:S(2)}) collective-permute-start(bf16[512,4096]{1,0:T(8,128)(2,1)} %slice.49), channel_id=1, source_target_pairs={{0,2},{1,3},{2,0},{3,1},{4,6},{5,7},{6,4},{7,5},{8,10},{9,11},{10,... | collective-permute-start | bytes 12582920 | tf_op jit(solution)/shard_map/ppermute | solution.py:533
  28.7 132.9 %collective-permute-start.6 = (bf16[128,4096]{1,0:T(8,128)(2,1)S(1)}, bf16[128,4096]{1,0:T(8,128)(2,1)}, u32[]{:S(2)}, u32[]{:S(2)}) collective-permute-start(bf16[128,4096]{1,0:T(8,128)(2,1)S(1)} %get-tuple-element.78), channel_id=1, source_target_pairs={{0,2},{1,3},{2,0},{3,1},{4,6},{5,7},{6,4},{7,5},{8,10},{9,11},{10,... | collective-permute-start | bytes 3145736 | tf_op jit(solution)/shard_map/ppermute | solution.py:533
  52.8 6.5 copy-start.10
  52.9 6.5 copy-start.13
  52.9 6.5 copy-start.12
  52.9 7.2 %copy-start.14 = (f32[32]{0:T(128)S(1)}, f32[32]{0:T(128)}, u32[]{:S(2)}) copy-start(f32[32]{0:T(128)} %param.23) | copy-start | bytes 388
  52.9 7.2 %copy-start.15 = (f32[32]{0:T(128)S(1)}, f32[32]{0:T(128)}, u32[]{:S(2)}) copy-start(f32[32]{0:T(128)} %param.24) | copy-start | bytes 388
  52.9 9.2 %copy-start.9 = (bf16[4,2048]{1,0:T(4,128)(2,1)S(1)}, bf16[4,2048]{1,0:T(4,128)(2,1)}, u32[]{:S(2)}) copy-start(bf16[4,2048]{1,0:T(4,128)(2,1)} %param.19) | copy-start | bytes 49156
  161.6 338.3 %all-gather.5.cloned.1.call-start = ((), (), s32[]{:S(2)}) async-start(), calls=%async_computation.1 | async-start | bytes 9437184 | tf_op jit(solution)/shard_map/all_gather | solution.py:580
  161.6 38.3 %collective-permute-start.3 = (bf16[512,4096]{1,0:T(8,128)(2,1)}, bf16[512,4096]{1,0:T(8,128)(2,1)}, u32[]{:S(2)}, u32[]{:S(2)}) collective-permute-start(bf16[512,4096]{1,0:T(8,128)(2,1)} %collective-permute-done.2.refs_0_.refs_1_), channel_id=1, source_target_pairs={{0,1},{1,0},{2,3},{3,2},{4,5},{5,4},{6,7},{7,6},{8,9},{9,8},{10,11... | collective-permute-start | bytes 12582920 | tf_op jit(solution)/shard_map/ppermute | solution.py:533
  166.4 93.6 %collective-permute-start.1 = (bf16[512,4096]{1,0:T(8,128)(2,1)}, bf16[512,4096]{1,0:T(8,128)(2,1)}, u32[]{:S(2)}, u32[]{:S(2)}) collective-permute-start(bf16[512,4096]{1,0:T(8,128)(2,1)} %slice.50), channel_id=1, source_target_pairs={{0,2},{1,3},{2,0},{3,1},{4,6},{5,7},{6,4},{7,5},{8,10},{9,11},{10,... | collective-permute-start | bytes 12582920 | tf_op jit(solution)/shard_map/ppermute | solution.py:533
  260.0 31.6 %collective-permute-start.4 = (bf16[512,4096]{1,0:T(8,128)(2,1)}, bf16[512,4096]{1,0:T(8,128)(2,1)}, u32[]{:S(2)}, u32[]{:S(2)}) collective-permute-start(bf16[512,4096]{1,0:T(8,128)(2,1)} %collective-permute-done.1.refs_0_), channel_id=1, source_target_pairs={{0,1},{1,0},{2,3},{3,2},{4,5},{5,4},{6,7},{7,6},{8,9},{9,8},{10,11... | collective-permute-start | bytes 12582920 | tf_op jit(solution)/shard_map/ppermute | solution.py:533
  260.0 102.3 %collective-permute-start.7 = (bf16[128,4096]{1,0:T(8,128)(2,1)}, bf16[128,4096]{1,0:T(8,128)(2,1)}, u32[]{:S(2)}, u32[]{:S(2)}) collective-permute-start(bf16[128,4096]{1,0:T(8,128)(2,1)} %get-tuple-element.80), channel_id=1, source_target_pairs={{0,2},{1,3},{2,0},{3,1},{4,6},{5,7},{6,4},{7,5},{8,10},{9,11},{10,... | collective-permute-start | bytes 3145736 | tf_op jit(solution)/shard_map/ppermute | solution.py:533
  291.6 29.5 %copy-start.2 = (f32[1,136,2048]{2,1,0:T(8,128)S(1)}, f32[1,136,2048]{2,1,0:T(8,128)}, u32[]{:S(2)}) copy-start(f32[1,136,2048]{2,1,0:T(8,128)} %get-tuple-element.66.e2_ref) | copy-start | bytes 3342340
  324.0 38.3 %copy-start.11 = (bf16[2048]{0:T(1024)(128)(2,1)S(1)}, bf16[2048]{0:T(1024)(128)(2,1)}, u32[]{:S(2)}) copy-start(bf16[2048]{0:T(1024)(128)(2,1)} %param.26) | copy-start | bytes 12292
  324.0 38.3 %copy-start.16 = (f32[32]{0:T(128)S(1)}, f32[32]{0:T(128)}, u32[]{:S(2)}) copy-start(f32[32]{0:T(128)} %param.25) | copy-start | bytes 388
  407.5 116.9 %collective-permute-start.8 = (bf16[512,2048]{1,0:T(8,128)(2,1)}, bf16[512,2048]{1,0:T(8,128)(2,1)S(1)}, u32[]{:S(2)}, u32[]{:S(2)}) collective-permute-start(bf16[512,2048]{1,0:T(8,128)(2,1)} %get-tuple-element.90), channel_id=1, source_target_pairs={{0,2},{1,3},{2,0},{3,1},{4,6},{5,7},{6,4},{7,5},{8,10},{9,11},{10,... | collective-permute-start | bytes 6291464 | tf_op jit(solution)/shard_map/ppermute | solution.py:533
  407.9 91.9 %collective-permute-start.11 = (bf16[512,2048]{1,0:T(8,128)(2,1)}, bf16[512,2048]{1,0:T(8,128)(2,1)}, u32[]{:S(2)}, u32[]{:S(2)}) collective-permute-start(bf16[512,2048]{1,0:T(8,128)(2,1)} %get-tuple-element.92), channel_id=1, source_target_pairs={{0,2},{1,3},{2,0},{3,1},{4,6},{5,7},{6,4},{7,5},{8,10},{9,11},{10,... | collective-permute-start | bytes 6291464 | tf_op jit(solution)/shard_map/ppermute | solution.py:533
  524.4 96.7 %collective-permute-start.12 = (f32[512,4096]{1,0:T(8,128)}, f32[512,4096]{1,0:T(8,128)}, u32[]{:S(2)}, u32[]{:S(2)}) collective-permute-start(f32[512,4096]{1,0:T(8,128)} %out_proj.5), channel_id=1, source_target_pairs={{0,1},{1,0},{2,3},{3,2},{4,5},{5,4},{6,7},{7,6},{8,9},{9,8},{10,11... | collective-permute-start | bytes 25165832 | tf_op jit(solution)/shard_map/ppermute | solution.py:533
  550.2 114.9 %collective-permute-start.9 = (f32[512,4096]{1,0:T(8,128)}, f32[512,4096]{1,0:T(8,128)}, u32[]{:S(2)}, u32[]{:S(2)}) collective-permute-start(f32[512,4096]{1,0:T(8,128)} %out_proj.4), channel_id=1, source_target_pairs={{0,1},{1,0},{2,3},{3,2},{4,5},{5,4},{6,7},{7,6},{8,9},{9,8},{10,11... | collective-permute-start | bytes 25165832 | tf_op jit(solution)/shard_map/ppermute | solution.py:533
  572.4 48.7 %collective-permute-start.10 = (bf16[512,2048]{1,0:T(8,128)(2,1)}, bf16[512,2048]{1,0:T(8,128)(2,1)S(1)}, u32[]{:S(2)}, u32[]{:S(2)}) collective-permute-start(bf16[512,2048]{1,0:T(8,128)(2,1)} %get-tuple-element.91), channel_id=1, source_target_pairs={{0,2},{1,3},{2,0},{3,1},{4,6},{5,7},{6,4},{7,5},{8,10},{9,11},{10,... | collective-permute-start | bytes 6291464 | tf_op jit(solution)/shard_map/ppermute | solution.py:533
  594.6 70.5 %collective-permute-start.5 = (bf16[512,2048]{1,0:T(8,128)(2,1)}, bf16[512,2048]{1,0:T(8,128)(2,1)S(1)}, u32[]{:S(2)}, u32[]{:S(2)}) collective-permute-start(bf16[512,2048]{1,0:T(8,128)(2,1)} %get-tuple-element.77), channel_id=1, source_target_pairs={{0,2},{1,3},{2,0},{3,1},{4,6},{5,7},{6,4},{7,5},{8,10},{9,11},{10,... | collective-permute-start | bytes 6291464 | tf_op jit(solution)/shard_map/ppermute | solution.py:533
  (9 other events, 15.8 us)
Sparse Core Ops, SparseCore 0:
  161.7 123.9 all-gather.2
  362.4 123.4 all-gather.4

commit v2 on v1

--- a/solution.py
+++ b/solution.py
@@ -52,10 +52,10 @@
     return pl.ds(start if isinstance(start, int) else pl.multiple_of(start, 16), size)
 
 
-def front_kernel(pre, *refs, nx, per, hrows):
+def front_kernel(pre, *refs, nx, per, hrows, more):
     xs_, hs_, auxs = refs[:nx], refs[nx:2 * nx], refs[2 * nx:3 * nx]
-    (wx_ref, wb_ref, wdt_ref, cin_ref, cw_ref, cwb_ref, hp_ref,
-     xa_ref, bca_ref, dc_ref, cout_ref, xbuf, pbuf, bbuf, xw, bt, cum_all, wgt, abuf, sem) = refs[3 * nx:]
+    wx_ref, wb_ref, wdt_ref, cw_ref, cwb_ref, hp_ref, *cins = refs[3 * nx:][:6 + more]
+    (xa_ref, bca_ref, dc_ref, cout_ref, xbuf, pbuf, bbuf, xw, bt, cum_all, wgt, abuf, sem) = refs[3 * nx + 6 + more:]
     n = pl.program_id(0)
     last_n = XW // XT
     nm = nx * per
@@ -143,8 +143,12 @@
             for p in range(XT // T):
                 cs = slice(p * T, (p + 1) * T)
                 carry = pair_bcast(cr, p)
-                cout_ref[i, 0:T, cs] = cin_ref[i, 0:T, cs] * jnp.broadcast_to(carry[0:1], (T, T)) + upd[:, cs]
-                cout_ref[i, T:T + 8, cs] = cin_ref[i, T:T + 8, cs] * carry
+                if cins:
+                    cout_ref[i, :T, cs] = cins[0][i, :T, cs] * jnp.broadcast_to(carry[:1], (T, T)) + upd[:, cs]
+                    cout_ref[i, T:, cs] = cins[0][i, T:, cs] * carry
+                else:
+                    cout_ref[i, :T, cs] = upd[:, cs]
+                    cout_ref[i, T:, cs] = carry
 
     @pl.when(n == 0)
     def _():
@@ -202,7 +206,7 @@
     state = pl.BlockSpec((nx, T + 8, XT), lambda j, b: (0, 0, prev(j)))
     in_specs = [hbm] * (2 * nx) + [pl.BlockSpec((per * MT, T), lambda j, b, f=f: (f(b), 0), pipeline_mode=ONE) for f in amaps] + [
         pl.BlockSpec((D, XT), lambda j, b: (0, nt + jnp.minimum(j, nt - 1))), whole(D, NB), whole(D, HEADS),
-        state, cols(8), whole(8, NB), whole(8, T)]
+        cols(SUB), whole(SUB, NB), whole(SUB, T)] + ([] if cin is None else [state])
     gs = pltpu.PrefetchScalarGridSpec(
         num_scalar_prefetch=1, grid=(nt + 1,), in_specs=in_specs,
         out_specs=[cols(n), whole(n, NB, mode=None), whole(n, T, mode=None), state],
@@ -212,13 +216,13 @@
                         pltpu.SemaphoreType.DMA((nm,))],
     )
     return pl.pallas_call(
-        functools.partial(front_kernel, nx=nx, per=per, hrows=hrows), grid_spec=gs,
+        functools.partial(front_kernel, nx=nx, per=per, hrows=hrows, more=int(cin is not None)), grid_spec=gs,
         out_shape=[jax.ShapeDtypeStruct((n, XW), bf16), jax.ShapeDtypeStruct((n, NB), bf16),
                    jax.ShapeDtypeStruct((n, T), f32), jax.ShapeDtypeStruct((nx, T + 8, XW), f32)],
         compiler_params=pltpu.CompilerParams(dimension_semantics=("arbitrary",), vmem_limit_bytes=62 * MIB),
         cost_estimate=pl.CostEstimate(flops=n * 25_000_000, bytes_accessed=n * 10000, transcendentals=n * 4096),
         name="front",
-    )(pre, *xs, *halos, *[aux] * nx, w2, wb, wdt, cin, *consts)
+    )(pre, *xs, *halos, *[aux] * nx, w2, wb, wdt, *consts, *([] if cin is None else [cin]))
 
 
 def mixz_kernel(pre, *refs, nx):
@@ -237,7 +241,6 @@
             xv[...] = xs_[k][...]
             av[...] = auxs[k][...]
 
-    zbuf[...] = jnp.dot(xv[...], wz_ref[...], preferred_element_type=f32).astype(bf16).astype(f32)
     rows = lax.broadcasted_iota(jnp.int32, (T, T), 0)
     cols = lax.broadcasted_iota(jnp.int32, (T, T), 1)
     lo_half = cols < 64
@@ -256,6 +259,8 @@
         sm = jnp.where(mask, mac(cg, bg, 1, 1), 0.0)
         ybuf[...] = mac(cg, state[...].astype(bf16))
         sq = jnp.zeros((T, T), f32)
+        if t == 0:
+            zbuf[...] = jnp.dot(xv[...], wz_ref[...], preferred_element_type=f32).astype(bf16).astype(f32)
         for p in range(GW // T):
             cs = slice(p * T, (p + 1) * T)
             xa = xa_ref[rs, cs]
@@ -321,12 +326,26 @@
     return 2 * y + c
 
 
+NCH = 2
+
+
 def count(flag):
     return jnp.where(flag, 1, 0)
 
 
-def ahead_kernel(n_blocks, seg_ref, tail_ref, segs_ref, tails_ref, send_sem, recv_sem):
+def ahead_kernel(n_blocks, n_pl, seg_ref, tail_ref, x_hbm, w_hbm, segs_ref, tails_ref, x0_hbm, x1_hbm, w0_hbm, w1_hbm,
+                 xbuf, wbuf, in_sem, out_sem, send_sem, recv_sem):
     me, blk = lax.axis_index('tp'), lax.axis_index('sp')
+    step = w0_hbm.shape[0]
+    place = lax.axis_index('dp') * n_blocks + blk
+    moves = []
+    for k, (xo, wo) in enumerate(((x0_hbm, w0_hbm), (x1_hbm, w1_hbm))):
+        at = pl.multiple_of((k * n_pl + place) * step, HALO)
+        for j, (src, buf, dst) in enumerate(((x_hbm.at[pl.ds(k * xo.shape[0], xo.shape[0])], xbuf.at[k], xo),
+                                             (w_hbm.at[pl.ds(at, step)], wbuf.at[k], wo))):
+            moves.append((pltpu.make_async_copy(src, buf, in_sem.at[k, j]), pltpu.make_async_copy(buf, dst, out_sem.at[k, j])))
+    for load, _ in moves:
+        load.start()
     barrier = pltpu.get_barrier_semaphore()
     others = [{'tp': seq_slot(me, s)} for s in (1, 2, 3)]
     before = {'sp': jnp.maximum(blk - 1, 0), 'tp': 3}
@@ -364,6 +383,9 @@
             for c in cs:
                 c.start()
 
+    for load, store in moves:
+        load.wait()
+        store.start()
     segs_ref[me + 1] = seg_ref[...]
     tails_ref[me + 1] = tail_ref[...]
 
@@ -388,20 +410,26 @@
         for c in outer[0]:
             c.wait_recv()
 
-
-def ahead_call(seg, x, n_blocks):
+    for _, store in moves:
+        store.wait()
+
+
+def ahead_call(seg, x, w, n_blocks, n_pl):
     rows = x.shape[0]
-    vmem = pl.BlockSpec(memory_space=pltpu.VMEM)
+    half, step = rows // NCH, w.shape[0] // (NCH * n_pl)
+    vmem, hbm = pl.BlockSpec(memory_space=pltpu.VMEM), pl.BlockSpec(memory_space=pl.ANY)
+    sds = jax.ShapeDtypeStruct
     return pl.pallas_call(
-        functools.partial(ahead_kernel, n_blocks),
+        functools.partial(ahead_kernel, n_blocks, n_pl),
         grid=(1,),
-        in_specs=[vmem, pl.BlockSpec((HALO, D), lambda i: (rows // HALO - 1, 0))],
-        out_specs=[vmem, vmem],
-        out_shape=[jax.ShapeDtypeStruct((5, rows // T, T), jnp.int32), jax.ShapeDtypeStruct((5, HALO, D), bf16)],
-        scratch_shapes=[pltpu.SemaphoreType.DMA((7, 2)), pltpu.SemaphoreType.DMA((4, 2))],
-        compiler_params=pltpu.CompilerParams(collective_id=0, has_side_effects=True, vmem_limit_bytes=16 * MIB),
+        in_specs=[vmem, pl.BlockSpec((HALO, D), lambda i: (rows // HALO - 1, 0)), hbm, hbm],
+        out_specs=[vmem] * 2 + [hbm] * 4,
+        out_shape=[sds((5, rows // T, T), jnp.int32), sds((5, HALO, D), bf16)] + [sds((half, D), bf16)] * 2 + [sds((step, D), bf16)] * 2,
+        scratch_shapes=[pltpu.VMEM((NCH, half, D), bf16), pltpu.VMEM((NCH, step, D), bf16), pltpu.SemaphoreType.DMA((NCH, 2)),
+                        pltpu.SemaphoreType.DMA((NCH, 2)), pltpu.SemaphoreType.DMA((7, 2)), pltpu.SemaphoreType.DMA((4, 2))],
+        compiler_params=pltpu.CompilerParams(collective_id=0, has_side_effects=True, vmem_limit_bytes=24 * MIB),
         name="ahead",
-    )(seg.reshape(rows // T, T), x)
+    )(seg.reshape(rows // T, T), x, x, w)
 
 
 CW = 256
@@ -537,7 +565,6 @@
     return lax.optimization_barrier((v,) + deps)[0]
 
 
-NCH = 2
 CORE_SWAP = [(i, i ^ 1) for i in range(4)]
 CHIP_SWAP = [(i, i ^ 2) for i in range(4)]
 
@@ -562,19 +589,14 @@
 
     def body(x_loc, seg_loc, w_zx, w_bc, w_dt, conv_x, conv_bc, bias_x, bias_bc, a_log, dt_bias, d_skip, norm_w, w_out):
         rows, d = x_loc.shape
-        me, blk = lax.axis_index('tp'), lax.axis_index('sp')
+        me = lax.axis_index('tp')
         ch = rows // NCH
         per, kper = rows // MT, ch // MT
-        segs, tails = ahead_call(seg_loc, x_loc, n_blocks)
-        x_snd, segs = lax.optimization_barrier((x_loc, segs))
-        x_par = send(x_snd, CORE_SWAP)
-        parts = [x_snd[:ch]]
-        parts.append(after(x_snd, parts[0])[ch:])
-        x_dir = [send(v, CHIP_SWAP) for v in parts]
-        place = lax.axis_index('dp') * n_blocks + blk
-        half = w_out.shape[0] // 2
-        step = half // (mesh.shape['dp'] * n_blocks)
-        w_half = [send(after(lax.dynamic_slice(w_out, (h * half + place * step, 0), (step, d)), segs), CHIP_SWAP) for h in range(2)]
+        n_pl = mesh.shape['dp'] * n_blocks
+        segs, tails, *parts = ahead_call(seg_loc, x_loc, w_out, n_blocks, n_pl)
+        x_par = send(after(x_loc, segs), CORE_SWAP)
+        x_dir = [send(v, CHIP_SWAP) for v in parts[:NCH]]
+        w_half = [send(v, CHIP_SWAP) for v in parts[NCH:]]
 
         def w_gather(h, dep):
             return lax.all_gather(after(w_half[h], dep), ('dp', 'sp'), axis=0, tiled=True)
@@ -587,7 +609,6 @@
         cwb = pad(jnp.concatenate([conv_bc.reshape(4, NB), bias_bc.reshape(1, NB)], axis=0))
         hp1 = jnp.pad(jnp.stack([dt_bias, a_log]), ((0, 6), (0, T - HEADS)))
         hp2 = pad(jnp.stack([jnp.repeat(d_skip, HEAD), norm_w.astype(f32)]))
-        init = jnp.broadcast_to((jnp.arange(T + SUB) >= T).astype(f32)[None, :, None], (2, T + SUB, XW))
         pre = jnp.stack([seq_slot(me, s) for s in range(4)]).astype(jnp.int32)
         weights = (w2, wb, w_dt)
         consts = (cw, cwb, hp1)
@@ -597,16 +618,17 @@
                               weights, carry, consts, per=per)
 
         tail_row = lambda s: (lambda b: b[s] * HALO)
-        *own, ends = front((0, 1), 0, [x_loc, x_par], [tails] * 2, [tail_row(0), tail_row(1)], init, per)
+        *own, ends = front((0, 1), 0, [x_loc, x_par], [tails] * 2, [tail_row(0), tail_row(1)], None, per)
         w_rem = [w_gather(0, ends)]
         x_dir[0] = after(x_dir[0], ends)
-        rem, carry, x_fwd = [[], []], [init[:1], after(init[:1], ends)], []
+        rem, carry, x_fwd = [[], []], [None, None], []
+        last = ends
         for k in range(NCH):
             x_fwd.append(send(x_dir[k], CORE_SWAP))
             for r, xs in ((0, x_dir), (1, x_fwd)):
                 halo = (tails, tail_row(2 + r)) if k == 0 else (xs[k - 1], lambda b: ch - HALO)
-                c = after(carry[r], carry[0]) if r else after(carry[0], carry[1])
-                *arrs, carry[r] = front((2 + r,), k, [xs[k]], [halo[0]], [halo[1]], c, kper)
+                *arrs, carry[r] = front((2 + r,), k, [after(xs[k], last)], [halo[0]], [halo[1]], carry[r], kper)
+                last = carry[r]
                 rem[r].append(arrs)
             if k + 1 < NCH:
                 x_dir[k + 1] = after(x_dir[k + 1], carry[1])

time: 708 us -> 695 us (0.982)
  the two profiles are of different devices: /device:TPU:28 before, /device:TPU:30 now
where the time goes in v2:
time: 695 us; the launch traced here: 687 us
  Pallas kernels  511 us (74%)
  waiting for transfers between devices  98 us (14%)
  local copies, waits for them, and re-layouts  43.3 us (6%)
  between operations  14 us (2%)
  starting transfers between devices  11 us (2%)
  other arithmetic  9.33 us (1%)
    pallas_call x5, Pallas kernels, front_call(): pl.pallas_call(functools.partial(front_kernel, nx=nx, per=per, hrows=hrow...  210 us
    pallas_call x5, Pallas kernels, mixz_call(): pl.pallas_call(functools.partial(mixz_kernel, nx=nx), grid_spec=gs, out_s...  154 us
    pallas_call x4, Pallas kernels, out_call(): pl.pallas_call(out_kernel, grid=(D // NT,), in_specs=specs, out_specs=pl....  100 us
    ppermute x13, waiting for transfers between devices, send(): return lax.ppermute(v, 'tp', perm)  98 us
    unnamed x43, local copies, waits for them, and re-layouts  42.1 us
    pallas_call x1, Pallas kernels, chain_call(): pl.pallas_call(functools.partial(chain_kernel, n_blocks), in_specs=[hbm]...  36.3 us
  transfers between devices with their start and end apart: 15, of which 4 were waited for; matrix products, arithmetic and copies ran while one was open for 6% of the time, Pallas kernels for 69%

profile of v2, /device:TPU:30, one launch (start us, length us, event | category | flops | bytes accessed | tf_op | source)
XLA Modules:
  0.0 687.0 jit_solution(6327575689089493293)
XLA Ops:
  7.2 10.9 %ahead.1 = (s32[5,8,128]{2,1,0:T(8,128)S(1)}, bf16[5,16,4096]{2,1,0:T(8,128)(2,1)S(1)}, bf16[512,4096]{1,0:T(8,128)(2,1)}, bf16[512,4096]{1,0:T(8,128)(2,1)S(1)}...) custom-call(s32[8,128]{1,0:T(8,128)S(1)} %bitcast.37, bf16[1024,4096]{1,0:T(8,128)(2,1)} %refs_0_.7, ...), custom_call_target="tpu_custom_call" | custom-call | tf_op jit(solution)/shard_map/ahead/pallas_call | solution.py:422
  21.0 2.3 collective-permute-start.2
  24.3 23.2 %copy.21 = bf16[512,8,2,2048]{3,1,2,0:T(8,128)(2,1)} copy(bf16[512,8,2,2048]{3,2,1,0:T(2,128)(2,1)} %bitcast.57) | data formatting | bytes 67108864
  47.6 5.1 copy.22
  57.5 5.3 select_select_fusion.refs_4_.refs_5_.refs_2_.refs_3_.refs_1_
  62.7 91.7 %front.5 = (bf16[2048,2048]{1,0:T(8,128)(2,1)}, bf16[2048,512]{1,0:T(8,128)(2,1)}, f32[2048,128]{1,0:T(8,128)}, f32[2,136,2048]{2,1,0:T(8,128)}) custom-call(s32[4]{0:T(128)} %pad_add_fusion.1.pre, bf16[1024,4096]{1,0:T(8,128)(2,1)} %refs_0_.7, bf16[1024,4096]{1,0:T(8,128)(2,1)} %collective-permute-done.refs_1_, bf16[80,4096]{1,0:T(8,128)(2,1)} %bitcast.38, ...), custom_call_target="tpu_custom_call" | custom-call | flops 51200000000 | bytes 20480000 | tf_op jit(solution)/shard_map/front/pallas_call | solution.py:218
  156.9 29.1 %front.6 = (bf16[512,2048]{1,0:T(8,128)(2,1)}, bf16[512,512]{1,0:T(8,128)(2,1)}, f32[512,128]{1,0:T(8,128)}, f32[1,136,2048]{2,1,0:T(8,128)}) custom-call(s32[4]{0:T(128)} %pad_add_fusion.1.pre, bf16[512,4096]{1,0:T(8,128)(2,1)} %collective-permute-done.2.refs_0_.refs_1_, bf16[80,4096]{1,0:T(8,128)(2,1)} %bitcast.40, ...), custom_call_target="tpu_custom_call" | custom-call | flops 12800000000 | bytes 5120000 | tf_op jit(solution)/shard_map/front/pallas_call | solution.py:218
  186.0 29.2 %front.7 = (bf16[512,2048]{1,0:T(8,128)(2,1)}, bf16[512,512]{1,0:T(8,128)(2,1)}, f32[512,128]{1,0:T(8,128)}, f32[1,136,2048]{2,1,0:T(8,128)}) custom-call(s32[4]{0:T(128)} %pad_add_fusion.1.pre, bf16[512,4096]{1,0:T(8,128)(2,1)} %collective-permute-done.3.refs_0_.refs_1_, bf16[80,4096]{1,0:T(8,128)(2,1)} %bitcast.41, ...), custom_call_target="tpu_custom_call" | custom-call | flops 12800000000 | bytes 5120000 | tf_op jit(solution)/shard_map/front/pallas_call | solution.py:218
  215.2 33.1 %collective-permute-done.1.refs_0_ = bf16[512,4096]{1,0:T(8,128)(2,1)} collective-permute-done((bf16[512,4096]{1,0:T(8,128)(2,1)}, bf16[512,4096]{1,0:T(8,128)(2,1)}, u32[]{:S(2)}, u32[]{:S(2)}) %collective-permute-start.1) | collective-permute-done | bytes 4194336 | tf_op jit(solution)/shard_map/ppermute | solution.py:561
  250.1 30.1 %front.8 = (bf16[512,2048]{1,0:T(8,128)(2,1)}, bf16[512,512]{1,0:T(8,128)(2,1)}, f32[512,128]{1,0:T(8,128)}, f32[1,136,2048]{2,1,0:T(8,128)}) custom-call(s32[4]{0:T(128)} %pad_add_fusion.1.pre, bf16[512,4096]{1,0:T(8,128)(2,1)} %collective-permute-done.1.refs_0_, bf16[512,4096]{1,0:T(8,128)(2,1)} %collective-permute-done.2.refs_0_.refs_1_, ...), custom_call_target="tpu_custom_call" | custom-call | flops 12800000000 | bytes 5120000 | tf_op jit(solution)/shard_map/front/pallas_call | solution.py:218
  280.2 29.5 %front.9 = (bf16[512,2048]{1,0:T(8,128)(2,1)}, bf16[512,512]{1,0:T(8,128)(2,1)}, f32[512,128]{1,0:T(8,128)}, f32[1,136,2048]{2,1,0:T(8,128)}) custom-call(s32[4]{0:T(128)} %pad_add_fusion.1.pre, bf16[512,4096]{1,0:T(8,128)(2,1)} %collective-permute-done.4.refs_0_, bf16[512,4096]{1,0:T(8,128)(2,1)} %collective-permute-done.3.refs_0_.refs_1_, ...), custom_call_target="tpu_custom_call" | custom-call | flops 12800000000 | bytes 5120000 | tf_op jit(solution)/shard_map/front/pallas_call | solution.py:218
  312.7 36.3 %chain.1.refs_9_.refs_7_ = f32[4,128,2048]{2,1,0:T(8,128)S(1)} custom-call(f32[2,136,2048]{2,1,0:T(8,128)S(1)} %copy-done.1, f32[1,136,2048]{2,1,0:T(8,128)S(1)} %copy-done.2, f32[1,136,2048]{2,1,0:T(8,128)S(1)} %copy-done.3), custom_call_target="tpu_custom_call" | custom-call | tf_op jit(solution)/shard_map/chain/pallas_call | solution.py:505
  351.9 21.9 %mixz.8 = (bf16[512,2048]{1,0:T(8,128)(2,1)}, f32[1,128,2048]{2,1,0:T(8,128)}) custom-call(s32[4]{0:T(128)} %pad_add_fusion.1.pre, bf16[512,4096]{1,0:T(8,128)(2,1)} %collective-permute-done.3.refs_0_.refs_1_, f32[4096,128]{1,0:T(8,128)} %select_select_fusion.refs_4_.refs_5_.refs_2_.refs_3_.refs_1_, bf16[512,2048]{1,0:T(8,128)(2,1)} %get-tuple-element.83.refs_2_, ...), custom_call_target="tpu_custom_call" | custom-call | flops 10240000000 | bytes 7168000 | tf_op jit(solution)/shard_map/mixz/pallas_call | solution.py:314
  373.8 21.6 %mixz.9 = (bf16[512,2048]{1,0:T(8,128)(2,1)}, f32[1,128,2048]{2,1,0:T(8,128)}) custom-call(s32[4]{0:T(128)} %pad_add_fusion.1.pre, bf16[512,4096]{1,0:T(8,128)(2,1)} %collective-permute-done.4.refs_0_, f32[4096,128]{1,0:T(8,128)} %select_select_fusion.refs_4_.refs_5_.refs_2_.refs_3_.refs_1_, bf16[512,2048]{1,0:T(8,128)(2,1)} %get-tuple-element.80.refs_2_, ...), custom_call_target="tpu_custom_call" | custom-call | flops 10240000000 | bytes 7168000 | tf_op jit(solution)/shard_map/mixz/pallas_call | solution.py:314
  397.5 67.5 %mixz.5 = (bf16[2048,2048]{1,0:T(8,128)(2,1)}, f32[2,128,2048]{2,1,0:T(8,128)}) custom-call(s32[4]{0:T(128)} %pad_add_fusion.1.pre, bf16[1024,4096]{1,0:T(8,128)(2,1)} %refs_0_.7, bf16[1024,4096]{1,0:T(8,128)(2,1)} %collective-permute-done.refs_1_, f32[4096,128]{1,0:T(8,128)} %select_select_fusion.refs_4_.refs_5_.refs_2_.refs_3_.refs_1_, ...), custom_call_target="tpu_custom_call" | custom-call | flops 40960000000 | bytes 28672000 | tf_op jit(solution)/shard_map/mixz/pallas_call | solution.py:314
  465.0 22.8 %collective-permute-done.11.yr_ref = bf16[512,2048]{1,0:T(8,128)(2,1)} collective-permute-done((bf16[512,2048]{1,0:T(8,128)(2,1)}, bf16[512,2048]{1,0:T(8,128)(2,1)}, u32[]{:S(2)}, u32[]{:S(2)}) %collective-permute-start.11) | collective-permute-done | bytes 2097184 | tf_op jit(solution)/shard_map/ppermute | solution.py:561
  487.8 24.6 %out_proj.5 = f32[512,4096]{1,0:T(8,128)} custom-call(bf16[2048,2048]{1,0:T(8,128)(2,1)} %get-tuple-element.67.y_ref, bf16[512,2048]{1,0:T(8,128)(2,1)} %collective-permute-done.11.yr_ref, bf16[2048,4096]{1,0:T(8,128)(2,1)} %w_ref.7, bf16[1024,4096]{1,0:T(8,128)(2,1)} %all-gather.3.cloned.1.call-done.wr0_ref, ...), custom_call_target="tpu_custom_call" | custom-call | flops 16896000000 | bytes 51200000 | tf_op jit(solution)/shard_map/out_proj/pallas_call | solution.py:548
  513.7 24.4 %out_proj.4 = f32[512,4096]{1,0:T(8,128)} custom-call(bf16[2048,2048]{1,0:T(8,128)(2,1)} %get-tuple-element.67.y_ref, bf16[512,2048]{1,0:T(8,128)(2,1)} %copy-done.18, bf16[2048,4096]{1,0:T(8,128)(2,1)} %w_ref.7, bf16[1024,4096]{1,0:T(8,128)(2,1)} %all-gather.3.cloned.1.call-done.wr0_ref, bf16[1024,4096]{1,0:T(8,128)(2,1)} %all-gather.5.cloned.1.call-done.wr1_ref), custom_call_target="tpu_custom_call" | custom-call | flops 16896000000 | bytes 51200000 | tf_op jit(solution)/shard_map/out_proj/pallas_call | solution.py:548
  538.6 21.5 %mixz.6 = (bf16[512,2048]{1,0:T(8,128)(2,1)}, f32[1,128,2048]{2,1,0:T(8,128)}) custom-call(s32[4]{0:T(128)} %pad_add_fusion.1.pre, bf16[512,4096]{1,0:T(8,128)(2,1)} %collective-permute-done.2.refs_0_.refs_1_, f32[4096,128]{1,0:T(8,128)} %select_select_fusion.refs_4_.refs_5_.refs_2_.refs_3_.refs_1_, bf16[512,2048]{1,0:T(8,128)(2,1)} %get-tuple-element.71.refs_2_, ...), custom_call_target="tpu_custom_call" | custom-call | flops 10240000000 | bytes 7168000 | tf_op jit(solution)/shard_map/mixz/pallas_call | solution.py:314
  560.4 21.5 %mixz.7 = (bf16[512,2048]{1,0:T(8,128)(2,1)}, f32[1,128,2048]{2,1,0:T(8,128)}) custom-call(s32[4]{0:T(128)} %pad_add_fusion.1.pre, bf16[512,4096]{1,0:T(8,128)(2,1)} %collective-permute-done.1.refs_0_, f32[4096,128]{1,0:T(8,128)} %select_select_fusion.refs_4_.refs_5_.refs_2_.refs_3_.refs_1_, bf16[512,2048]{1,0:T(8,128)(2,1)} %get-tuple-element.68.refs_2_, ...), custom_call_target="tpu_custom_call" | custom-call | flops 10240000000 | bytes 7168000 | tf_op jit(solution)/shard_map/mixz/pallas_call | solution.py:314
  583.6 25.2 %collective-permute-done.10.yr_ref = bf16[512,2048]{1,0:T(8,128)(2,1)S(1)} collective-permute-done((bf16[512,2048]{1,0:T(8,128)(2,1)}, bf16[512,2048]{1,0:T(8,128)(2,1)S(1)}, u32[]{:S(2)}, u32[]{:S(2)}) %collective-permute-start.10) | collective-permute-done | bytes 2097184 | tf_op jit(solution)/shard_map/ppermute | solution.py:561
  610.1 25.8 %out_proj.6.refs_2_ = bf16[1024,4096]{1,0:T(8,128)(2,1)} custom-call(bf16[2048,2048]{1,0:T(8,128)(2,1)} %get-tuple-element.67.y_ref, bf16[512,2048]{1,0:T(8,128)(2,1)} %copy-done.7, bf16[2048,4096]{1,0:T(8,128)(2,1)} %w_ref.7, bf16[1024,4096]{1,0:T(8,128)(2,1)} %all-gather.3.cloned.1.call-done.wr0_ref, ...), custom_call_target="tpu_custom_call" | custom-call | flops 16896000000 | bytes 51200000 | tf_op jit(solution)/shard_map/out_proj/pallas_call | solution.py:548
  635.9 16.8 %collective-permute-done.5.yr_ref = bf16[512,2048]{1,0:T(8,128)(2,1)S(1)} collective-permute-done((bf16[512,2048]{1,0:T(8,128)(2,1)}, bf16[512,2048]{1,0:T(8,128)(2,1)S(1)}, u32[]{:S(2)}, u32[]{:S(2)}) %collective-permute-start.5) | collective-permute-done | bytes 2097184 | tf_op jit(solution)/shard_map/ppermute | solution.py:561
  654.1 25.8 %out_proj.7 = bf16[1024,4096]{1,0:T(8,128)(2,1)} custom-call(bf16[2048,2048]{1,0:T(8,128)(2,1)} %get-tuple-element.67.y_ref, bf16[512,2048]{1,0:T(8,128)(2,1)} %copy-done.8, bf16[2048,4096]{1,0:T(8,128)(2,1)} %w_ref.7, bf16[1024,4096]{1,0:T(8,128)(2,1)} %all-gather.3.cloned.1.call-done.wr0_ref, ...), custom_call_target="tpu_custom_call", output_to_operand_aliasing={{}: (7, {})} | custom-call | flops 16896000000 | bytes 51200000 | tf_op jit(solution)/shard_map/out_proj/pallas_call | solution.py:548
  (90 shorter events, 27.8 us)
Async XLA Ops:
  6.5 481.3 %all-gather.3.cloned.1.call-start = ((), (), s32[]{:S(2)}) async-start(), calls=%async_computation | async-start | bytes 9437184 | tf_op jit(solution)/shard_map/all_gather | solution.py:602
  20.9 41.8 %collective-permute-start = (bf16[1024,4096]{1,0:T(8,128)(2,1)}, bf16[1024,4096]{1,0:T(8,128)(2,1)}, u32[]{:S(2)}, u32[]{:S(2)}) collective-permute-start(bf16[1024,4096]{1,0:T(8,128)(2,1)} %refs_0_.7), channel_id=1, source_target_pairs={{0,1},{1,0},{2,3},{3,2},{4,5},{5,4},{6,7},{7,6},{8,9},{9,8},{10,11... | collective-permute-start | bytes 25165832 | tf_op jit(solution)/shard_map/ppermute | solution.py:561
  21.0 133.7 %collective-permute-start.2 = (bf16[512,4096]{1,0:T(8,128)(2,1)}, bf16[512,4096]{1,0:T(8,128)(2,1)}, u32[]{:S(2)}, u32[]{:S(2)}) collective-permute-start(bf16[512,4096]{1,0:T(8,128)(2,1)} %get-tuple-element.56), channel_id=1, source_target_pairs={{0,2},{1,3},{2,0},{3,1},{4,6},{5,7},{6,4},{7,5},{8,10},{9,11},{10,... | collective-permute-start | bytes 12582920 | tf_op jit(solution)/shard_map/ppermute | solution.py:561
  23.2 131.2 %collective-permute-start.6 = (bf16[128,4096]{1,0:T(8,128)(2,1)S(1)}, bf16[128,4096]{1,0:T(8,128)(2,1)}, u32[]{:S(2)}, u32[]{:S(2)}) collective-permute-start(bf16[128,4096]{1,0:T(8,128)(2,1)S(1)} %get-tuple-element.76), channel_id=1, source_target_pairs={{0,2},{1,3},{2,0},{3,1},{4,6},{5,7},{6,4},{7,5},{8,10},{9,11},{10,... | collective-permute-start | bytes 3145736 | tf_op jit(solution)/shard_map/ppermute | solution.py:561
  47.5 6.5 copy-start.11
  47.5 6.5 copy-start.14
  47.5 6.5 copy-start.13
  47.5 7.2 %copy-start.15 = (f32[32]{0:T(128)S(1)}, f32[32]{0:T(128)}, u32[]{:S(2)}) copy-start(f32[32]{0:T(128)} %param.23) | copy-start | bytes 388
  47.5 7.2 %copy-start.16 = (f32[32]{0:T(128)S(1)}, f32[32]{0:T(128)}, u32[]{:S(2)}) copy-start(f32[32]{0:T(128)} %param.24) | copy-start | bytes 388
  47.6 9.2 %copy-start.10 = (bf16[4,2048]{1,0:T(4,128)(2,1)S(1)}, bf16[4,2048]{1,0:T(4,128)(2,1)}, u32[]{:S(2)}) copy-start(bf16[4,2048]{1,0:T(4,128)(2,1)} %param.19) | copy-start | bytes 49156
  154.5 333.3 %all-gather.5.cloned.1.call-start = ((), (), s32[]{:S(2)}) async-start(), calls=%async_computation.1 | async-start | bytes 9437184 | tf_op jit(solution)/shard_map/all_gather | solution.py:602
  154.7 31.3 %collective-permute-start.3 = (bf16[512,4096]{1,0:T(8,128)(2,1)}, bf16[512,4096]{1,0:T(8,128)(2,1)}, u32[]{:S(2)}, u32[]{:S(2)}) collective-permute-start(bf16[512,4096]{1,0:T(8,128)(2,1)} %collective-permute-done.2.refs_0_.refs_1_), channel_id=1, source_target_pairs={{0,1},{1,0},{2,3},{3,2},{4,5},{5,4},{6,7},{7,6},{8,9},{9,8},{10,11... | collective-permute-start | bytes 12582920 | tf_op jit(solution)/shard_map/ppermute | solution.py:561
  154.8 93.5 %collective-permute-start.1 = (bf16[512,4096]{1,0:T(8,128)(2,1)}, bf16[512,4096]{1,0:T(8,128)(2,1)}, u32[]{:S(2)}, u32[]{:S(2)}) collective-permute-start(bf16[512,4096]{1,0:T(8,128)(2,1)} %copy-done.5), channel_id=1, source_target_pairs={{0,2},{1,3},{2,0},{3,1},{4,6},{5,7},{6,4},{7,5},{8,10},{9,11},{10,... | collective-permute-start | bytes 12582920 | tf_op jit(solution)/shard_map/ppermute | solution.py:561
  248.3 31.9 %collective-permute-start.4 = (bf16[512,4096]{1,0:T(8,128)(2,1)}, bf16[512,4096]{1,0:T(8,128)(2,1)}, u32[]{:S(2)}, u32[]{:S(2)}) collective-permute-start(bf16[512,4096]{1,0:T(8,128)(2,1)} %collective-permute-done.1.refs_0_), channel_id=1, source_target_pairs={{0,1},{1,0},{2,3},{3,2},{4,5},{5,4},{6,7},{7,6},{8,9},{9,8},{10,11... | collective-permute-start | bytes 12582920 | tf_op jit(solution)/shard_map/ppermute | solution.py:561
  248.3 102.7 %collective-permute-start.7 = (bf16[128,4096]{1,0:T(8,128)(2,1)}, bf16[128,4096]{1,0:T(8,128)(2,1)}, u32[]{:S(2)}, u32[]{:S(2)}) collective-permute-start(bf16[128,4096]{1,0:T(8,128)(2,1)} %get-tuple-element.78), channel_id=1, source_target_pairs={{0,2},{1,3},{2,0},{3,1},{4,6},{5,7},{6,4},{7,5},{8,10},{9,11},{10,... | collective-permute-start | bytes 3145736 | tf_op jit(solution)/shard_map/ppermute | solution.py:561
  280.2 29.6 %copy-start.2 = (f32[1,136,2048]{2,1,0:T(8,128)S(1)}, f32[1,136,2048]{2,1,0:T(8,128)}, u32[]{:S(2)}) copy-start(f32[1,136,2048]{2,1,0:T(8,128)} %get-tuple-element.64.e2_ref) | copy-start | bytes 3342340
  312.7 38.4 %copy-start.12 = (bf16[2048]{0:T(1024)(128)(2,1)S(1)}, bf16[2048]{0:T(1024)(128)(2,1)}, u32[]{:S(2)}) copy-start(bf16[2048]{0:T(1024)(128)(2,1)} %param.26) | copy-start | bytes 12292
  312.7 38.4 %copy-start.17 = (f32[32]{0:T(128)S(1)}, f32[32]{0:T(128)}, u32[]{:S(2)}) copy-start(f32[32]{0:T(128)} %param.25) | copy-start | bytes 388
  395.5 116.9 %collective-permute-start.8 = (bf16[512,2048]{1,0:T(8,128)(2,1)}, bf16[512,2048]{1,0:T(8,128)(2,1)S(1)}, u32[]{:S(2)}, u32[]{:S(2)}) collective-permute-start(bf16[512,2048]{1,0:T(8,128)(2,1)} %get-tuple-element.88), channel_id=1, source_target_pairs={{0,2},{1,3},{2,0},{3,1},{4,6},{5,7},{6,4},{7,5},{8,10},{9,11},{10,... | collective-permute-start | bytes 6291464 | tf_op jit(solution)/shard_map/ppermute | solution.py:561
  395.8 92.0 %collective-permute-start.11 = (bf16[512,2048]{1,0:T(8,128)(2,1)}, bf16[512,2048]{1,0:T(8,128)(2,1)}, u32[]{:S(2)}, u32[]{:S(2)}) collective-permute-start(bf16[512,2048]{1,0:T(8,128)(2,1)} %get-tuple-element.90), channel_id=1, source_target_pairs={{0,2},{1,3},{2,0},{3,1},{4,6},{5,7},{6,4},{7,5},{8,10},{9,11},{10,... | collective-permute-start | bytes 6291464 | tf_op jit(solution)/shard_map/ppermute | solution.py:561
  512.4 96.4 %collective-permute-start.12 = (f32[512,4096]{1,0:T(8,128)}, f32[512,4096]{1,0:T(8,128)}, u32[]{:S(2)}, u32[]{:S(2)}) collective-permute-start(f32[512,4096]{1,0:T(8,128)} %out_proj.5), channel_id=1, source_target_pairs={{0,1},{1,0},{2,3},{3,2},{4,5},{5,4},{6,7},{7,6},{8,9},{9,8},{10,11... | collective-permute-start | bytes 25165832 | tf_op jit(solution)/shard_map/ppermute | solution.py:561
  538.1 114.7 %collective-permute-start.9 = (f32[512,4096]{1,0:T(8,128)}, f32[512,4096]{1,0:T(8,128)}, u32[]{:S(2)}, u32[]{:S(2)}) collective-permute-start(f32[512,4096]{1,0:T(8,128)} %out_proj.4), channel_id=1, source_target_pairs={{0,1},{1,0},{2,3},{3,2},{4,5},{5,4},{6,7},{7,6},{8,9},{9,8},{10,11... | collective-permute-start | bytes 25165832 | tf_op jit(solution)/shard_map/ppermute | solution.py:561
  560.1 48.7 %collective-permute-start.10 = (bf16[512,2048]{1,0:T(8,128)(2,1)}, bf16[512,2048]{1,0:T(8,128)(2,1)S(1)}, u32[]{:S(2)}, u32[]{:S(2)}) collective-permute-start(bf16[512,2048]{1,0:T(8,128)(2,1)} %get-tuple-element.89), channel_id=1, source_target_pairs={{0,2},{1,3},{2,0},{3,1},{4,6},{5,7},{6,4},{7,5},{8,10},{9,11},{10,... | collective-permute-start | bytes 6291464 | tf_op jit(solution)/shard_map/ppermute | solution.py:561
  581.9 70.8 %collective-permute-start.5 = (bf16[512,2048]{1,0:T(8,128)(2,1)}, bf16[512,2048]{1,0:T(8,128)(2,1)S(1)}, u32[]{:S(2)}, u32[]{:S(2)}) collective-permute-start(bf16[512,2048]{1,0:T(8,128)(2,1)} %get-tuple-element.75), channel_id=1, source_target_pairs={{0,2},{1,3},{2,0},{3,1},{4,6},{5,7},{6,4},{7,5},{8,10},{9,11},{10,... | collective-permute-start | bytes 6291464 | tf_op jit(solution)/shard_map/ppermute | solution.py:561
  (10 other events, 17.7 us)
Sparse Core Ops, SparseCore 0:
  154.6 123.0 all-gather.2
  351.2 122.5 all-gather.4

commit v3 on v2

--- a/solution.py
+++ b/solution.py
@@ -52,10 +52,10 @@
     return pl.ds(start if isinstance(start, int) else pl.multiple_of(start, 16), size)
 
 
-def front_kernel(pre, *refs, nx, per, hrows, more):
+def front_kernel(pre, *refs, nx, per, hrows, more, skip):
     xs_, hs_, auxs = refs[:nx], refs[nx:2 * nx], refs[2 * nx:3 * nx]
     wx_ref, wb_ref, wdt_ref, cw_ref, cwb_ref, hp_ref, *cins = refs[3 * nx:][:6 + more]
-    (xa_ref, bca_ref, dc_ref, cout_ref, xbuf, pbuf, bbuf, xw, bt, cum_all, wgt, abuf, sem) = refs[3 * nx + 6 + more:]
+    (xa_ref, bca_ref, dc_ref, cout_ref, xbuf, pbuf, bbuf, xw, bt, cum_all, wgt, abuf, sem) = refs[3 * nx + 6 + more + skip:]
     n = pl.program_id(0)
     last_n = XW // XT
     nm = nx * per
@@ -193,7 +193,7 @@
         end_state()
 
 
-def front_call(pre, aux, amaps, xs, halos, hrows, weights, cin, consts, *, per):
+def front_call(pre, aux, amaps, xs, halos, hrows, weights, cin, consts, into, part, parts, *, per):
     nx = len(xs)
     nm = nx * per
     n = nm * MT
@@ -201,33 +201,35 @@
     w2, wb, wdt = weights
     hbm = pl.BlockSpec(memory_space=pl.ANY)
     prev = lambda j: jnp.maximum(j - 1, 0)
-    whole = lambda *shape, mode=ONE: pl.BlockSpec(shape, lambda j, b: (0,) * len(shape), pipeline_mode=mode)
-    cols = lambda k: pl.BlockSpec((k, XT), lambda j, b: (0, prev(j)))
+    whole = lambda *shape, mode=ONE, r=0: pl.BlockSpec(shape, lambda j, b: (r, 0), pipeline_mode=mode)
+    cols = lambda k, r=0: pl.BlockSpec((k, XT), lambda j, b: (r, prev(j)))
     state = pl.BlockSpec((nx, T + 8, XT), lambda j, b: (0, 0, prev(j)))
     in_specs = [hbm] * (2 * nx) + [pl.BlockSpec((per * MT, T), lambda j, b, f=f: (f(b), 0), pipeline_mode=ONE) for f in amaps] + [
         pl.BlockSpec((D, XT), lambda j, b: (0, nt + jnp.minimum(j, nt - 1))), whole(D, NB), whole(D, HEADS),
-        cols(SUB), whole(SUB, NB), whole(SUB, T)] + ([] if cin is None else [state])
+        cols(SUB), whole(SUB, NB), whole(SUB, T)] + ([] if cin is None else [state]) + [hbm] * len(into)
+    n_in = len(in_specs) + 1
     gs = pltpu.PrefetchScalarGridSpec(
         num_scalar_prefetch=1, grid=(nt + 1,), in_specs=in_specs,
-        out_specs=[cols(n), whole(n, NB, mode=None), whole(n, T, mode=None), state],
+        out_specs=[cols(n, part), whole(n, NB, mode=None, r=part), whole(n, T, mode=None, r=part), state],
         scratch_shapes=[pltpu.VMEM((nm, MH, D), bf16), pltpu.VMEM((2, nm, MH, XT), f32), pltpu.VMEM((MH, NB + T), f32),
                         pltpu.VMEM((n, XT), bf16), pltpu.VMEM((nx, 2, T, per * MT), bf16),
                         pltpu.VMEM((n + 8 * (nx + 1), T), f32), pltpu.VMEM((n, T), f32), pltpu.VMEM((nm, MT, T), f32),
                         pltpu.SemaphoreType.DMA((nm,))],
     )
     return pl.pallas_call(
-        functools.partial(front_kernel, nx=nx, per=per, hrows=hrows, more=int(cin is not None)), grid_spec=gs,
-        out_shape=[jax.ShapeDtypeStruct((n, XW), bf16), jax.ShapeDtypeStruct((n, NB), bf16),
-                   jax.ShapeDtypeStruct((n, T), f32), jax.ShapeDtypeStruct((nx, T + 8, XW), f32)],
+        functools.partial(front_kernel, nx=nx, per=per, hrows=hrows, more=int(cin is not None), skip=len(into)), grid_spec=gs,
+        out_shape=[jax.ShapeDtypeStruct((parts * n, XW), bf16), jax.ShapeDtypeStruct((parts * n, NB), bf16),
+                   jax.ShapeDtypeStruct((parts * n, T), f32), jax.ShapeDtypeStruct((nx, T + SUB, XW), f32)],
+        input_output_aliases={n_in - len(into) + o: o for o in range(len(into))},
         compiler_params=pltpu.CompilerParams(dimension_semantics=("arbitrary",), vmem_limit_bytes=62 * MIB),
         cost_estimate=pl.CostEstimate(flops=n * 25_000_000, bytes_accessed=n * 10000, transcendentals=n * 4096),
         name="front",
-    )(pre, *xs, *halos, *[aux] * nx, w2, wb, wdt, *consts, *([] if cin is None else [cin]))
-
-
-def mixz_kernel(pre, *refs, nx):
-    xs_, auxs = refs[:nx], refs[nx:2 * nx]
-    (xa_ref, bg_ref, cg_ref, dc_ref, wz_ref, cin_ref, hp_ref, yn_ref, cout_ref, xv, av, zbuf, ybuf, xw, state) = refs[2 * nx:]
+    )(pre, *xs, *halos, *[aux] * nx, w2, wb, wdt, *consts, *([] if cin is None else [cin]), *into)
+
+
+def mixz_kernel(pre, *refs, ns, pers):
+    xs_, auxs = refs[:ns], refs[ns:2 * ns]
+    (xa_ref, bg_ref, cg_ref, dc_ref, wz_ref, cin_ref, hp_ref, yn_ref, cout_ref, xv, av, zbuf, ybuf, xw, state) = refs[2 * ns:]
     g, i, tile = pl.program_id(0), pl.program_id(1), pl.program_id(2)
     n_tiles = pl.num_programs(2)
 
@@ -235,8 +237,9 @@
     def _():
         state[...] = cin_ref[0]
 
-    for k in range(nx):
-        @pl.when(i == k)
+    src = (i * n_tiles + tile) // pers
+    for k in range(ns):
+        @pl.when(src == k)
         def _():
             xv[...] = xs_[k][...]
             av[...] = auxs[k][...]
@@ -294,30 +297,31 @@
         cout_ref[0] = state[...]
 
 
-def mixz_call(pre, aux, amaps, xs, arrs, w2, cin, hp, *, per, cofs):
-    nx = len(xs)
+def mixz_call(pre, aux, amaps, xs, arrs, w2, cin, hp, *, nx, per, ofs, cofs):
+    ns = len(xs)
+    pers = nx * per // ns
     n = nx * per * MT
     xa, bca, dc = arrs
-    piece = lambda k: (lambda g, i, t: jnp.clip((i - k) * per + t, 0, per - 1))
-    rows = lambda w, c: pl.BlockSpec((MT, w), lambda g, i, t, b: (i * per + t, c(g)))
+    piece = lambda k: (lambda i, t: jnp.clip(i * per + t - k * pers, 0, pers - 1))
+    rows = lambda w, c, o=ofs: pl.BlockSpec((MT, w), lambda g, i, t, b: (o + i * per + t, c(g)))
     state = lambda ofs: pl.BlockSpec((1, T, GW), lambda g, i, t, b: (ofs + i, 0, g))
     cols = lambda k: pl.BlockSpec((k, GW), lambda g, i, t, b: (0, g))
-    in_specs = [pl.BlockSpec((MT, D), lambda g, i, t, b, k=k: (piece(k)(g, i, t), 0)) for k in range(nx)]
-    in_specs += [pl.BlockSpec((MT, T), lambda g, i, t, b, k=k: (amaps[k](b) * per + piece(k)(g, i, t), 0)) for k in range(nx)]
+    in_specs = [pl.BlockSpec((MT, D), lambda g, i, t, b, k=k: (piece(k)(i, t), 0)) for k in range(ns)]
+    in_specs += [pl.BlockSpec((MT, T), lambda g, i, t, b, k=k: (amaps[k](b) * pers + piece(k)(i, t), 0)) for k in range(ns)]
     same = lambda g: g
     in_specs += [rows(GW, same), rows(T, same), rows(T, lambda g: 2 + g), rows(T, lambda g: 0), cols(D), state(cofs), cols(8)]
     gs = pltpu.PrefetchScalarGridSpec(
-        num_scalar_prefetch=1, grid=(2, nx, per), in_specs=in_specs, out_specs=[rows(GW, same), state(0)],
+        num_scalar_prefetch=1, grid=(2, nx, per), in_specs=in_specs, out_specs=[rows(GW, same, 0), state(0)],
         scratch_shapes=[pltpu.VMEM((MT, D), bf16), pltpu.VMEM((MT, T), f32), pltpu.VMEM((MT, GW), f32), pltpu.VMEM((T, GW), f32),
                         pltpu.VMEM((T, GW), bf16), pltpu.VMEM((T, GW), f32)],
     )
     return pl.pallas_call(
-        functools.partial(mixz_kernel, nx=nx), grid_spec=gs,
+        functools.partial(mixz_kernel, ns=ns, pers=pers), grid_spec=gs,
         out_shape=[jax.ShapeDtypeStruct((n, XW), bf16), jax.ShapeDtypeStruct((nx, T, XW), f32)],
         compiler_params=pltpu.CompilerParams(dimension_semantics=("arbitrary",) * 3, vmem_limit_bytes=60 * MIB),
         cost_estimate=pl.CostEstimate(flops=n * 20_000_000, bytes_accessed=n * 14000, transcendentals=n * 10000),
         name="mixz",
-    )(pre, *xs, *[aux] * nx, xa, bca, bca, dc, w2, cin, hp)
+    )(pre, *xs, *[aux] * ns, xa, bca, bca, dc, w2, cin, hp)
 
 
 def seq_slot(me, s):
@@ -435,7 +439,7 @@
 CW = 256
 
 
-def chain_kernel(n_blocks, e01_ref, e2_ref, e3_ref, out_ref, ebuf, sbuf, obuf, lsem, send_sem, recv_sem):
+def chain_kernel(n_blocks, e01_ref, e2_ref, e3_ref, out_hbm, ebuf, sbuf, obuf, out_ref, lsem, osem, send_sem, recv_sem):
     me, blk = lax.axis_index('tp'), lax.axis_index('sp')
     srcs = [e01_ref.at[0], e01_ref.at[1], e2_ref.at[0], e3_ref.at[0]]
     loads = [pltpu.make_async_copy(src, ebuf.at[seq_slot(me, s)], lsem.at[s]) for s, src in enumerate(srcs)]
@@ -471,6 +475,10 @@
 
     n = XW // CW
 
+    def store(j):
+        cs = pl.ds(j * CW, CW)
+        return pltpu.make_async_copy(out_ref.at[:, :, cs], out_hbm.at[:, :, cs], osem.at[j])
+
     def send(j):
         return pltpu.make_async_remote_copy(src_ref=obuf.at[j], dst_ref=sbuf.at[j], send_sem=send_sem.at[j],
                                             recv_sem=recv_sem.at[j], device_id=after, device_id_type=MESH)
@@ -492,23 +500,28 @@
         for q in range(4):
             v = through(q - 1, sbuf[j], cs) if q else sbuf[j]
             out_ref[seq_slot(me, q), :, cs] = v
+        store(j).start()
 
     @pl.when(blk < n_blocks - 1)
     def _():
         for j in range(n):
             send(j).wait_send()
 
+    for j in range(n):
+        store(j).wait()
+
 
 def chain_call(e01, e2, e3, n_blocks):
-    hbm = pl.BlockSpec(memory_space=pl.ANY)
+    hbm = pl.BlockSpec(memory_space=pltpu.HBM)
     n = XW // CW
     return pl.pallas_call(
         functools.partial(chain_kernel, n_blocks),
         in_specs=[hbm] * 3,
-        out_specs=pl.BlockSpec(memory_space=pltpu.VMEM),
+        out_specs=hbm,
         out_shape=jax.ShapeDtypeStruct((4, T, XW), f32),
         scratch_shapes=[pltpu.VMEM((4, T + SUB, XW), f32), pltpu.VMEM((n, T, CW), f32), pltpu.VMEM((n, T, CW), f32),
-                        pltpu.SemaphoreType.DMA((4,)), pltpu.SemaphoreType.DMA((n,)), pltpu.SemaphoreType.DMA((n,))],
+                        pltpu.VMEM((4, T, XW), f32),                         pltpu.SemaphoreType.DMA((4,)), pltpu.SemaphoreType.DMA((n,)),
+                        pltpu.SemaphoreType.DMA((n,)), pltpu.SemaphoreType.DMA((n,))],
         compiler_params=pltpu.CompilerParams(collective_id=1, has_side_effects=True, vmem_limit_bytes=40 * MIB),
         name="chain",
     )(e01, e2, e3)
@@ -528,14 +541,14 @@
     refs[-1][...] = acc.astype(refs[-1].dtype)
 
 
-def out_call(run, part, y, yr, w, wr, x=None, other=None, into=None):
-    rows = yr.shape[0]
+def out_call(run, part, y, yr, rpart, w, wr, x=None, other=None, into=None):
+    rows = TOK // NCH
     h = XW // 2
     at = lambda r: (lambda j: (r, j))
     cols = at(0)
     ins = [y, yr, w, *wr]
     specs = [pl.BlockSpec((rows, XW), lambda j: (run * (TOK // rows) + part, 0), pipeline_mode=ONE),
-             pl.BlockSpec((rows, XW), lambda j: (0, 0), pipeline_mode=ONE),
+             pl.BlockSpec((rows, XW), lambda j: (rpart, 0), pipeline_mode=ONE),
              pl.BlockSpec((XW, NT), cols), pl.BlockSpec((h, NT), cols), pl.BlockSpec((h, NT), cols)]
     alias = {}
     if x is not None:
@@ -613,12 +626,12 @@
         weights = (w2, wb, w_dt)
         consts = (cw, cwb, hp1)
 
-        def front(slots, part, xs, halos, hrows, carry, per):
-            return front_call(pre, aux, [lambda b, s=s: b[s] * (rows // (per * MT)) + part for s in slots], xs, halos, hrows,
-                              weights, carry, consts, per=per)
+        def front(slots, part, parts, xs, halos, hrows, carry, into, per):
+            return front_call(pre, aux, [lambda b, s=s: b[s] * parts + part for s in slots], xs, halos, hrows,
+                              weights, carry, consts, into, part, parts, per=per)
 
         tail_row = lambda s: (lambda b: b[s] * HALO)
-        *own, ends = front((0, 1), 0, [x_loc, x_par], [tails] * 2, [tail_row(0), tail_row(1)], None, per)
+        *own, ends = front((0, 1), 0, 1, [x_loc, x_par], [tails] * 2, [tail_row(0), tail_row(1)], None, [], per)
         w_rem = [w_gather(0, ends)]
         x_dir[0] = after(x_dir[0], ends)
         rem, carry, x_fwd = [[], []], [None, None], []
@@ -627,34 +640,33 @@
             x_fwd.append(send(x_dir[k], CORE_SWAP))
             for r, xs in ((0, x_dir), (1, x_fwd)):
                 halo = (tails, tail_row(2 + r)) if k == 0 else (xs[k - 1], lambda b: ch - HALO)
-                *arrs, carry[r] = front((2 + r,), k, [after(xs[k], last)], [halo[0]], [halo[1]], carry[r], kper)
+                *rem[r], carry[r] = front((2 + r,), k, NCH, [after(xs[k], last)], [halo[0]], [halo[1]], carry[r], rem[r], kper)
                 last = carry[r]
-                rem[r].append(arrs)
             if k + 1 < NCH:
                 x_dir[k + 1] = after(x_dir[k + 1], carry[1])
         starts = chain_call(ends, carry[0], carry[1], n_blocks)
         w_rem.append(w_gather(1, starts))
 
-        def mix(slots, part, xs, arrs, start, cofs, per):
-            return mixz_call(pre, aux, [lambda b, s=s: b[s] * (rows // (per * MT)) + part for s in slots], xs, arrs, w2, start, hp2,
-                             per=per, cofs=cofs)
-
+        def mix(amaps, xs, arrs, start, **kw):
+            return mixz_call(pre, aux, amaps, xs, arrs, w2, start, hp2, **kw)
+
+        part_of = lambda s, k: (lambda b: b[s] * NCH + k)
         y_in = [[], []]
-        last = starts
-        for r, xs in ((1, x_fwd), (0, x_dir)):
-            c, cofs = after(starts, last), 2 + r
-            for k in range(NCH):
-                yn, c = mix((2 + r,), k, [xs[k]], rem[r][k], c, cofs, kper)
-                last, cofs = c, 0
-                y_in[r].append(send(yn, CHIP_SWAP))
-        y_own, _ = mix((0, 1), 0, [x_loc, x_par], own, after(starts, last), 0, per)
+        c, cofs = starts, 3
+        for k in range(NCH):
+            yn, c = mix([part_of(3, k)], [x_fwd[k]], rem[1], c, nx=1, per=kper, ofs=k * kper, cofs=cofs)
+            cofs = 0
+            y_in[1].append(send(yn, CHIP_SWAP))
+        yn, c = mix([part_of(2, k) for k in range(NCH)], x_dir, rem[0], after(starts, c), nx=1, per=per, ofs=0, cofs=2)
+        y_in[0] = send(yn, CHIP_SWAP)
+        y_own, _ = mix([lambda b: b[0], lambda b: b[1]], [x_loc, x_par], own, after(starts, c), nx=2, per=per, ofs=0, cofs=0)
         other = []
         for k in range(NCH):
-            part = out_call(1, k, y_own, y_in[1][k], w_out, w_rem)
+            part = out_call(1, k, y_own, y_in[1][k], 0, w_out, w_rem)
             other.append(send(part, CORE_SWAP))
         y = None
         for k in range(NCH):
-            y = out_call(0, k, y_own, y_in[0][k], w_out, w_rem, x_loc, other[k], y)
+            y = out_call(0, k, y_own, y_in[0], k, w_out, w_rem, x_loc, other[k], y)
         return y
 
     return jax.shard_map(body, mesh=mesh, in_specs=(token_spec, seg_spec) + weight_specs, out_specs=token_spec, check_vma=False)

time: 695 us -> 739 us (1.063)
  waiting for transfers between devices: 98 us -> 147 us
    ppermute x13 -> x12, waiting for transfers between devices: 98 us -> 147 us  [send(): return lax.ppermute(v, 'tp', perm)]
    pallas_call x5 -> x4, Pallas kernels: 154 us -> 151 us  [mixz_call(): pl.pallas_call(functools.partial(mixz_kernel, ns=ns, pers=pers), grid_spe...]
    unnamed x43 -> x41, local copies, waits for them, and re-layouts: 42.1 us -> 41.4 us
  transfers between devices with their start and end apart: 15 -> 14, of which waited for: 4 -> 3; matrix products, arithmetic and copies ran while one was open for 6% -> 5% of each run, Pallas kernels for 69% -> 65%
where the time goes in v3:
time: 739 us; the launch traced here: 731 us
  Pallas kernels  509 us (69%)
  waiting for transfers between devices  147 us (20%)
  local copies, waits for them, and re-layouts  42.6 us (6%)
  between operations  13.9 us (2%)
  other arithmetic  9.42 us (1%)
  starting transfers between devices  9.32 us (1%)
    pallas_call x5, Pallas kernels, front_call(): pl.pallas_call(functools.partial(front_kernel, nx=nx, per=per, hrows=hrow...  209 us
    pallas_call x4, Pallas kernels, mixz_call(): pl.pallas_call(functools.partial(mixz_kernel, ns=ns, pers=pers), grid_spe...  151 us
    ppermute x12, waiting for transfers between devices, send(): return lax.ppermute(v, 'tp', perm)  147 us
    pallas_call x4, Pallas kernels, out_call(): pl.pallas_call(out_kernel, grid=(D // NT,), in_specs=specs, out_specs=pl....  100 us
    unnamed x41, local copies, waits for them, and re-layouts  41.4 us
    pallas_call x1, Pallas kernels, chain_call(): pl.pallas_call(functools.partial(chain_kernel, n_blocks), in_specs=[hbm]...  37.3 us
  transfers between devices with their start and end apart: 14, of which 3 were waited for; matrix products, arithmetic and copies ran while one was open for 5% of the time, Pallas kernels for 65%

profile of v3, /device:TPU:30, one launch (start us, length us, event | category | flops | bytes accessed | tf_op | source)
XLA Modules:
  0.0 731.3 jit_solution(1404142886110852762)
XLA Ops:
  7.2 10.9 %ahead.1 = (s32[5,8,128]{2,1,0:T(8,128)S(1)}, bf16[5,16,4096]{2,1,0:T(8,128)(2,1)S(1)}, bf16[512,4096]{1,0:T(8,128)(2,1)}, bf16[512,4096]{1,0:T(8,128)(2,1)S(1)}...) custom-call(s32[8,128]{1,0:T(8,128)S(1)} %bitcast.37, bf16[1024,4096]{1,0:T(8,128)(2,1)} %refs_0_.7, ...), custom_call_target="tpu_custom_call" | custom-call | tf_op jit(solution)/shard_map/ahead/pallas_call | solution.py:426
  21.0 2.3 collective-permute-start.2
  24.4 23.2 %copy.27 = bf16[512,8,2,2048]{3,1,2,0:T(8,128)(2,1)} copy(bf16[512,8,2,2048]{3,2,1,0:T(2,128)(2,1)} %bitcast.56) | data formatting | bytes 67108864
  47.7 5.1 copy.28
  57.6 5.3 select_select_fusion.refs_4_.refs_5_.refs_2_.refs_3_.refs_1_
  62.9 91.7 %front.5 = (bf16[2048,2048]{1,0:T(8,128)(2,1)}, bf16[2048,512]{1,0:T(8,128)(2,1)}, f32[2048,128]{1,0:T(8,128)}, f32[2,136,2048]{2,1,0:T(8,128)}) custom-call(s32[4]{0:T(128)} %pad_add_fusion.1.pre, bf16[1024,4096]{1,0:T(8,128)(2,1)} %refs_0_.7, bf16[1024,4096]{1,0:T(8,128)(2,1)} %collective-permute-done.refs_1_, bf16[80,4096]{1,0:T(8,128)(2,1)} %bitcast.38, ...), custom_call_target="tpu_custom_call" | custom-call | flops 51200000000 | bytes 20480000 | tf_op jit(solution)/shard_map/front/pallas_call | solution.py:219
  154.9 2.1 collective-permute-start.1
  157.0 29.1 %front.6 = (bf16[1024,2048]{1,0:T(8,128)(2,1)}, bf16[1024,512]{1,0:T(8,128)(2,1)}, f32[1024,128]{1,0:T(8,128)}, f32[1,136,2048]{2,1,0:T(8,128)}) custom-call(s32[4]{0:T(128)} %pad_add_fusion.1.pre, bf16[512,4096]{1,0:T(8,128)(2,1)} %collective-permute-done.2.refs_0_.refs_1_, bf16[80,4096]{1,0:T(8,128)(2,1)} %bitcast.40, ...), custom_call_target="tpu_custom_call" | custom-call | flops 12800000000 | bytes 5120000 | tf_op jit(solution)/shard_map/front/pallas_call | solution.py:219
  186.1 29.3 %front.7 = (bf16[1024,2048]{1,0:T(8,128)(2,1)}, bf16[1024,512]{1,0:T(8,128)(2,1)}, f32[1024,128]{1,0:T(8,128)}, f32[1,136,2048]{2,1,0:T(8,128)}) custom-call(s32[4]{0:T(128)} %pad_add_fusion.1.pre, bf16[512,4096]{1,0:T(8,128)(2,1)} %collective-permute-done.3.refs_0_.refs_1_, bf16[80,4096]{1,0:T(8,128)(2,1)} %bitcast.41, ...), custom_call_target="tpu_custom_call" | custom-call | flops 12800000000 | bytes 5120000 | tf_op jit(solution)/shard_map/front/pallas_call | solution.py:219
  215.4 33.1 %collective-permute-done.1.refs_0_.refs_1_ = bf16[512,4096]{1,0:T(8,128)(2,1)} collective-permute-done((bf16[512,4096]{1,0:T(8,128)(2,1)}, bf16[512,4096]{1,0:T(8,128)(2,1)}, u32[]{:S(2)}, u32[]{:S(2)}) %collective-permute-start.1) | collective-permute-done | bytes 4194336 | tf_op jit(solution)/shard_map/ppermute | solution.py:574
  250.2 29.8 %front.8 = (bf16[1024,2048]{1,0:T(8,128)(2,1)}, bf16[1024,512]{1,0:T(8,128)(2,1)}, f32[1024,128]{1,0:T(8,128)}, f32[1,136,2048]{2,1,0:T(8,128)}) custom-call(s32[4]{0:T(128)} %pad_add_fusion.1.pre, bf16[512,4096]{1,0:T(8,128)(2,1)} %collective-permute-done.1.refs_0_.refs_1_, ...), custom_call_target="tpu_custom_call", output_to_operand_aliasing={{0}: (11, {}), {1}: (12, {}), {2}: (13, {})} | custom-call | flops 12800000000 | bytes 5120000 | tf_op jit(solution)/shard_map/front/pallas_call | solution.py:219
  280.1 29.5 %front.9 = (bf16[1024,2048]{1,0:T(8,128)(2,1)}, bf16[1024,512]{1,0:T(8,128)(2,1)}, f32[1024,128]{1,0:T(8,128)}, f32[1,136,2048]{2,1,0:T(8,128)}) custom-call(s32[4]{0:T(128)} %pad_add_fusion.1.pre, bf16[512,4096]{1,0:T(8,128)(2,1)} %collective-permute-done.4.refs_0_, ...), custom_call_target="tpu_custom_call", output_to_operand_aliasing={{0}: (11, {}), {1}: (12, {}), {2}: (13, {})} | custom-call | flops 12800000000 | bytes 5120000 | tf_op jit(solution)/shard_map/front/pallas_call | solution.py:219
  312.5 37.3 %chain.1.refs_9_.refs_7_ = f32[4,128,2048]{2,1,0:T(8,128)S(1)} custom-call(f32[2,136,2048]{2,1,0:T(8,128)S(1)} %copy-done.1, f32[1,136,2048]{2,1,0:T(8,128)S(1)} %copy-done.2, f32[1,136,2048]{2,1,0:T(8,128)S(1)} %copy-done.3), custom_call_target="tpu_custom_call" | custom-call | tf_op jit(solution)/shard_map/chain/pallas_call | solution.py:517
  349.8 2.1 copy-done
  352.8 22.4 %mixz.6 = (bf16[512,2048]{1,0:T(8,128)(2,1)}, f32[1,128,2048]{2,1,0:T(8,128)}) custom-call(s32[4]{0:T(128)} %pad_add_fusion.1.pre, bf16[512,4096]{1,0:T(8,128)(2,1)} %collective-permute-done.3.refs_0_.refs_1_, f32[4096,128]{1,0:T(8,128)} %select_select_fusion.refs_4_.refs_5_.refs_2_.refs_3_.refs_1_, bf16[1024,2048]{1,0:T(8,128)(2,1)} %get-tuple-element.79.refs_2_, ...), custom_call_target="tpu_custom_call" | custom-call | flops 10240000000 | bytes 7168000 | tf_op jit(solution)/shard_map/mixz/pallas_call | solution.py:318
  375.2 22.1 %mixz.7 = (bf16[512,2048]{1,0:T(8,128)(2,1)}, f32[1,128,2048]{2,1,0:T(8,128)}) custom-call(s32[4]{0:T(128)} %pad_add_fusion.1.pre, bf16[512,4096]{1,0:T(8,128)(2,1)} %collective-permute-done.4.refs_0_, f32[4096,128]{1,0:T(8,128)} %select_select_fusion.refs_4_.refs_5_.refs_2_.refs_3_.refs_1_, bf16[1024,2048]{1,0:T(8,128)(2,1)} %get-tuple-element.79.refs_2_, ...), custom_call_target="tpu_custom_call" | custom-call | flops 10240000000 | bytes 7168000 | tf_op jit(solution)/shard_map/mixz/pallas_call | solution.py:318
  399.3 68.4 %mixz.4 = (bf16[2048,2048]{1,0:T(8,128)(2,1)}, f32[2,128,2048]{2,1,0:T(8,128)}) custom-call(s32[4]{0:T(128)} %pad_add_fusion.1.pre, bf16[1024,4096]{1,0:T(8,128)(2,1)} %refs_0_.7, bf16[1024,4096]{1,0:T(8,128)(2,1)} %collective-permute-done.refs_1_, f32[4096,128]{1,0:T(8,128)} %select_select_fusion.refs_4_.refs_5_.refs_2_.refs_3_.refs_1_, ...), custom_call_target="tpu_custom_call" | custom-call | flops 40960000000 | bytes 28672000 | tf_op jit(solution)/shard_map/mixz/pallas_call | solution.py:318
  467.8 21.8 %collective-permute-done.10.yr_ref = bf16[512,2048]{1,0:T(8,128)(2,1)} collective-permute-done((bf16[512,2048]{1,0:T(8,128)(2,1)}, bf16[512,2048]{1,0:T(8,128)(2,1)}, u32[]{:S(2)}, u32[]{:S(2)}) %collective-permute-start.10) | collective-permute-done | bytes 2097184 | tf_op jit(solution)/shard_map/ppermute | solution.py:574
  489.6 24.4 %out_proj.5 = f32[512,4096]{1,0:T(8,128)} custom-call(bf16[2048,2048]{1,0:T(8,128)(2,1)} %get-tuple-element.70.y_ref, bf16[512,2048]{1,0:T(8,128)(2,1)} %collective-permute-done.10.yr_ref, bf16[2048,4096]{1,0:T(8,128)(2,1)} %w_ref.7, bf16[1024,4096]{1,0:T(8,128)(2,1)} %all-gather.3.cloned.1.call-done.wr0_ref, ...), custom_call_target="tpu_custom_call" | custom-call | flops 16896000000 | bytes 51200000 | tf_op jit(solution)/shard_map/out_proj/pallas_call | solution.py:561
  515.3 24.4 %out_proj.4 = f32[512,4096]{1,0:T(8,128)} custom-call(bf16[2048,2048]{1,0:T(8,128)(2,1)} %get-tuple-element.70.y_ref, bf16[512,2048]{1,0:T(8,128)(2,1)} %copy-done.17, bf16[2048,4096]{1,0:T(8,128)(2,1)} %w_ref.7, bf16[1024,4096]{1,0:T(8,128)(2,1)} %all-gather.3.cloned.1.call-done.wr0_ref, bf16[1024,4096]{1,0:T(8,128)(2,1)} %all-gather.5.cloned.1.call-done.wr1_ref), custom_call_target="tpu_custom_call" | custom-call | flops 16896000000 | bytes 51200000 | tf_op jit(solution)/shard_map/out_proj/pallas_call | solution.py:561
  540.2 37.8 %mixz.5 = (bf16[1024,2048]{1,0:T(8,128)(2,1)}, f32[1,128,2048]{2,1,0:T(8,128)}) custom-call(s32[4]{0:T(128)} %pad_add_fusion.1.pre, bf16[512,4096]{1,0:T(8,128)(2,1)} %collective-permute-done.2.refs_0_.refs_1_, bf16[512,4096]{1,0:T(8,128)(2,1)} %collective-permute-done.1.refs_0_.refs_1_, ...), custom_call_target="tpu_custom_call" | custom-call | flops 20480000000 | bytes 14336000 | tf_op jit(solution)/shard_map/mixz/pallas_call | solution.py:318
  578.4 92.4 %collective-permute-done.5.yr_ref = bf16[1024,2048]{1,0:T(8,128)(2,1)S(1)} collective-permute-done((bf16[1024,2048]{1,0:T(8,128)(2,1)}, bf16[1024,2048]{1,0:T(8,128)(2,1)S(1)}, u32[]{:S(2)}, u32[]{:S(2)}) %collective-permute-start.5) | collective-permute-done | bytes 4194336 | tf_op jit(solution)/shard_map/ppermute | solution.py:574
  672.7 25.8 %out_proj.6.refs_2_ = bf16[1024,4096]{1,0:T(8,128)(2,1)} custom-call(bf16[2048,2048]{1,0:T(8,128)(2,1)} %get-tuple-element.70.y_ref, bf16[1024,2048]{1,0:T(8,128)(2,1)} %copy-done.7, bf16[2048,4096]{1,0:T(8,128)(2,1)} %w_ref.7, bf16[1024,4096]{1,0:T(8,128)(2,1)} %all-gather.3.cloned.1.call-done.wr0_ref, ...), custom_call_target="tpu_custom_call" | custom-call | flops 16896000000 | bytes 51200000 | tf_op jit(solution)/shard_map/out_proj/pallas_call | solution.py:561
  698.5 25.8 %out_proj.7 = bf16[1024,4096]{1,0:T(8,128)(2,1)} custom-call(bf16[2048,2048]{1,0:T(8,128)(2,1)} %get-tuple-element.70.y_ref, bf16[1024,2048]{1,0:T(8,128)(2,1)} %copy-done.7, bf16[2048,4096]{1,0:T(8,128)(2,1)} %w_ref.7, bf16[1024,4096]{1,0:T(8,128)(2,1)} %all-gather.3.cloned.1.call-done.wr0_ref, ...), custom_call_target="tpu_custom_call", output_to_operand_aliasing={{}: (7, {})} | custom-call | flops 16896000000 | bytes 51200000 | tf_op jit(solution)/shard_map/out_proj/pallas_call | solution.py:561
  (85 shorter events, 21.4 us)
Async XLA Ops:
  6.5 483.1 %all-gather.3.cloned.1.call-start = ((), (), s32[]{:S(2)}) async-start(), calls=%async_computation | async-start | bytes 9437184 | tf_op jit(solution)/shard_map/all_gather | solution.py:615
  21.0 41.9 %collective-permute-start = (bf16[1024,4096]{1,0:T(8,128)(2,1)}, bf16[1024,4096]{1,0:T(8,128)(2,1)}, u32[]{:S(2)}, u32[]{:S(2)}) collective-permute-start(bf16[1024,4096]{1,0:T(8,128)(2,1)} %refs_0_.7), channel_id=1, source_target_pairs={{0,1},{1,0},{2,3},{3,2},{4,5},{5,4},{6,7},{7,6},{8,9},{9,8},{10,11... | collective-permute-start | bytes 25165832 | tf_op jit(solution)/shard_map/ppermute | solution.py:574
  21.0 133.8 %collective-permute-start.2 = (bf16[512,4096]{1,0:T(8,128)(2,1)}, bf16[512,4096]{1,0:T(8,128)(2,1)}, u32[]{:S(2)}, u32[]{:S(2)}) collective-permute-start(bf16[512,4096]{1,0:T(8,128)(2,1)} %get-tuple-element.53), channel_id=1, source_target_pairs={{0,2},{1,3},{2,0},{3,1},{4,6},{5,7},{6,4},{7,5},{8,10},{9,11},{10,... | collective-permute-start | bytes 12582920 | tf_op jit(solution)/shard_map/ppermute | solution.py:574
  23.3 131.3 %collective-permute-start.6 = (bf16[128,4096]{1,0:T(8,128)(2,1)S(1)}, bf16[128,4096]{1,0:T(8,128)(2,1)}, u32[]{:S(2)}, u32[]{:S(2)}) collective-permute-start(bf16[128,4096]{1,0:T(8,128)(2,1)S(1)} %get-tuple-element.75), channel_id=1, source_target_pairs={{0,2},{1,3},{2,0},{3,1},{4,6},{5,7},{6,4},{7,5},{8,10},{9,11},{10,... | collective-permute-start | bytes 3145736 | tf_op jit(solution)/shard_map/ppermute | solution.py:574
  47.6 5.2 copy-start.8
  47.6 6.5 copy-start.10
  47.6 6.5 copy-start.13
  47.6 6.5 copy-start.12
  47.6 7.2 copy-start.14
  47.6 7.2 copy-start.15
  47.6 9.3 %copy-start.9 = (bf16[4,2048]{1,0:T(4,128)(2,1)S(1)}, bf16[4,2048]{1,0:T(4,128)(2,1)}, u32[]{:S(2)}) copy-start(bf16[4,2048]{1,0:T(4,128)(2,1)} %param.19) | copy-start | bytes 49156
  154.6 335.0 %all-gather.5.cloned.1.call-start = ((), (), s32[]{:S(2)}) async-start(), calls=%async_computation.1 | async-start | bytes 9437184 | tf_op jit(solution)/shard_map/all_gather | solution.py:615
  154.8 31.2 %collective-permute-start.3 = (bf16[512,4096]{1,0:T(8,128)(2,1)}, bf16[512,4096]{1,0:T(8,128)(2,1)}, u32[]{:S(2)}, u32[]{:S(2)}) collective-permute-start(bf16[512,4096]{1,0:T(8,128)(2,1)} %collective-permute-done.2.refs_0_.refs_1_), channel_id=1, source_target_pairs={{0,1},{1,0},{2,3},{3,2},{4,5},{5,4},{6,7},{7,6},{8,9},{9,8},{10,11... | collective-permute-start | bytes 12582920 | tf_op jit(solution)/shard_map/ppermute | solution.py:574
  154.9 93.5 %collective-permute-start.1 = (bf16[512,4096]{1,0:T(8,128)(2,1)}, bf16[512,4096]{1,0:T(8,128)(2,1)}, u32[]{:S(2)}, u32[]{:S(2)}) collective-permute-start(bf16[512,4096]{1,0:T(8,128)(2,1)} %copy-done.5), channel_id=1, source_target_pairs={{0,2},{1,3},{2,0},{3,1},{4,6},{5,7},{6,4},{7,5},{8,10},{9,11},{10,... | collective-permute-start | bytes 12582920 | tf_op jit(solution)/shard_map/ppermute | solution.py:574
  248.5 31.6 %collective-permute-start.4 = (bf16[512,4096]{1,0:T(8,128)(2,1)}, bf16[512,4096]{1,0:T(8,128)(2,1)}, u32[]{:S(2)}, u32[]{:S(2)}) collective-permute-start(bf16[512,4096]{1,0:T(8,128)(2,1)} %collective-permute-done.1.refs_0_.refs_1_), channel_id=1, source_target_pairs={{0,1},{1,0},{2,3},{3,2},{4,5},{5,4},{6,7},{7,6},{8,9},{9,8},{10,11... | collective-permute-start | bytes 12582920 | tf_op jit(solution)/shard_map/ppermute | solution.py:574
  248.5 103.4 %collective-permute-start.7 = (bf16[128,4096]{1,0:T(8,128)(2,1)}, bf16[128,4096]{1,0:T(8,128)(2,1)}, u32[]{:S(2)}, u32[]{:S(2)}) collective-permute-start(bf16[128,4096]{1,0:T(8,128)(2,1)} %get-tuple-element.77), channel_id=1, source_target_pairs={{0,2},{1,3},{2,0},{3,1},{4,6},{5,7},{6,4},{7,5},{8,10},{9,11},{10,... | collective-permute-start | bytes 3145736 | tf_op jit(solution)/shard_map/ppermute | solution.py:574
  280.1 29.5 %copy-start.2 = (f32[1,136,2048]{2,1,0:T(8,128)S(1)}, f32[1,136,2048]{2,1,0:T(8,128)}, u32[]{:S(2)}) copy-start(f32[1,136,2048]{2,1,0:T(8,128)} %get-tuple-element.64.e2_ref) | copy-start | bytes 3342340
  312.5 39.4 %copy-start.11 = (bf16[2048]{0:T(1024)(128)(2,1)S(1)}, bf16[2048]{0:T(1024)(128)(2,1)}, u32[]{:S(2)}) copy-start(bf16[2048]{0:T(1024)(128)(2,1)} %param.26) | copy-start | bytes 12292
  312.5 39.4 %copy-start.16 = (f32[32]{0:T(128)S(1)}, f32[32]{0:T(128)}, u32[]{:S(2)}) copy-start(f32[32]{0:T(128)} %param.25) | copy-start | bytes 388
  397.3 116.7 %collective-permute-start.8 = (bf16[512,2048]{1,0:T(8,128)(2,1)}, bf16[512,2048]{1,0:T(8,128)(2,1)S(1)}, u32[]{:S(2)}, u32[]{:S(2)}) collective-permute-start(bf16[512,2048]{1,0:T(8,128)(2,1)} %get-tuple-element.83), channel_id=1, source_target_pairs={{0,2},{1,3},{2,0},{3,1},{4,6},{5,7},{6,4},{7,5},{8,10},{9,11},{10,... | collective-permute-start | bytes 6291464 | tf_op jit(solution)/shard_map/ppermute | solution.py:574
  397.7 91.9 %collective-permute-start.10 = (bf16[512,2048]{1,0:T(8,128)(2,1)}, bf16[512,2048]{1,0:T(8,128)(2,1)}, u32[]{:S(2)}, u32[]{:S(2)}) collective-permute-start(bf16[512,2048]{1,0:T(8,128)(2,1)} %get-tuple-element.84), channel_id=1, source_target_pairs={{0,2},{1,3},{2,0},{3,1},{4,6},{5,7},{6,4},{7,5},{8,10},{9,11},{10,... | collective-permute-start | bytes 6291464 | tf_op jit(solution)/shard_map/ppermute | solution.py:574
  514.0 156.8 %collective-permute-start.11 = (f32[512,4096]{1,0:T(8,128)}, f32[512,4096]{1,0:T(8,128)}, u32[]{:S(2)}, u32[]{:S(2)}) collective-permute-start(f32[512,4096]{1,0:T(8,128)} %out_proj.5), channel_id=1, source_target_pairs={{0,1},{1,0},{2,3},{3,2},{4,5},{5,4},{6,7},{7,6},{8,9},{9,8},{10,11... | collective-permute-start | bytes 25165832 | tf_op jit(solution)/shard_map/ppermute | solution.py:574
  539.7 158.8 %collective-permute-start.9 = (f32[512,4096]{1,0:T(8,128)}, f32[512,4096]{1,0:T(8,128)}, u32[]{:S(2)}, u32[]{:S(2)}) collective-permute-start(f32[512,4096]{1,0:T(8,128)} %out_proj.4), channel_id=1, source_target_pairs={{0,1},{1,0},{2,3},{3,2},{4,5},{5,4},{6,7},{7,6},{8,9},{9,8},{10,11... | collective-permute-start | bytes 25165832 | tf_op jit(solution)/shard_map/ppermute | solution.py:574
  578.0 92.8 %collective-permute-start.5 = (bf16[1024,2048]{1,0:T(8,128)(2,1)}, bf16[1024,2048]{1,0:T(8,128)(2,1)S(1)}, u32[]{:S(2)}, u32[]{:S(2)}) collective-permute-start(bf16[1024,2048]{1,0:T(8,128)(2,1)} %get-tuple-element.74), channel_id=1, source_target_pairs={{0,2},{1,3},{2,0},{3,1},{4,6},{5,7},{6,4},{7,5},{8,10},{9,11},{10,... | collective-permute-start | bytes 12582920 | tf_op jit(solution)/shard_map/ppermute | solution.py:574
  (8 other events, 11.8 us)
Sparse Core Ops, SparseCore 0:
  154.7 123.0 all-gather.2
  352.0 122.5 all-gather.4

commit v4 on v3

--- a/solution.py
+++ b/solution.py
@@ -52,10 +52,10 @@
     return pl.ds(start if isinstance(start, int) else pl.multiple_of(start, 16), size)
 
 
-def front_kernel(pre, *refs, nx, per, hrows, more, skip):
-    xs_, hs_, auxs = refs[:nx], refs[nx:2 * nx], refs[2 * nx:3 * nx]
-    wx_ref, wb_ref, wdt_ref, cw_ref, cwb_ref, hp_ref, *cins = refs[3 * nx:][:6 + more]
-    (xa_ref, bca_ref, dc_ref, cout_ref, xbuf, pbuf, bbuf, xw, bt, cum_all, wgt, abuf, sem) = refs[3 * nx + 6 + more + skip:]
+def front_kernel(pre, *refs, nx, per, where, ns, more, skip):
+    srcs, auxs = refs[:ns], refs[ns:ns + nx]
+    wx_ref, wb_ref, wdt_ref, cw_ref, cwb_ref, hp_ref, *cins = refs[ns + nx:][:6 + more]
+    (xa_ref, bca_ref, dc_ref, cout_ref, xbuf, pbuf, bbuf, xw, bt, cum_all, wgt, abuf, sem) = refs[ns + nx + 6 + more + skip:]
     n = pl.program_id(0)
     last_n = XW // XT
     nm = nx * per
@@ -64,11 +64,12 @@
     tiles = [slice(t * T, (t + 1) * T) for t in range(MT // T)]
 
     def copies(m):
-        i, s = divmod(m, per)
-        if s:
-            return [pltpu.make_async_copy(xs_[i].at[rows_from(s * MT - HALO, MH)], xbuf.at[m], sem.at[m])]
-        return [pltpu.make_async_copy(hs_[i].at[rows_from(hrows[i](pre), HALO)], xbuf.at[m, pl.ds(0, HALO)], sem.at[m]),
-                pltpu.make_async_copy(xs_[i].at[pl.ds(0, MT)], xbuf.at[m, pl.ds(HALO, MT)], sem.at[m])]
+        src, row, halo, h = where[m]
+        h = h(pre) if callable(h) else h
+        if halo == src:
+            return [pltpu.make_async_copy(srcs[src].at[rows_from(row - HALO, MH)], xbuf.at[m], sem.at[m])]
+        return [pltpu.make_async_copy(srcs[halo].at[rows_from(h, HALO)], xbuf.at[m, pl.ds(0, HALO)], sem.at[m]),
+                pltpu.make_async_copy(srcs[src].at[pl.ds(row, MT)], xbuf.at[m, pl.ds(HALO, MT)], sem.at[m])]
 
     def left(i):
         return slice(nm * MT + SUB * (i + 1), nm * MT + SUB * (i + 2))
@@ -193,8 +194,18 @@
         end_state()
 
 
-def front_call(pre, aux, amaps, xs, halos, hrows, weights, cin, consts, into, part, parts, *, per):
-    nx = len(xs)
+def front_call(pre, aux, amaps, runs, weights, cin, consts, into, part, parts, *, per):
+    nx = len(runs)
+    srcs, where = [], []
+    for ahead, row, arrays in runs:
+        srcs.append(ahead)
+        halo = len(srcs) - 1
+        for arr in arrays:
+            srcs.append(arr)
+            for r in range(0, min(arr.shape[0], per * MT), MT):
+                where.append((len(srcs) - 1, r, halo, row))
+                halo, row = len(srcs) - 1, r + MT - HALO
+    ns = len(srcs)
     nm = nx * per
     n = nm * MT
     nt = XW // XT
@@ -204,7 +215,7 @@
     whole = lambda *shape, mode=ONE, r=0: pl.BlockSpec(shape, lambda j, b: (r, 0), pipeline_mode=mode)
     cols = lambda k, r=0: pl.BlockSpec((k, XT), lambda j, b: (r, prev(j)))
     state = pl.BlockSpec((nx, T + 8, XT), lambda j, b: (0, 0, prev(j)))
-    in_specs = [hbm] * (2 * nx) + [pl.BlockSpec((per * MT, T), lambda j, b, f=f: (f(b), 0), pipeline_mode=ONE) for f in amaps] + [
+    in_specs = [hbm] * ns + [pl.BlockSpec((per * MT, T), lambda j, b, f=f: (f(b), 0), pipeline_mode=ONE) for f in amaps] + [
         pl.BlockSpec((D, XT), lambda j, b: (0, nt + jnp.minimum(j, nt - 1))), whole(D, NB), whole(D, HEADS),
         cols(SUB), whole(SUB, NB), whole(SUB, T)] + ([] if cin is None else [state]) + [hbm] * len(into)
     n_in = len(in_specs) + 1
@@ -217,17 +228,17 @@
                         pltpu.SemaphoreType.DMA((nm,))],
     )
     return pl.pallas_call(
-        functools.partial(front_kernel, nx=nx, per=per, hrows=hrows, more=int(cin is not None), skip=len(into)), grid_spec=gs,
+        functools.partial(front_kernel, nx=nx, per=per, where=where, ns=ns, more=int(cin is not None), skip=len(into)), grid_spec=gs,
         out_shape=[jax.ShapeDtypeStruct((parts * n, XW), bf16), jax.ShapeDtypeStruct((parts * n, NB), bf16),
                    jax.ShapeDtypeStruct((parts * n, T), f32), jax.ShapeDtypeStruct((nx, T + SUB, XW), f32)],
         input_output_aliases={n_in - len(into) + o: o for o in range(len(into))},
         compiler_params=pltpu.CompilerParams(dimension_semantics=("arbitrary",), vmem_limit_bytes=62 * MIB),
         cost_estimate=pl.CostEstimate(flops=n * 25_000_000, bytes_accessed=n * 10000, transcendentals=n * 4096),
         name="front",
-    )(pre, *xs, *halos, *[aux] * nx, w2, wb, wdt, *consts, *([] if cin is None else [cin]), *into)
-
-
-def mixz_kernel(pre, *refs, ns, pers):
+    )(pre, *srcs, *[aux] * nx, w2, wb, wdt, *consts, *([] if cin is None else [cin]), *into)
+
+
+def mixz_kernel(pre, *refs, ns, first):
     xs_, auxs = refs[:ns], refs[ns:2 * ns]
     (xa_ref, bg_ref, cg_ref, dc_ref, wz_ref, cin_ref, hp_ref, yn_ref, cout_ref, xv, av, zbuf, ybuf, xw, state) = refs[2 * ns:]
     g, i, tile = pl.program_id(0), pl.program_id(1), pl.program_id(2)
@@ -237,9 +248,9 @@
     def _():
         state[...] = cin_ref[0]
 
-    src = (i * n_tiles + tile) // pers
+    at = i * n_tiles + tile
     for k in range(ns):
-        @pl.when(src == k)
+        @pl.when((at >= first[k]) & (at < first[k + 1]))
         def _():
             xv[...] = xs_[k][...]
             av[...] = auxs[k][...]
@@ -299,15 +310,17 @@
 
 def mixz_call(pre, aux, amaps, xs, arrs, w2, cin, hp, *, nx, per, ofs, cofs):
     ns = len(xs)
-    pers = nx * per // ns
+    first = [0]
+    for v in xs:
+        first.append(min(first[-1] + v.shape[0] // MT, nx * per))
     n = nx * per * MT
     xa, bca, dc = arrs
-    piece = lambda k: (lambda i, t: jnp.clip(i * per + t - k * pers, 0, pers - 1))
+    piece = lambda k: (lambda i, t: jnp.clip(i * per + t - first[k], 0, first[k + 1] - first[k] - 1))
     rows = lambda w, c, o=ofs: pl.BlockSpec((MT, w), lambda g, i, t, b: (o + i * per + t, c(g)))
     state = lambda ofs: pl.BlockSpec((1, T, GW), lambda g, i, t, b: (ofs + i, 0, g))
     cols = lambda k: pl.BlockSpec((k, GW), lambda g, i, t, b: (0, g))
     in_specs = [pl.BlockSpec((MT, D), lambda g, i, t, b, k=k: (piece(k)(i, t), 0)) for k in range(ns)]
-    in_specs += [pl.BlockSpec((MT, T), lambda g, i, t, b, k=k: (amaps[k](b) * pers + piece(k)(i, t), 0)) for k in range(ns)]
+    in_specs += [pl.BlockSpec((MT, T), lambda g, i, t, b, k=k: (amaps[k](b) + piece(k)(i, t), 0)) for k in range(ns)]
     same = lambda g: g
     in_specs += [rows(GW, same), rows(T, same), rows(T, lambda g: 2 + g), rows(T, lambda g: 0), cols(D), state(cofs), cols(8)]
     gs = pltpu.PrefetchScalarGridSpec(
@@ -316,7 +329,7 @@
                         pltpu.VMEM((T, GW), bf16), pltpu.VMEM((T, GW), f32)],
     )
     return pl.pallas_call(
-        functools.partial(mixz_kernel, ns=ns, pers=pers), grid_spec=gs,
+        functools.partial(mixz_kernel, ns=ns, first=first), grid_spec=gs,
         out_shape=[jax.ShapeDtypeStruct((n, XW), bf16), jax.ShapeDtypeStruct((nx, T, XW), f32)],
         compiler_params=pltpu.CompilerParams(dimension_semantics=("arbitrary",) * 3, vmem_limit_bytes=60 * MIB),
         cost_estimate=pl.CostEstimate(flops=n * 20_000_000, bytes_accessed=n * 14000, transcendentals=n * 10000),
@@ -330,6 +343,7 @@
     return 2 * y + c
 
 
+PARTS = (2, 1, 1)
 NCH = 2
 
 
@@ -337,17 +351,21 @@
     return jnp.where(flag, 1, 0)
 
 
-def ahead_kernel(n_blocks, n_pl, seg_ref, tail_ref, x_hbm, w_hbm, segs_ref, tails_ref, x0_hbm, x1_hbm, w0_hbm, w1_hbm,
-                 xbuf, wbuf, in_sem, out_sem, send_sem, recv_sem):
+def ahead_kernel(n_blocks, n_pl, seg_ref, tail_ref, x_hbm, w_hbm, segs_ref, tails_ref, *refs):
     me, blk = lax.axis_index('tp'), lax.axis_index('sp')
-    step = w0_hbm.shape[0]
+    *outs, xbuf, wbuf, in_sem, out_sem, send_sem, recv_sem = refs
+    xs, ws = outs[:len(PARTS)], outs[len(PARTS):]
+    step = ws[0].shape[0]
     place = lax.axis_index('dp') * n_blocks + blk
-    moves = []
-    for k, (xo, wo) in enumerate(((x0_hbm, w0_hbm), (x1_hbm, w1_hbm))):
-        at = pl.multiple_of((k * n_pl + place) * step, HALO)
-        for j, (src, buf, dst) in enumerate(((x_hbm.at[pl.ds(k * xo.shape[0], xo.shape[0])], xbuf.at[k], xo),
-                                             (w_hbm.at[pl.ds(at, step)], wbuf.at[k], wo))):
-            moves.append((pltpu.make_async_copy(src, buf, in_sem.at[k, j]), pltpu.make_async_copy(buf, dst, out_sem.at[k, j])))
+    pieces, row = [], 0
+    for dst in xs:
+        size = dst.shape[0]
+        pieces.append((x_hbm.at[pl.ds(row, size)], xbuf.at[pl.ds(row, size)], dst))
+        row += size
+    for k, dst in enumerate(ws):
+        pieces.append((w_hbm.at[pl.ds(pl.multiple_of((k * n_pl + place) * step, HALO), step)], wbuf.at[k], dst))
+    moves = [(pltpu.make_async_copy(src, buf, in_sem.at[k]), pltpu.make_async_copy(buf, dst, out_sem.at[k]))
+             for k, (src, buf, dst) in enumerate(pieces)]
     for load, _ in moves:
         load.start()
     barrier = pltpu.get_barrier_semaphore()
@@ -420,17 +438,18 @@
 
 def ahead_call(seg, x, w, n_blocks, n_pl):
     rows = x.shape[0]
-    half, step = rows // NCH, w.shape[0] // (NCH * n_pl)
+    step = w.shape[0] // (NCH * n_pl)
+    n_out = len(PARTS) + NCH
     vmem, hbm = pl.BlockSpec(memory_space=pltpu.VMEM), pl.BlockSpec(memory_space=pl.ANY)
     sds = jax.ShapeDtypeStruct
     return pl.pallas_call(
         functools.partial(ahead_kernel, n_blocks, n_pl),
         grid=(1,),
         in_specs=[vmem, pl.BlockSpec((HALO, D), lambda i: (rows // HALO - 1, 0)), hbm, hbm],
-        out_specs=[vmem] * 2 + [hbm] * 4,
-        out_shape=[sds((5, rows // T, T), jnp.int32), sds((5, HALO, D), bf16)] + [sds((half, D), bf16)] * 2 + [sds((step, D), bf16)] * 2,
-        scratch_shapes=[pltpu.VMEM((NCH, half, D), bf16), pltpu.VMEM((NCH, step, D), bf16), pltpu.SemaphoreType.DMA((NCH, 2)),
-                        pltpu.SemaphoreType.DMA((NCH, 2)), pltpu.SemaphoreType.DMA((7, 2)), pltpu.SemaphoreType.DMA((4, 2))],
+        out_specs=[vmem] * 2 + [hbm] * n_out,
+        out_shape=[sds((5, rows // T, T), jnp.int32), sds((5, HALO, D), bf16)] + [sds((p * MT, D), bf16) for p in PARTS] + [sds((step, D), bf16)] * NCH,
+        scratch_shapes=[pltpu.VMEM((rows, D), bf16), pltpu.VMEM((NCH, step, D), bf16), pltpu.SemaphoreType.DMA((n_out,)),
+                        pltpu.SemaphoreType.DMA((n_out,)), pltpu.SemaphoreType.DMA((7, 2)), pltpu.SemaphoreType.DMA((4, 2))],
         compiler_params=pltpu.CompilerParams(collective_id=0, has_side_effects=True, vmem_limit_bytes=24 * MIB),
         name="ahead",
     )(seg.reshape(rows // T, T), x, x, w)
@@ -522,7 +541,7 @@
         scratch_shapes=[pltpu.VMEM((4, T + SUB, XW), f32), pltpu.VMEM((n, T, CW), f32), pltpu.VMEM((n, T, CW), f32),
                         pltpu.VMEM((4, T, XW), f32),                         pltpu.SemaphoreType.DMA((4,)), pltpu.SemaphoreType.DMA((n,)),
                         pltpu.SemaphoreType.DMA((n,)), pltpu.SemaphoreType.DMA((n,))],
-        compiler_params=pltpu.CompilerParams(collective_id=1, has_side_effects=True, vmem_limit_bytes=40 * MIB),
+        compiler_params=pltpu.CompilerParams(collective_id=1, has_side_effects=True, vmem_limit_bytes=63 * MIB),
         name="chain",
     )(e01, e2, e3)
 
@@ -603,13 +622,12 @@
     def body(x_loc, seg_loc, w_zx, w_bc, w_dt, conv_x, conv_bc, bias_x, bias_bc, a_log, dt_bias, d_skip, norm_w, w_out):
         rows, d = x_loc.shape
         me = lax.axis_index('tp')
-        ch = rows // NCH
-        per, kper = rows // MT, ch // MT
+        per, kper = rows // MT, rows // (NCH * MT)
         n_pl = mesh.shape['dp'] * n_blocks
         segs, tails, *parts = ahead_call(seg_loc, x_loc, w_out, n_blocks, n_pl)
         x_par = send(after(x_loc, segs), CORE_SWAP)
-        x_dir = [send(v, CHIP_SWAP) for v in parts[:NCH]]
-        w_half = [send(v, CHIP_SWAP) for v in parts[NCH:]]
+        x_dir = [send(v, CHIP_SWAP) for v in parts[:len(PARTS)]]
+        w_half = [send(v, CHIP_SWAP) for v in parts[len(PARTS):]]
 
         def w_gather(h, dep):
             return lax.all_gather(after(w_half[h], dep), ('dp', 'sp'), axis=0, tiled=True)
@@ -626,47 +644,46 @@
         weights = (w2, wb, w_dt)
         consts = (cw, cwb, hp1)
 
-        def front(slots, part, parts, xs, halos, hrows, carry, into, per):
-            return front_call(pre, aux, [lambda b, s=s: b[s] * parts + part for s in slots], xs, halos, hrows,
-                              weights, carry, consts, into, part, parts, per=per)
+        def front(slots, part, parts, runs, carry, into, per):
+            return front_call(pre, aux, [lambda b, s=s: b[s] * parts + part for s in slots], runs, weights, carry, consts,
+                              into, part, parts, per=per)
 
         tail_row = lambda s: (lambda b: b[s] * HALO)
-        *own, ends = front((0, 1), 0, 1, [x_loc, x_par], [tails] * 2, [tail_row(0), tail_row(1)], None, [], per)
+        *own, ends = front((0, 1), 0, 1, [(tails, tail_row(0), [x_loc]), (tails, tail_row(1), [x_par])], None, [], per)
         w_rem = [w_gather(0, ends)]
         x_dir[0] = after(x_dir[0], ends)
-        rem, carry, x_fwd = [[], []], [None, None], []
-        last = ends
-        for k in range(NCH):
-            x_fwd.append(send(x_dir[k], CORE_SWAP))
-            for r, xs in ((0, x_dir), (1, x_fwd)):
-                halo = (tails, tail_row(2 + r)) if k == 0 else (xs[k - 1], lambda b: ch - HALO)
-                *rem[r], carry[r] = front((2 + r,), k, NCH, [after(xs[k], last)], [halo[0]], [halo[1]], carry[r], rem[r], kper)
-                last = carry[r]
-            if k + 1 < NCH:
-                x_dir[k + 1] = after(x_dir[k + 1], carry[1])
-        starts = chain_call(ends, carry[0], carry[1], n_blocks)
+        x_fwd = [send(x_dir[0], CORE_SWAP)]
+        *rem2, c2 = front((2,), 0, NCH, [(tails, tail_row(2), x_dir[:1])], None, [], kper)
+        *rem3, c3 = front((3,), 0, NCH, [(tails, tail_row(3), [after(x_fwd[0], c2)])], None, [], kper)
+        x_dir[1] = after(x_dir[1], c2)
+        x_fwd.append(send(x_dir[1], CORE_SWAP))
+        end = lambda k: PARTS[k] * MT - HALO
+        *rem2, c2 = front((2,), 2, 4, [(x_dir[0], end(0), [after(x_dir[1], c3)])], c2, rem2, 1)
+        x_dir[2] = after(x_dir[2], c2)
+        x_fwd.append(send(x_dir[2], CORE_SWAP))
+        *rem2, c2 = front((2,), 3, 4, [(x_dir[1], end(1), [x_dir[2]])], c2, rem2, 1)
+        *rem3, c3 = front((3,), 1, NCH, [(x_fwd[0], end(0), [after(x_fwd[1], c2), x_fwd[2]])], c3, rem3, kper)
+        starts = chain_call(ends, c2, c3, n_blocks)
         w_rem.append(w_gather(1, starts))
 
         def mix(amaps, xs, arrs, start, **kw):
             return mixz_call(pre, aux, amaps, xs, arrs, w2, start, hp2, **kw)
 
-        part_of = lambda s, k: (lambda b: b[s] * NCH + k)
-        y_in = [[], []]
-        c, cofs = starts, 3
-        for k in range(NCH):
-            yn, c = mix([part_of(3, k)], [x_fwd[k]], rem[1], c, nx=1, per=kper, ofs=k * kper, cofs=cofs)
-            cofs = 0
-            y_in[1].append(send(yn, CHIP_SWAP))
-        yn, c = mix([part_of(2, k) for k in range(NCH)], x_dir, rem[0], after(starts, c), nx=1, per=per, ofs=0, cofs=2)
-        y_in[0] = send(yn, CHIP_SWAP)
-        y_own, _ = mix([lambda b: b[0], lambda b: b[1]], [x_loc, x_par], own, after(starts, c), nx=2, per=per, ofs=0, cofs=0)
+        at = lambda s, k=0: (lambda b: b[s] * per + k)
+        yn, c = mix([at(3)], x_fwd[:1], rem3, starts, nx=1, per=kper, ofs=0, cofs=3)
+        y_in = [send(yn, CHIP_SWAP)]
+        yn, c = mix([at(3, 2), at(3, 3)], x_fwd[1:], rem3, c, nx=1, per=kper, ofs=kper, cofs=0)
+        y_in.append(send(yn, CHIP_SWAP))
+        yn, c = mix([at(2), at(2, 2), at(2, 3)], x_dir, rem2, after(starts, c), nx=1, per=per, ofs=0, cofs=2)
+        y_in.append(send(yn, CHIP_SWAP))
+        y_own, _ = mix([at(0), at(1)], [x_loc, x_par], own, after(starts, c), nx=2, per=per, ofs=0, cofs=0)
         other = []
         for k in range(NCH):
-            part = out_call(1, k, y_own, y_in[1][k], 0, w_out, w_rem)
+            part = out_call(1, k, y_own, y_in[k], 0, w_out, w_rem)
             other.append(send(part, CORE_SWAP))
         y = None
         for k in range(NCH):
-            y = out_call(0, k, y_own, y_in[0], k, w_out, w_rem, x_loc, other[k], y)
+            y = out_call(0, k, y_own, y_in[2], k, w_out, w_rem, x_loc, other[k], y)
         return y
 
     return jax.shard_map(body, mesh=mesh, in_specs=(token_spec, seg_spec) + weight_specs, out_specs=token_spec, check_vma=False)

time: 739 us -> 822 us (1.11)
  the two profiles are of different devices: /device:TPU:30 before, /device:TPU:24 now
where the time goes in v4:
time: 822 us; the launch traced here: 814 us
  Pallas kernels  519 us (63%)
  waiting for transfers between devices  222 us (27%)
  local copies, waits for them, and re-layouts  40.2 us (5%)
  between operations  14.2 us (2%)
  starting transfers between devices  10.3 us (1%)
  other arithmetic  9.12 us (1%)
    ppermute x14, waiting for transfers between devices, send(): return lax.ppermute(v, 'tp', perm)  222 us
    pallas_call x6, Pallas kernels, front_call(): pl.pallas_call(functools.partial(front_kernel, nx=nx, per=per, where=wher...  218 us
    pallas_call x4, Pallas kernels, mixz_call(): pl.pallas_call(functools.partial(mixz_kernel, ns=ns, first=first), grid_s...  150 us
    pallas_call x4, Pallas kernels, out_call(): pl.pallas_call(out_kernel, grid=(D // NT,), in_specs=specs, out_specs=pl....  101 us
    unnamed x37, local copies, waits for them, and re-layouts  39.2 us
    pallas_call x1, Pallas kernels, chain_call(): pl.pallas_call(functools.partial(chain_kernel, n_blocks), in_specs=[hbm]...  37.6 us
  transfers between devices with their start and end apart: 16, of which 4 were waited for; matrix products, arithmetic and copies ran while one was open for 5% of the time, Pallas kernels for 59%

profile of v4, /device:TPU:24, one launch (start us, length us, event | category | flops | bytes accessed | tf_op | source)
XLA Modules:
  0.0 814.1 jit_solution(14630119409848370920)
XLA Ops:
  7.2 12.3 %ahead.1 = (s32[5,8,128]{2,1,0:T(8,128)S(1)}, bf16[5,16,4096]{2,1,0:T(8,128)(2,1)S(1)}, bf16[512,4096]{1,0:T(8,128)(2,1)S(1)}, bf16[256,4096]{1,0:T(8,128)(2,1)S...) custom-call(s32[8,128]{1,0:T(8,128)S(1)} %bitcast.37, ...), custom_call_target="tpu_custom_call" | custom-call | tf_op jit(solution)/shard_map/ahead/pallas_call | solution.py:445
  26.4 23.2 %copy.31 = bf16[512,8,2,2048]{3,1,2,0:T(8,128)(2,1)} copy(bf16[512,8,2,2048]{3,2,1,0:T(2,128)(2,1)} %bitcast.58) | data formatting | bytes 67108864
  49.7 5.1 copy.32
  59.4 5.2 select_select_fusion.refs_4_.refs_5_.refs_2_.refs_3_.refs_1_
  64.7 91.7 %front.6 = (bf16[2048,2048]{1,0:T(8,128)(2,1)}, bf16[2048,512]{1,0:T(8,128)(2,1)}, f32[2048,128]{1,0:T(8,128)}, f32[2,136,2048]{2,1,0:T(8,128)}) custom-call(s32[4]{0:T(128)} %pad_add_fusion.1.pre, bf16[80,4096]{1,0:T(8,128)(2,1)} %bitcast.38, bf16[1024,4096]{1,0:T(8,128)(2,1)} %refs_0_.5, bf16[80,4096]{1,0:T(8,128)(2,1)} %bitcast.39, ...), custom_call_target="tpu_custom_call" | custom-call | flops 51200000000 | bytes 20480000 | tf_op jit(solution)/shard_map/front/pallas_call | solution.py:230
  156.7 2.1 collective-permute-start.2
  158.8 90.9 %collective-permute-done.2.refs_1_.refs_0_ = bf16[512,4096]{1,0:T(8,128)(2,1)} collective-permute-done((bf16[512,4096]{1,0:T(8,128)(2,1)}, bf16[512,4096]{1,0:T(8,128)(2,1)}, u32[]{:S(2)}, u32[]{:S(2)}) %collective-permute-start.2) | collective-permute-done | bytes 4194336 | tf_op jit(solution)/shard_map/ppermute | solution.py:593
  251.7 29.2 %front.7 = (bf16[1024,2048]{1,0:T(8,128)(2,1)}, bf16[1024,512]{1,0:T(8,128)(2,1)}, f32[1024,128]{1,0:T(8,128)}, f32[1,136,2048]{2,1,0:T(8,128)}) custom-call(s32[4]{0:T(128)} %pad_add_fusion.1.pre, bf16[80,4096]{1,0:T(8,128)(2,1)} %bitcast.40, bf16[512,4096]{1,0:T(8,128)(2,1)} %collective-permute-done.2.refs_1_.refs_0_, ...), custom_call_target="tpu_custom_call" | custom-call | flops 12800000000 | bytes 5120000 | tf_op jit(solution)/shard_map/front/pallas_call | solution.py:230
  280.9 17.6 %collective-permute-done.1.refs_1_.refs_0_ = bf16[256,4096]{1,0:T(8,128)(2,1)} collective-permute-done((bf16[256,4096]{1,0:T(8,128)(2,1)}, bf16[256,4096]{1,0:T(8,128)(2,1)}, u32[]{:S(2)}, u32[]{:S(2)}) %collective-permute-start.1) | collective-permute-done | bytes 2097184 | tf_op jit(solution)/shard_map/ppermute | solution.py:593
  298.5 29.2 %front.8 = (bf16[1024,2048]{1,0:T(8,128)(2,1)}, bf16[1024,512]{1,0:T(8,128)(2,1)}, f32[1024,128]{1,0:T(8,128)}, f32[1,136,2048]{2,1,0:T(8,128)}) custom-call(s32[4]{0:T(128)} %pad_add_fusion.1.pre, bf16[80,4096]{1,0:T(8,128)(2,1)} %bitcast.41, bf16[512,4096]{1,0:T(8,128)(2,1)} %collective-permute-done.4.refs_1_.refs_0_, ...), custom_call_target="tpu_custom_call" | custom-call | flops 12800000000 | bytes 5120000 | tf_op jit(solution)/shard_map/front/pallas_call | solution.py:230
  327.7 19.4 %front.9 = (bf16[1024,2048]{1,0:T(8,128)(2,1)}, bf16[1024,512]{1,0:T(8,128)(2,1)}, f32[1024,128]{1,0:T(8,128)}, f32[1,136,2048]{2,1,0:T(8,128)}) custom-call(s32[4]{0:T(128)} %pad_add_fusion.1.pre, bf16[512,4096]{1,0:T(8,128)(2,1)} %collective-permute-done.2.refs_1_.refs_0_, ...), custom_call_target="tpu_custom_call", output_to_operand_aliasing={{0}: (11, {}), {1}: (12, {}), {2}: (13, {})} | custom-call | flops 6400000000 | bytes 2560000 | tf_op jit(solution)/shard_map/front/pallas_call | solution.py:230
  349.4 18.9 %front.10 = (bf16[1024,2048]{1,0:T(8,128)(2,1)}, bf16[1024,512]{1,0:T(8,128)(2,1)}, f32[1024,128]{1,0:T(8,128)}, f32[1,136,2048]{2,1,0:T(8,128)}) custom-call(s32[4]{0:T(128)} %pad_add_fusion.1.pre, bf16[256,4096]{1,0:T(8,128)(2,1)} %collective-permute-done.1.refs_1_.refs_0_, ...), custom_call_target="tpu_custom_call", output_to_operand_aliasing={{0}: (11, {}), {1}: (12, {}), {2}: (13, {})} | custom-call | flops 6400000000 | bytes 2560000 | tf_op jit(solution)/shard_map/front/pallas_call | solution.py:230
  368.4 29.5 %front.11 = (bf16[1024,2048]{1,0:T(8,128)(2,1)}, bf16[1024,512]{1,0:T(8,128)(2,1)}, f32[1024,128]{1,0:T(8,128)}, f32[1,136,2048]{2,1,0:T(8,128)}) custom-call(s32[4]{0:T(128)} %pad_add_fusion.1.pre, bf16[512,4096]{1,0:T(8,128)(2,1)} %collective-permute-done.4.refs_1_.refs_0_, ...), custom_call_target="tpu_custom_call", output_to_operand_aliasing={{0}: (12, {}), {1}: (13, {}), {2}: (14, {})} | custom-call | flops 12800000000 | bytes 5120000 | tf_op jit(solution)/shard_map/front/pallas_call | solution.py:230
  397.9 37.6 %chain.1.refs_9_.refs_11_.refs_7_ = f32[4,128,2048]{2,1,0:T(8,128)} custom-call(f32[2,136,2048]{2,1,0:T(8,128)} %get-tuple-element.56.e01_ref, f32[1,136,2048]{2,1,0:T(8,128)} %get-tuple-element.74.e2_ref, f32[1,136,2048]{2,1,0:T(8,128)} %get-tuple-element.79.e3_ref), custom_call_target="tpu_custom_call" | custom-call | tf_op jit(solution)/shard_map/chain/pallas_call | solution.py:536
  436.5 22.3 %mixz.6 = (bf16[512,2048]{1,0:T(8,128)(2,1)}, f32[1,128,2048]{2,1,0:T(8,128)}) custom-call(s32[4]{0:T(128)} %pad_add_fusion.1.pre, bf16[512,4096]{1,0:T(8,128)(2,1)} %collective-permute-done.4.refs_1_.refs_0_, f32[4096,128]{1,0:T(8,128)} %select_select_fusion.refs_4_.refs_5_.refs_2_.refs_3_.refs_1_, bf16[1024,2048]{1,0:T(8,128)(2,1)} %get-tuple-element.89.refs_2_.refs_4_, ...), custom_call_target="tpu_custom_call" | custom-call | flops 10240000000 | bytes 7168000 | tf_op jit(solution)/shard_map/mixz/pallas_call | solution.py:331
  458.8 21.6 %mixz.7 = (bf16[512,2048]{1,0:T(8,128)(2,1)}, f32[1,128,2048]{2,1,0:T(8,128)}) custom-call(s32[4]{0:T(128)} %pad_add_fusion.1.pre, bf16[256,4096]{1,0:T(8,128)(2,1)} %collective-permute-done.5.refs_1_.refs_0_, bf16[256,4096]{1,0:T(8,128)(2,1)} %collective-permute-done.6.refs_2_.refs_1_, ...), custom_call_target="tpu_custom_call" | custom-call | flops 10240000000 | bytes 7168000 | tf_op jit(solution)/shard_map/mixz/pallas_call | solution.py:331
  482.5 68.3 %mixz.4 = (bf16[2048,2048]{1,0:T(8,128)(2,1)}, f32[2,128,2048]{2,1,0:T(8,128)}) custom-call(s32[4]{0:T(128)} %pad_add_fusion.1.pre, bf16[1024,4096]{1,0:T(8,128)(2,1)} %refs_0_.5, bf16[1024,4096]{1,0:T(8,128)(2,1)} %collective-permute-done.refs_3_.refs_1_, f32[4096,128]{1,0:T(8,128)} %select_select_fusion.refs_4_.refs_5_.refs_2_.refs_3_.refs_1_, ...), custom_call_target="tpu_custom_call" | custom-call | flops 40960000000 | bytes 28672000 | tf_op jit(solution)/shard_map/mixz/pallas_call | solution.py:331
  550.8 21.1 %collective-permute-done.12.yr_ref = bf16[512,2048]{1,0:T(8,128)(2,1)} collective-permute-done((bf16[512,2048]{1,0:T(8,128)(2,1)}, bf16[512,2048]{1,0:T(8,128)(2,1)}, u32[]{:S(2)}, u32[]{:S(2)}) %collective-permute-start.12) | collective-permute-done | bytes 2097184 | tf_op jit(solution)/shard_map/ppermute | solution.py:593
  571.9 24.7 %out_proj.5 = f32[512,4096]{1,0:T(8,128)} custom-call(bf16[2048,2048]{1,0:T(8,128)(2,1)} %get-tuple-element.80.y_ref, bf16[512,2048]{1,0:T(8,128)(2,1)} %collective-permute-done.12.yr_ref, bf16[2048,4096]{1,0:T(8,128)(2,1)} %w_ref.7, bf16[1024,4096]{1,0:T(8,128)(2,1)} %all-gather.3.cloned.1.call-done.wr0_ref, ...), custom_call_target="tpu_custom_call" | custom-call | flops 16896000000 | bytes 51200000 | tf_op jit(solution)/shard_map/out_proj/pallas_call | solution.py:580
  597.9 24.4 %out_proj.4 = f32[512,4096]{1,0:T(8,128)} custom-call(bf16[2048,2048]{1,0:T(8,128)(2,1)} %get-tuple-element.80.y_ref, bf16[512,2048]{1,0:T(8,128)(2,1)} %copy-done.15, bf16[2048,4096]{1,0:T(8,128)(2,1)} %w_ref.7, bf16[1024,4096]{1,0:T(8,128)(2,1)} %all-gather.3.cloned.1.call-done.wr0_ref, bf16[1024,4096]{1,0:T(8,128)(2,1)} %all-gather.5.cloned.1.call-done.wr1_ref), custom_call_target="tpu_custom_call" | custom-call | flops 16896000000 | bytes 51200000 | tf_op jit(solution)/shard_map/out_proj/pallas_call | solution.py:580
  622.8 37.6 %mixz.5 = (bf16[1024,2048]{1,0:T(8,128)(2,1)}, f32[1,128,2048]{2,1,0:T(8,128)}) custom-call(s32[4]{0:T(128)} %pad_add_fusion.1.pre, bf16[512,4096]{1,0:T(8,128)(2,1)} %collective-permute-done.2.refs_1_.refs_0_, bf16[256,4096]{1,0:T(8,128)(2,1)} %collective-permute-done.1.refs_1_.refs_0_, bf16[256,4096]{1,0:T(8,128)(2,1)} %collective-permute-done.3.refs_1_.refs_2_, ...), custom_call_target="tpu_custom_call" | custom-call | flops 20480000000 | bytes 14336000 | tf_op jit(solution)/shard_map/mixz/pallas_call | solution.py:331
  661.1 92.1 %collective-permute-done.7.yr_ref = bf16[1024,2048]{1,0:T(8,128)(2,1)S(1)} collective-permute-done((bf16[1024,2048]{1,0:T(8,128)(2,1)}, bf16[1024,2048]{1,0:T(8,128)(2,1)S(1)}, u32[]{:S(2)}, u32[]{:S(2)}) %collective-permute-start.7) | collective-permute-done | bytes 4194336 | tf_op jit(solution)/shard_map/ppermute | solution.py:593
  755.1 25.9 %out_proj.6.refs_2_ = bf16[1024,4096]{1,0:T(8,128)(2,1)} custom-call(bf16[2048,2048]{1,0:T(8,128)(2,1)} %get-tuple-element.80.y_ref, bf16[1024,2048]{1,0:T(8,128)(2,1)} %copy-done.5, bf16[2048,4096]{1,0:T(8,128)(2,1)} %w_ref.7, bf16[1024,4096]{1,0:T(8,128)(2,1)} %all-gather.3.cloned.1.call-done.wr0_ref, ...), custom_call_target="tpu_custom_call" | custom-call | flops 16896000000 | bytes 51200000 | tf_op jit(solution)/shard_map/out_proj/pallas_call | solution.py:580
  781.0 25.8 %out_proj.7 = bf16[1024,4096]{1,0:T(8,128)(2,1)} custom-call(bf16[2048,2048]{1,0:T(8,128)(2,1)} %get-tuple-element.80.y_ref, bf16[1024,2048]{1,0:T(8,128)(2,1)} %copy-done.5, bf16[2048,4096]{1,0:T(8,128)(2,1)} %w_ref.7, bf16[1024,4096]{1,0:T(8,128)(2,1)} %all-gather.3.cloned.1.call-done.wr0_ref, ...), custom_call_target="tpu_custom_call", output_to_operand_aliasing={{}: (7, {})} | custom-call | flops 16896000000 | bytes 51200000 | tf_op jit(solution)/shard_map/out_proj/pallas_call | solution.py:580
  (86 shorter events, 24.2 us)
Async XLA Ops:
  6.5 565.4 %all-gather.3.cloned.1.call-start = ((), (), s32[]{:S(2)}) async-start(), calls=%async_computation | async-start | bytes 9437184 | tf_op jit(solution)/shard_map/all_gather | solution.py:633
  25.0 39.6 %collective-permute-start = (bf16[1024,4096]{1,0:T(8,128)(2,1)}, bf16[1024,4096]{1,0:T(8,128)(2,1)}, u32[]{:S(2)}, u32[]{:S(2)}) collective-permute-start(bf16[1024,4096]{1,0:T(8,128)(2,1)} %refs_0_.5), channel_id=1, source_target_pairs={{0,1},{1,0},{2,3},{3,2},{4,5},{5,4},{6,7},{7,6},{8,9},{9,8},{10,11... | collective-permute-start | bytes 25165832 | tf_op jit(solution)/shard_map/ppermute | solution.py:593
  25.4 131.0 %collective-permute-start.8 = (bf16[128,4096]{1,0:T(8,128)(2,1)S(1)}, bf16[128,4096]{1,0:T(8,128)(2,1)}, u32[]{:S(2)}, u32[]{:S(2)}) collective-permute-start(bf16[128,4096]{1,0:T(8,128)(2,1)S(1)} %get-tuple-element.85), channel_id=1, source_target_pairs={{0,2},{1,3},{2,0},{3,1},{4,6},{5,7},{6,4},{7,5},{8,10},{9,11},{10,... | collective-permute-start | bytes 3145736 | tf_op jit(solution)/shard_map/ppermute | solution.py:593
  49.6 6.6 copy-start.8
  49.6 6.6 copy-start.11
  49.6 6.6 copy-start.10
  49.6 7.2 copy-start.12
  49.7 7.2 copy-start.13
  49.7 9.1 %copy-start.7 = (bf16[4,2048]{1,0:T(4,128)(2,1)S(1)}, bf16[4,2048]{1,0:T(4,128)(2,1)}, u32[]{:S(2)}) copy-start(bf16[4,2048]{1,0:T(4,128)(2,1)} %param.19) | copy-start | bytes 49156
  156.4 415.5 %all-gather.5.cloned.1.call-start = ((), (), s32[]{:S(2)}) async-start(), calls=%async_computation.1 | async-start | bytes 9437184 | tf_op jit(solution)/shard_map/all_gather | solution.py:633
  156.7 93.0 %collective-permute-start.2 = (bf16[512,4096]{1,0:T(8,128)(2,1)}, bf16[512,4096]{1,0:T(8,128)(2,1)}, u32[]{:S(2)}, u32[]{:S(2)}) collective-permute-start(bf16[512,4096]{1,0:T(8,128)(2,1)} %copy-done.1), channel_id=1, source_target_pairs={{0,2},{1,3},{2,0},{3,1},{4,6},{5,7},{6,4},{7,5},{8,10},{9,11},{10,... | collective-permute-start | bytes 12582920 | tf_op jit(solution)/shard_map/ppermute | solution.py:593
  249.7 48.8 %collective-permute-start.4 = (bf16[512,4096]{1,0:T(8,128)(2,1)}, bf16[512,4096]{1,0:T(8,128)(2,1)}, u32[]{:S(2)}, u32[]{:S(2)}) collective-permute-start(bf16[512,4096]{1,0:T(8,128)(2,1)} %collective-permute-done.2.refs_1_.refs_0_), channel_id=1, source_target_pairs={{0,1},{1,0},{2,3},{3,2},{4,5},{5,4},{6,7},{7,6},{8,9},{9,8},{10,11... | collective-permute-start | bytes 12582920 | tf_op jit(solution)/shard_map/ppermute | solution.py:593
  249.7 48.8 %collective-permute-start.1 = (bf16[256,4096]{1,0:T(8,128)(2,1)}, bf16[256,4096]{1,0:T(8,128)(2,1)}, u32[]{:S(2)}, u32[]{:S(2)}) collective-permute-start(bf16[256,4096]{1,0:T(8,128)(2,1)} %copy-done.3), channel_id=1, source_target_pairs={{0,2},{1,3},{2,0},{3,1},{4,6},{5,7},{6,4},{7,5},{8,10},{9,11},{10,... | collective-permute-start | bytes 6291464 | tf_op jit(solution)/shard_map/ppermute | solution.py:593
  251.4 95.7 %collective-permute-start.3 = (bf16[256,4096]{1,0:T(8,128)(2,1)}, bf16[256,4096]{1,0:T(8,128)(2,1)}, u32[]{:S(2)}, u32[]{:S(2)}) collective-permute-start(bf16[256,4096]{1,0:T(8,128)(2,1)} %copy-done.2), channel_id=1, source_target_pairs={{0,2},{1,3},{2,0},{3,1},{4,6},{5,7},{6,4},{7,5},{8,10},{9,11},{10,... | collective-permute-start | bytes 6291464 | tf_op jit(solution)/shard_map/ppermute | solution.py:593
  298.5 69.9 %collective-permute-start.5 = (bf16[256,4096]{1,0:T(8,128)(2,1)}, bf16[256,4096]{1,0:T(8,128)(2,1)}, u32[]{:S(2)}, u32[]{:S(2)}) collective-permute-start(bf16[256,4096]{1,0:T(8,128)(2,1)} %collective-permute-done.1.refs_1_.refs_0_), channel_id=1, source_target_pairs={{0,1},{1,0},{2,3},{3,2},{4,5},{5,4},{6,7},{7,6},{8,9},{9,8},{10,11... | collective-permute-start | bytes 6291464 | tf_op jit(solution)/shard_map/ppermute | solution.py:593
  347.1 21.3 %collective-permute-start.6 = (bf16[256,4096]{1,0:T(8,128)(2,1)}, bf16[256,4096]{1,0:T(8,128)(2,1)}, u32[]{:S(2)}, u32[]{:S(2)}) collective-permute-start(bf16[256,4096]{1,0:T(8,128)(2,1)} %collective-permute-done.3.refs_1_.refs_2_), channel_id=1, source_target_pairs={{0,1},{1,0},{2,3},{3,2},{4,5},{5,4},{6,7},{7,6},{8,9},{9,8},{10,11... | collective-permute-start | bytes 6291464 | tf_op jit(solution)/shard_map/ppermute | solution.py:593
  347.7 87.9 %collective-permute-start.9 = (bf16[128,4096]{1,0:T(8,128)(2,1)}, bf16[128,4096]{1,0:T(8,128)(2,1)}, u32[]{:S(2)}, u32[]{:S(2)}) collective-permute-start(bf16[128,4096]{1,0:T(8,128)(2,1)} %get-tuple-element.87), channel_id=1, source_target_pairs={{0,2},{1,3},{2,0},{3,1},{4,6},{5,7},{6,4},{7,5},{8,10},{9,11},{10,... | collective-permute-start | bytes 3145736 | tf_op jit(solution)/shard_map/ppermute | solution.py:593
  397.9 37.7 %copy-start.9 = (bf16[2048]{0:T(1024)(128)(2,1)S(1)}, bf16[2048]{0:T(1024)(128)(2,1)}, u32[]{:S(2)}) copy-start(bf16[2048]{0:T(1024)(128)(2,1)} %param.26) | copy-start | bytes 12292
  397.9 37.7 %copy-start.14 = (f32[32]{0:T(128)S(1)}, f32[32]{0:T(128)}, u32[]{:S(2)}) copy-start(f32[32]{0:T(128)} %param.25) | copy-start | bytes 388
  480.4 116.2 %collective-permute-start.10 = (bf16[512,2048]{1,0:T(8,128)(2,1)}, bf16[512,2048]{1,0:T(8,128)(2,1)S(1)}, u32[]{:S(2)}, u32[]{:S(2)}) collective-permute-start(bf16[512,2048]{1,0:T(8,128)(2,1)} %get-tuple-element.93), channel_id=1, source_target_pairs={{0,2},{1,3},{2,0},{3,1},{4,6},{5,7},{6,4},{7,5},{8,10},{9,11},{10,... | collective-permute-start | bytes 6291464 | tf_op jit(solution)/shard_map/ppermute | solution.py:593
  481.1 90.8 %collective-permute-start.12 = (bf16[512,2048]{1,0:T(8,128)(2,1)}, bf16[512,2048]{1,0:T(8,128)(2,1)}, u32[]{:S(2)}, u32[]{:S(2)}) collective-permute-start(bf16[512,2048]{1,0:T(8,128)(2,1)} %get-tuple-element.94), channel_id=1, source_target_pairs={{0,2},{1,3},{2,0},{3,1},{4,6},{5,7},{6,4},{7,5},{8,10},{9,11},{10,... | collective-permute-start | bytes 6291464 | tf_op jit(solution)/shard_map/ppermute | solution.py:593
  596.6 156.6 %collective-permute-start.13 = (f32[512,4096]{1,0:T(8,128)}, f32[512,4096]{1,0:T(8,128)}, u32[]{:S(2)}, u32[]{:S(2)}) collective-permute-start(f32[512,4096]{1,0:T(8,128)} %out_proj.5), channel_id=1, source_target_pairs={{0,1},{1,0},{2,3},{3,2},{4,5},{5,4},{6,7},{7,6},{8,9},{9,8},{10,11... | collective-permute-start | bytes 25165832 | tf_op jit(solution)/shard_map/ppermute | solution.py:593
  622.3 158.7 %collective-permute-start.11 = (f32[512,4096]{1,0:T(8,128)}, f32[512,4096]{1,0:T(8,128)}, u32[]{:S(2)}, u32[]{:S(2)}) collective-permute-start(f32[512,4096]{1,0:T(8,128)} %out_proj.4), channel_id=1, source_target_pairs={{0,1},{1,0},{2,3},{3,2},{4,5},{5,4},{6,7},{7,6},{8,9},{9,8},{10,11... | collective-permute-start | bytes 25165832 | tf_op jit(solution)/shard_map/ppermute | solution.py:593
  660.4 92.8 %collective-permute-start.7 = (bf16[1024,2048]{1,0:T(8,128)(2,1)}, bf16[1024,2048]{1,0:T(8,128)(2,1)S(1)}, u32[]{:S(2)}, u32[]{:S(2)}) collective-permute-start(bf16[1024,2048]{1,0:T(8,128)(2,1)} %get-tuple-element.84), channel_id=1, source_target_pairs={{0,2},{1,3},{2,0},{3,1},{4,6},{5,7},{6,4},{7,5},{8,10},{9,11},{10,... | collective-permute-start | bytes 12582920 | tf_op jit(solution)/shard_map/ppermute | solution.py:593
  (8 other events, 14.6 us)
Sparse Core Ops, SparseCore 0:
  156.6 123.9 all-gather.2
  435.8 122.5 all-gather.4

commit v5 on v4

--- a/solution.py
+++ b/solution.py
@@ -40,6 +40,10 @@
     return jnp.where(lanes < HEAD, lane_bcast(cols, 2 * p), lane_bcast(cols, 2 * p + 1))
 
 
+def columns(flags):
+    return jnp.concatenate([flags, jnp.zeros((T - SUB, T), f32)], axis=0).T
+
+
 def row(ref, r):
     return ref[r:r + 1, :]
 
@@ -61,6 +65,7 @@
     nm = nx * per
     rows = lax.broadcasted_iota(jnp.int32, (T, T), 0)
     cols = lax.broadcasted_iota(jnp.int32, (T, T), 1)
+    lo_half = cols < HEAD
     tiles = [slice(t * T, (t + 1) * T) for t in range(MT // T)]
 
     def copies(m):
@@ -159,7 +164,8 @@
         bbuf[:, NB:] = jnp.zeros((MH, T), f32)
         for m in range(nm):
             i, s = divmod(m, per)
-            abuf[m] = auxs[i][s * MT:(s + 1) * MT, :]
+            for ts in tiles:
+                abuf[m, ts, :] = columns(auxs[i][(s * MT + ts.start) // T])
 
         @pl.loop(0, nm)
         def _(m):
@@ -169,7 +175,7 @@
                     for c in copies(k):
                         c.wait()
             bbuf[:, 0:NB] = jnp.dot(xbuf[m], wb_ref[...], preferred_element_type=f32).astype(bf16).astype(f32)
-            bbuf[:, NB:NB + HEADS] = jnp.dot(xbuf[m], wdt_ref[...], preferred_element_type=f32).astype(bf16).astype(f32)
+            bbuf[:, NB:NB + HEADS] = mac(xbuf[m], wdt_ref[...], 1, 1).astype(bf16).astype(f32)
             x_dot(m)
             setup(m, m // per, lax.rem(m, per))
 
@@ -215,8 +221,8 @@
     whole = lambda *shape, mode=ONE, r=0: pl.BlockSpec(shape, lambda j, b: (r, 0), pipeline_mode=mode)
     cols = lambda k, r=0: pl.BlockSpec((k, XT), lambda j, b: (r, prev(j)))
     state = pl.BlockSpec((nx, T + 8, XT), lambda j, b: (0, 0, prev(j)))
-    in_specs = [hbm] * ns + [pl.BlockSpec((per * MT, T), lambda j, b, f=f: (f(b), 0), pipeline_mode=ONE) for f in amaps] + [
-        pl.BlockSpec((D, XT), lambda j, b: (0, nt + jnp.minimum(j, nt - 1))), whole(D, NB), whole(D, HEADS),
+    in_specs = [hbm] * ns + [pl.BlockSpec((per * MT // T, SUB, T), lambda j, b, f=f: (f(b), 0, 0), pipeline_mode=ONE) for f in amaps] + [
+        pl.BlockSpec((D, XT), lambda j, b: (0, nt + jnp.minimum(j, nt - 1))), whole(D, NB), whole(HEADS, D),
         cols(SUB), whole(SUB, NB), whole(SUB, T)] + ([] if cin is None else [state]) + [hbm] * len(into)
     n_in = len(in_specs) + 1
     gs = pltpu.PrefetchScalarGridSpec(
@@ -261,9 +267,8 @@
     zero = jnp.zeros((T, T), bf16)
     for t in range(MT // T):
         rs = slice(t * T, (t + 1) * T)
-        aux = av[rs, :]
-        auxt = aux.T
-        mask = (rows >= cols) & (lane_bcast(aux, 5) == jnp.broadcast_to(auxt[5:6, :], (T, T)))
+        aux = columns(av[t])
+        mask = (rows >= cols) & (lane_bcast(aux, 5) == jnp.broadcast_to(av[t, 5:6, :], (T, T)))
         k_in = lane_bcast(aux, 3)
         k_end = lane_bcast(aux, 4)
         dc = pltpu.roll(dc_ref[rs, :], lax.rem(T - 16 * g, T), 1)
@@ -320,12 +325,12 @@
     state = lambda ofs: pl.BlockSpec((1, T, GW), lambda g, i, t, b: (ofs + i, 0, g))
     cols = lambda k: pl.BlockSpec((k, GW), lambda g, i, t, b: (0, g))
     in_specs = [pl.BlockSpec((MT, D), lambda g, i, t, b, k=k: (piece(k)(i, t), 0)) for k in range(ns)]
-    in_specs += [pl.BlockSpec((MT, T), lambda g, i, t, b, k=k: (amaps[k](b) + piece(k)(i, t), 0)) for k in range(ns)]
+    in_specs += [pl.BlockSpec((MT // T, SUB, T), lambda g, i, t, b, k=k: (amaps[k](b) + piece(k)(i, t), 0, 0)) for k in range(ns)]
     same = lambda g: g
     in_specs += [rows(GW, same), rows(T, same), rows(T, lambda g: 2 + g), rows(T, lambda g: 0), cols(D), state(cofs), cols(8)]
     gs = pltpu.PrefetchScalarGridSpec(
         num_scalar_prefetch=1, grid=(2, nx, per), in_specs=in_specs, out_specs=[rows(GW, same, 0), state(0)],
-        scratch_shapes=[pltpu.VMEM((MT, D), bf16), pltpu.VMEM((MT, T), f32), pltpu.VMEM((MT, GW), f32), pltpu.VMEM((T, GW), f32),
+        scratch_shapes=[pltpu.VMEM((MT, D), bf16), pltpu.VMEM((MT // T, SUB, T), f32), pltpu.VMEM((MT, GW), f32), pltpu.VMEM((T, GW), f32),
                         pltpu.VMEM((T, GW), bf16), pltpu.VMEM((T, GW), f32)],
     )
     return pl.pallas_call(
@@ -351,9 +356,23 @@
     return jnp.where(flag, 1, 0)
 
 
-def ahead_kernel(n_blocks, n_pl, seg_ref, tail_ref, x_hbm, w_hbm, segs_ref, tails_ref, *refs):
+def token_flags(segs_ref, q, flags_ref):
+    seg = segs_ref[q + 1]
+    shape = seg.shape
+    tiles, lanes = (lax.broadcasted_iota(jnp.int32, shape, d) for d in range(2))
+    before = jnp.where(tiles == 0, jnp.broadcast_to(segs_ref[q][shape[0] - 1:, :], shape), pltpu.roll(seg, 1, 0))
+    back = [jnp.where(lanes < d, pltpu.roll(before, d, 1), pltpu.roll(seg, d, 1)) for d in (1, 2, 3)]
+    back += [jnp.broadcast_to(back[0][:, :1], shape), jnp.broadcast_to(seg[:, T - 1:], shape)]
+    flags = [jnp.where(seg == v, 1.0, 0.0) for v in back] + [(seg - jnp.broadcast_to(segs_ref[1][:1, :1], shape)).astype(f32)]
+    for t in range(shape[0]):
+        for f, v in enumerate(flags):
+            flags_ref[q * shape[0] + t, f:f + 1, :] = v[t:t + 1, :]
+        flags_ref[q * shape[0] + t, len(flags):, :] = jnp.zeros((SUB - len(flags), T), f32)
+
+
+def ahead_kernel(n_blocks, n_pl, seg_ref, tail_ref, x_hbm, w_hbm, flags_ref, tails_ref, *refs):
     me, blk = lax.axis_index('tp'), lax.axis_index('sp')
-    *outs, xbuf, wbuf, in_sem, out_sem, send_sem, recv_sem = refs
+    *outs, segs_ref, xbuf, wbuf, in_sem, out_sem, send_sem, recv_sem = refs
     xs, ws = outs[:len(PARTS)], outs[len(PARTS):]
     step = ws[0].shape[0]
     place = lax.axis_index('dp') * n_blocks + blk
@@ -432,6 +451,8 @@
         for c in outer[0]:
             c.wait_recv()
 
+    for q in range(4):
+        token_flags(segs_ref, q, flags_ref)
     for _, store in moves:
         store.wait()
 
@@ -447,8 +468,8 @@
         grid=(1,),
         in_specs=[vmem, pl.BlockSpec((HALO, D), lambda i: (rows // HALO - 1, 0)), hbm, hbm],
         out_specs=[vmem] * 2 + [hbm] * n_out,
-        out_shape=[sds((5, rows // T, T), jnp.int32), sds((5, HALO, D), bf16)] + [sds((p * MT, D), bf16) for p in PARTS] + [sds((step, D), bf16)] * NCH,
-        scratch_shapes=[pltpu.VMEM((rows, D), bf16), pltpu.VMEM((NCH, step, D), bf16), pltpu.SemaphoreType.DMA((n_out,)),
+        out_shape=[sds((4 * rows // T, SUB, T), f32), sds((5, HALO, D), bf16)] + [sds((p * MT, D), bf16) for p in PARTS] + [sds((step, D), bf16)] * NCH,
+        scratch_shapes=[pltpu.VMEM((5, rows // T, T), jnp.int32), pltpu.VMEM((rows, D), bf16), pltpu.VMEM((NCH, step, D), bf16), pltpu.SemaphoreType.DMA((n_out,)),
                         pltpu.SemaphoreType.DMA((n_out,)), pltpu.SemaphoreType.DMA((7, 2)), pltpu.SemaphoreType.DMA((4, 2))],
         compiler_params=pltpu.CompilerParams(collective_id=0, has_side_effects=True, vmem_limit_bytes=24 * MIB),
         name="ahead",
@@ -601,19 +622,6 @@
 CHIP_SWAP = [(i, i ^ 2) for i in range(4)]
 
 
-def token_aux(seg_ext):
-    seg = seg_ext[3:]
-    n = seg.shape[0]
-    tile_prev = jnp.repeat(seg_ext[2:n + 2:T], T)
-    tile_last = jnp.repeat(seg[T - 1::T], T)
-    cols = [seg == seg_ext[3 - k:n + 3 - k] for k in (1, 2, 3)] + [seg == tile_prev, seg == tile_last, seg - seg_ext[0]]
-    lane = lax.broadcasted_iota(jnp.int32, (n, T), 1)
-    out = jnp.zeros((n, T), f32)
-    for i, c in enumerate(cols):
-        out = jnp.where(lane == i, c.astype(f32)[:, None], out)
-    return out
-
-
 def solution(mesh):
     n_blocks = mesh.shape['sp']
     token_spec = seg_spec = P(('dp', 'sp', 'tp'))
@@ -624,15 +632,14 @@
         me = lax.axis_index('tp')
         per, kper = rows // MT, rows // (NCH * MT)
         n_pl = mesh.shape['dp'] * n_blocks
-        segs, tails, *parts = ahead_call(seg_loc, x_loc, w_out, n_blocks, n_pl)
-        x_par = send(after(x_loc, segs), CORE_SWAP)
+        aux, tails, *parts = ahead_call(seg_loc, x_loc, w_out, n_blocks, n_pl)
+        x_par = send(after(x_loc, aux), CORE_SWAP)
         x_dir = [send(v, CHIP_SWAP) for v in parts[:len(PARTS)]]
         w_half = [send(v, CHIP_SWAP) for v in parts[len(PARTS):]]
 
         def w_gather(h, dep):
             return lax.all_gather(after(w_half[h], dep), ('dp', 'sp'), axis=0, tiled=True)
 
-        aux = token_aux(jnp.concatenate([segs[0].reshape(-1)[-3:], segs[1:].reshape(-1)]))
         tails = tails.reshape(-1, d)
         w2, wb = w_zx.reshape(d, 2 * XW), w_bc.reshape(d, NB)
         pad = lambda v: jnp.pad(v.astype(f32), ((0, SUB - v.shape[0]), (0, 0)))
@@ -641,7 +648,7 @@
         hp1 = jnp.pad(jnp.stack([dt_bias, a_log]), ((0, 6), (0, T - HEADS)))
         hp2 = pad(jnp.stack([jnp.repeat(d_skip, HEAD), norm_w.astype(f32)]))
         pre = jnp.stack([seq_slot(me, s) for s in range(4)]).astype(jnp.int32)
-        weights = (w2, wb, w_dt)
+        weights = (w2, wb, w_dt.T)
         consts = (cw, cwb, hp1)
 
         def front(slots, part, parts, runs, carry, into, per):
@@ -655,10 +662,10 @@
         x_fwd = [send(x_dir[0], CORE_SWAP)]
         *rem2, c2 = front((2,), 0, NCH, [(tails, tail_row(2), x_dir[:1])], None, [], kper)
         *rem3, c3 = front((3,), 0, NCH, [(tails, tail_row(3), [after(x_fwd[0], c2)])], None, [], kper)
-        x_dir[1] = after(x_dir[1], c2)
+        x_dir[1] = after(x_dir[1], c3)
         x_fwd.append(send(x_dir[1], CORE_SWAP))
         end = lambda k: PARTS[k] * MT - HALO
-        *rem2, c2 = front((2,), 2, 4, [(x_dir[0], end(0), [after(x_dir[1], c3)])], c2, rem2, 1)
+        *rem2, c2 = front((2,), 2, 4, [(x_dir[0], end(0), [x_dir[1]])], c2, rem2, 1)
         x_dir[2] = after(x_dir[2], c2)
         x_fwd.append(send(x_dir[2], CORE_SWAP))
         *rem2, c2 = front((2,), 3, 4, [(x_dir[1], end(1), [x_dir[2]])], c2, rem2, 1)

time: 822 us -> 809 us (0.984)
  the two profiles are of different devices: /device:TPU:24 before, /device:TPU:26 now
where the time goes in v5:
time: 809 us; the launch traced here: 802 us
  Pallas kernels  519 us (64%)
  waiting for transfers between devices  218 us (27%)
  local copies, waits for them, and re-layouts  38.6 us (5%)
  between operations  14.1 us (2%)
  starting transfers between devices  9.8 us (1%)
    ppermute x14, waiting for transfers between devices, send(): return lax.ppermute(v, 'tp', perm)  218 us
    pallas_call x6, Pallas kernels, front_call(): pl.pallas_call(functools.partial(front_kernel, nx=nx, per=per, where=wher...  216 us
    pallas_call x4, Pallas kernels, mixz_call(): pl.pallas_call(functools.partial(mixz_kernel, ns=ns, first=first), grid_s...  152 us
    pallas_call x4, Pallas kernels, out_call(): pl.pallas_call(out_kernel, grid=(D // NT,), in_specs=specs, out_specs=pl....  101 us
    unnamed x36, local copies, waits for them, and re-layouts  38.4 us
    pallas_call x1, Pallas kernels, chain_call(): pl.pallas_call(functools.partial(chain_kernel, n_blocks), in_specs=[hbm]...  37.8 us
  transfers between devices with their start and end apart: 16, of which 4 were waited for; matrix products, arithmetic and copies ran while one was open for 4% of the time, Pallas kernels for 60%

profile of v5, /device:TPU:26, one launch (start us, length us, event | category | flops | bytes accessed | tf_op | source)
XLA Modules:
  0.0 802.4 jit_solution(17458404656889852449)
XLA Ops:
  7.2 12.5 %ahead.1 = (f32[32,8,128]{2,1,0:T(8,128)S(1)}, bf16[5,16,4096]{2,1,0:T(8,128)(2,1)S(1)}, bf16[512,4096]{1,0:T(8,128)(2,1)S(1)}, bf16[256,4096]{1,0:T(8,128)(2,1)...) custom-call(s32[8,128]{1,0:T(8,128)S(1)} %bitcast.19, ...), custom_call_target="tpu_custom_call" | custom-call | tf_op jit(solution)/shard_map/ahead/pallas_call | solution.py:466
  20.3 2.0 copy-done.2
  26.3 23.2 %copy.25 = bf16[512,8,2,2048]{3,1,2,0:T(8,128)(2,1)} copy(bf16[512,8,2,2048]{3,2,1,0:T(2,128)(2,1)} %bitcast.40) | data formatting | bytes 67108864
  49.6 5.0 copy.26
  57.2 90.9 %front.6 = (bf16[2048,2048]{1,0:T(8,128)(2,1)}, bf16[2048,512]{1,0:T(8,128)(2,1)}, f32[2048,128]{1,0:T(8,128)}, f32[2,136,2048]{2,1,0:T(8,128)}) custom-call(s32[4]{0:T(128)} %pad_add_fusion.pre, bf16[80,4096]{1,0:T(8,128)(2,1)} %bitcast.20, bf16[1024,4096]{1,0:T(8,128)(2,1)} %refs_0_.5, bf16[80,4096]{1,0:T(8,128)(2,1)} %bitcast.21, ...), custom_call_target="tpu_custom_call" | custom-call | flops 51200000000 | bytes 20480000 | tf_op jit(solution)/shard_map/front/pallas_call | solution.py:236
  148.4 2.1 collective-permute-start.2
  150.5 90.9 %collective-permute-done.2.refs_1_.refs_0_ = bf16[512,4096]{1,0:T(8,128)(2,1)} collective-permute-done((bf16[512,4096]{1,0:T(8,128)(2,1)}, bf16[512,4096]{1,0:T(8,128)(2,1)}, u32[]{:S(2)}, u32[]{:S(2)}) %collective-permute-start.2) | collective-permute-done | bytes 4194336 | tf_op jit(solution)/shard_map/ppermute | solution.py:614
  243.4 29.1 %front.7 = (bf16[1024,2048]{1,0:T(8,128)(2,1)}, bf16[1024,512]{1,0:T(8,128)(2,1)}, f32[1024,128]{1,0:T(8,128)}, f32[1,136,2048]{2,1,0:T(8,128)}) custom-call(s32[4]{0:T(128)} %pad_add_fusion.pre, bf16[80,4096]{1,0:T(8,128)(2,1)} %bitcast.22, bf16[512,4096]{1,0:T(8,128)(2,1)} %collective-permute-done.2.refs_1_.refs_0_, f32[32,8,128]{2,1,0:T(8,128)} %copy-done, ...), custom_call_target="tpu_custom_call" | custom-call | flops 12800000000 | bytes 5120000 | tf_op jit(solution)/shard_map/front/pallas_call | solution.py:236
  272.6 28.8 %front.8 = (bf16[1024,2048]{1,0:T(8,128)(2,1)}, bf16[1024,512]{1,0:T(8,128)(2,1)}, f32[1024,128]{1,0:T(8,128)}, f32[1,136,2048]{2,1,0:T(8,128)}) custom-call(s32[4]{0:T(128)} %pad_add_fusion.pre, bf16[80,4096]{1,0:T(8,128)(2,1)} %bitcast.23, bf16[512,4096]{1,0:T(8,128)(2,1)} %collective-permute-done.3.refs_1_.refs_0_, f32[32,8,128]{2,1,0:T(8,128)} %copy-done, ...), custom_call_target="tpu_custom_call" | custom-call | flops 12800000000 | bytes 5120000 | tf_op jit(solution)/shard_map/front/pallas_call | solution.py:236
  301.4 19.2 %front.9 = (bf16[1024,2048]{1,0:T(8,128)(2,1)}, bf16[1024,512]{1,0:T(8,128)(2,1)}, f32[1024,128]{1,0:T(8,128)}, f32[1,136,2048]{2,1,0:T(8,128)}) custom-call(s32[4]{0:T(128)} %pad_add_fusion.pre, bf16[512,4096]{1,0:T(8,128)(2,1)} %collective-permute-done.2.refs_1_.refs_0_, ...), custom_call_target="tpu_custom_call", output_to_operand_aliasing={{0}: (11, {}), {1}: (12, {}), {2}: (13, {})} | custom-call | flops 6400000000 | bytes 2560000 | tf_op jit(solution)/shard_map/front/pallas_call | solution.py:236
  320.6 14.1 %collective-permute-done.4.refs_1_.refs_2_ = bf16[256,4096]{1,0:T(8,128)(2,1)} collective-permute-done((bf16[256,4096]{1,0:T(8,128)(2,1)}, bf16[256,4096]{1,0:T(8,128)(2,1)}, u32[]{:S(2)}, u32[]{:S(2)}) %collective-permute-start.4) | collective-permute-done | bytes 2097184 | tf_op jit(solution)/shard_map/ppermute | solution.py:614
  336.4 18.7 %front.10 = (bf16[1024,2048]{1,0:T(8,128)(2,1)}, bf16[1024,512]{1,0:T(8,128)(2,1)}, f32[1024,128]{1,0:T(8,128)}, f32[1,136,2048]{2,1,0:T(8,128)}) custom-call(s32[4]{0:T(128)} %pad_add_fusion.pre, bf16[256,4096]{1,0:T(8,128)(2,1)} %collective-permute-done.1.refs_1_.refs_0_, ...), custom_call_target="tpu_custom_call", output_to_operand_aliasing={{0}: (11, {}), {1}: (12, {}), {2}: (13, {})} | custom-call | flops 6400000000 | bytes 2560000 | tf_op jit(solution)/shard_map/front/pallas_call | solution.py:236
  355.2 29.2 %front.11 = (bf16[1024,2048]{1,0:T(8,128)(2,1)}, bf16[1024,512]{1,0:T(8,128)(2,1)}, f32[1024,128]{1,0:T(8,128)}, f32[1,136,2048]{2,1,0:T(8,128)}) custom-call(s32[4]{0:T(128)} %pad_add_fusion.pre, bf16[512,4096]{1,0:T(8,128)(2,1)} %collective-permute-done.3.refs_1_.refs_0_, ...), custom_call_target="tpu_custom_call", output_to_operand_aliasing={{0}: (12, {}), {1}: (13, {}), {2}: (14, {})} | custom-call | flops 12800000000 | bytes 5120000 | tf_op jit(solution)/shard_map/front/pallas_call | solution.py:236
  384.4 37.8 %chain.1.refs_9_.refs_11_.refs_7_ = f32[4,128,2048]{2,1,0:T(8,128)} custom-call(f32[2,136,2048]{2,1,0:T(8,128)} %get-tuple-element.55.e01_ref, f32[1,136,2048]{2,1,0:T(8,128)} %get-tuple-element.72.e2_ref, f32[1,136,2048]{2,1,0:T(8,128)} %get-tuple-element.77.e3_ref), custom_call_target="tpu_custom_call" | custom-call | tf_op jit(solution)/shard_map/chain/pallas_call | solution.py:557
  423.1 22.3 %mixz.6 = (bf16[512,2048]{1,0:T(8,128)(2,1)}, f32[1,128,2048]{2,1,0:T(8,128)}) custom-call(s32[4]{0:T(128)} %pad_add_fusion.pre, bf16[512,4096]{1,0:T(8,128)(2,1)} %collective-permute-done.3.refs_1_.refs_0_, f32[32,8,128]{2,1,0:T(8,128)} %copy-done, bf16[1024,2048]{1,0:T(8,128)(2,1)} %get-tuple-element.87.refs_2_.refs_4_, ...), custom_call_target="tpu_custom_call" | custom-call | flops 10240000000 | bytes 7168000 | tf_op jit(solution)/shard_map/mixz/pallas_call | solution.py:336
  445.4 21.8 %mixz.7 = (bf16[512,2048]{1,0:T(8,128)(2,1)}, f32[1,128,2048]{2,1,0:T(8,128)}) custom-call(s32[4]{0:T(128)} %pad_add_fusion.pre, bf16[256,4096]{1,0:T(8,128)(2,1)} %collective-permute-done.5.refs_1_.refs_0_, bf16[256,4096]{1,0:T(8,128)(2,1)} %collective-permute-done.6.refs_2_.refs_1_, f32[32,8,128]{2,1,0:T(8,128)} %copy-done, f32[32,8,128]{2,1,0:T(8,128)} %copy-done, ...), custom_call_target="tpu_custom_call" | custom-call | flops 10240000000 | bytes 7168000 | tf_op jit(solution)/shard_map/mixz/pallas_call | solution.py:336
  469.4 69.6 %mixz.4 = (bf16[2048,2048]{1,0:T(8,128)(2,1)}, f32[2,128,2048]{2,1,0:T(8,128)}) custom-call(s32[4]{0:T(128)} %pad_add_fusion.pre, bf16[1024,4096]{1,0:T(8,128)(2,1)} %refs_0_.5, bf16[1024,4096]{1,0:T(8,128)(2,1)} %collective-permute-done.refs_3_.refs_1_, f32[32,8,128]{2,1,0:T(8,128)} %copy-done, f32[32,8,128]{2,1,0:T(8,128)} %copy-done, ...), custom_call_target="tpu_custom_call" | custom-call | flops 40960000000 | bytes 28672000 | tf_op jit(solution)/shard_map/mixz/pallas_call | solution.py:336
  538.9 20.9 %collective-permute-done.12.yr_ref = bf16[512,2048]{1,0:T(8,128)(2,1)} collective-permute-done((bf16[512,2048]{1,0:T(8,128)(2,1)}, bf16[512,2048]{1,0:T(8,128)(2,1)}, u32[]{:S(2)}, u32[]{:S(2)}) %collective-permute-start.12) | collective-permute-done | bytes 2097184 | tf_op jit(solution)/shard_map/ppermute | solution.py:614
  559.9 24.6 %out_proj.5 = f32[512,4096]{1,0:T(8,128)} custom-call(bf16[2048,2048]{1,0:T(8,128)(2,1)} %get-tuple-element.78.y_ref, bf16[512,2048]{1,0:T(8,128)(2,1)} %collective-permute-done.12.yr_ref, bf16[2048,4096]{1,0:T(8,128)(2,1)} %w_ref.7, bf16[1024,4096]{1,0:T(8,128)(2,1)} %all-gather.3.cloned.1.call-done.wr0_ref, ...), custom_call_target="tpu_custom_call" | custom-call | flops 16896000000 | bytes 51200000 | tf_op jit(solution)/shard_map/out_proj/pallas_call | solution.py:601
  585.8 24.4 %out_proj.4 = f32[512,4096]{1,0:T(8,128)} custom-call(bf16[2048,2048]{1,0:T(8,128)(2,1)} %get-tuple-element.78.y_ref, bf16[512,2048]{1,0:T(8,128)(2,1)} %copy-done.15, bf16[2048,4096]{1,0:T(8,128)(2,1)} %w_ref.7, bf16[1024,4096]{1,0:T(8,128)(2,1)} %all-gather.3.cloned.1.call-done.wr0_ref, bf16[1024,4096]{1,0:T(8,128)(2,1)} %all-gather.5.cloned.1.call-done.wr1_ref), custom_call_target="tpu_custom_call" | custom-call | flops 16896000000 | bytes 51200000 | tf_op jit(solution)/shard_map/out_proj/pallas_call | solution.py:601
  610.7 38.1 %mixz.5 = (bf16[1024,2048]{1,0:T(8,128)(2,1)}, f32[1,128,2048]{2,1,0:T(8,128)}) custom-call(s32[4]{0:T(128)} %pad_add_fusion.pre, bf16[512,4096]{1,0:T(8,128)(2,1)} %collective-permute-done.2.refs_1_.refs_0_, bf16[256,4096]{1,0:T(8,128)(2,1)} %collective-permute-done.1.refs_1_.refs_0_, bf16[256,4096]{1,0:T(8,128)(2,1)} %collective-permute-done.4.refs_1_.refs_2_, ...), custom_call_target="tpu_custom_call" | custom-call | flops 20480000000 | bytes 14336000 | tf_op jit(solution)/shard_map/mixz/pallas_call | solution.py:336
  649.4 92.1 %collective-permute-done.7.yr_ref = bf16[1024,2048]{1,0:T(8,128)(2,1)S(1)} collective-permute-done((bf16[1024,2048]{1,0:T(8,128)(2,1)}, bf16[1024,2048]{1,0:T(8,128)(2,1)S(1)}, u32[]{:S(2)}, u32[]{:S(2)}) %collective-permute-start.7) | collective-permute-done | bytes 4194336 | tf_op jit(solution)/shard_map/ppermute | solution.py:614
  743.5 25.8 %out_proj.6.refs_2_ = bf16[1024,4096]{1,0:T(8,128)(2,1)} custom-call(bf16[2048,2048]{1,0:T(8,128)(2,1)} %get-tuple-element.78.y_ref, bf16[1024,2048]{1,0:T(8,128)(2,1)} %copy-done.6, bf16[2048,4096]{1,0:T(8,128)(2,1)} %w_ref.7, bf16[1024,4096]{1,0:T(8,128)(2,1)} %all-gather.3.cloned.1.call-done.wr0_ref, ...), custom_call_target="tpu_custom_call" | custom-call | flops 16896000000 | bytes 51200000 | tf_op jit(solution)/shard_map/out_proj/pallas_call | solution.py:601
  769.3 25.8 %out_proj.7 = bf16[1024,4096]{1,0:T(8,128)(2,1)} custom-call(bf16[2048,2048]{1,0:T(8,128)(2,1)} %get-tuple-element.78.y_ref, bf16[1024,2048]{1,0:T(8,128)(2,1)} %copy-done.6, bf16[2048,4096]{1,0:T(8,128)(2,1)} %w_ref.7, bf16[1024,4096]{1,0:T(8,128)(2,1)} %all-gather.3.cloned.1.call-done.wr0_ref, ...), custom_call_target="tpu_custom_call", output_to_operand_aliasing={{}: (7, {})} | custom-call | flops 16896000000 | bytes 51200000 | tf_op jit(solution)/shard_map/out_proj/pallas_call | solution.py:601
  (71 shorter events, 19.4 us)
Async XLA Ops:
  6.5 553.3 %all-gather.3.cloned.1.call-start = ((), (), s32[]{:S(2)}) async-start(), calls=%async_computation | async-start | bytes 9437184 | tf_op jit(solution)/shard_map/all_gather | solution.py:641
  25.9 31.3 %collective-permute-start = (bf16[1024,4096]{1,0:T(8,128)(2,1)}, bf16[1024,4096]{1,0:T(8,128)(2,1)}, u32[]{:S(2)}, u32[]{:S(2)}) collective-permute-start(bf16[1024,4096]{1,0:T(8,128)(2,1)} %refs_0_.5), channel_id=1, source_target_pairs={{0,1},{1,0},{2,3},{3,2},{4,5},{5,4},{6,7},{7,6},{8,9},{9,8},{10,11... | collective-permute-start | bytes 25165832 | tf_op jit(solution)/shard_map/ppermute | solution.py:614
  26.3 121.8 %collective-permute-start.8 = (bf16[128,4096]{1,0:T(8,128)(2,1)S(1)}, bf16[128,4096]{1,0:T(8,128)(2,1)}, u32[]{:S(2)}, u32[]{:S(2)}) collective-permute-start(bf16[128,4096]{1,0:T(8,128)(2,1)S(1)} %get-tuple-element.83), channel_id=1, source_target_pairs={{0,2},{1,3},{2,0},{3,1},{4,6},{5,7},{6,4},{7,5},{8,10},{9,11},{10,... | collective-permute-start | bytes 3145736 | tf_op jit(solution)/shard_map/ppermute | solution.py:614
  49.5 5.1 copy-start.8
  49.5 5.1 copy-start.11
  49.5 5.1 copy-start.10
  49.6 5.8 copy-start.12
  49.6 5.8 copy-start.13
  49.6 7.0 copy-start.7
  148.2 411.7 %all-gather.5.cloned.1.call-start = ((), (), s32[]{:S(2)}) async-start(), calls=%async_computation.1 | async-start | bytes 9437184 | tf_op jit(solution)/shard_map/all_gather | solution.py:641
  148.4 93.0 %collective-permute-start.2 = (bf16[512,4096]{1,0:T(8,128)(2,1)}, bf16[512,4096]{1,0:T(8,128)(2,1)}, u32[]{:S(2)}, u32[]{:S(2)}) collective-permute-start(bf16[512,4096]{1,0:T(8,128)(2,1)} %copy-done.2), channel_id=1, source_target_pairs={{0,2},{1,3},{2,0},{3,1},{4,6},{5,7},{6,4},{7,5},{8,10},{9,11},{10,... | collective-permute-start | bytes 12582920 | tf_op jit(solution)/shard_map/ppermute | solution.py:614
  241.4 31.2 %collective-permute-start.3 = (bf16[512,4096]{1,0:T(8,128)(2,1)}, bf16[512,4096]{1,0:T(8,128)(2,1)}, u32[]{:S(2)}, u32[]{:S(2)}) collective-permute-start(bf16[512,4096]{1,0:T(8,128)(2,1)} %collective-permute-done.2.refs_1_.refs_0_), channel_id=1, source_target_pairs={{0,1},{1,0},{2,3},{3,2},{4,5},{5,4},{6,7},{7,6},{8,9},{9,8},{10,11... | collective-permute-start | bytes 12582920 | tf_op jit(solution)/shard_map/ppermute | solution.py:614
  241.4 60.0 %collective-permute-start.1 = (bf16[256,4096]{1,0:T(8,128)(2,1)}, bf16[256,4096]{1,0:T(8,128)(2,1)}, u32[]{:S(2)}, u32[]{:S(2)}) collective-permute-start(bf16[256,4096]{1,0:T(8,128)(2,1)} %copy-done.4), channel_id=1, source_target_pairs={{0,2},{1,3},{2,0},{3,1},{4,6},{5,7},{6,4},{7,5},{8,10},{9,11},{10,... | collective-permute-start | bytes 6291464 | tf_op jit(solution)/shard_map/ppermute | solution.py:614
  243.1 91.6 %collective-permute-start.4 = (bf16[256,4096]{1,0:T(8,128)(2,1)}, bf16[256,4096]{1,0:T(8,128)(2,1)}, u32[]{:S(2)}, u32[]{:S(2)}) collective-permute-start(bf16[256,4096]{1,0:T(8,128)(2,1)} %copy-done.3), channel_id=1, source_target_pairs={{0,2},{1,3},{2,0},{3,1},{4,6},{5,7},{6,4},{7,5},{8,10},{9,11},{10,... | collective-permute-start | bytes 6291464 | tf_op jit(solution)/shard_map/ppermute | solution.py:614
  301.4 53.8 %collective-permute-start.5 = (bf16[256,4096]{1,0:T(8,128)(2,1)}, bf16[256,4096]{1,0:T(8,128)(2,1)}, u32[]{:S(2)}, u32[]{:S(2)}) collective-permute-start(bf16[256,4096]{1,0:T(8,128)(2,1)} %collective-permute-done.1.refs_1_.refs_0_), channel_id=1, source_target_pairs={{0,1},{1,0},{2,3},{3,2},{4,5},{5,4},{6,7},{7,6},{8,9},{9,8},{10,11... | collective-permute-start | bytes 6291464 | tf_op jit(solution)/shard_map/ppermute | solution.py:614
  334.7 20.5 %collective-permute-start.6 = (bf16[256,4096]{1,0:T(8,128)(2,1)}, bf16[256,4096]{1,0:T(8,128)(2,1)}, u32[]{:S(2)}, u32[]{:S(2)}) collective-permute-start(bf16[256,4096]{1,0:T(8,128)(2,1)} %collective-permute-done.4.refs_1_.refs_2_), channel_id=1, source_target_pairs={{0,1},{1,0},{2,3},{3,2},{4,5},{5,4},{6,7},{7,6},{8,9},{9,8},{10,11... | collective-permute-start | bytes 6291464 | tf_op jit(solution)/shard_map/ppermute | solution.py:614
  334.7 87.5 %collective-permute-start.9 = (bf16[128,4096]{1,0:T(8,128)(2,1)}, bf16[128,4096]{1,0:T(8,128)(2,1)}, u32[]{:S(2)}, u32[]{:S(2)}) collective-permute-start(bf16[128,4096]{1,0:T(8,128)(2,1)} %get-tuple-element.85), channel_id=1, source_target_pairs={{0,2},{1,3},{2,0},{3,1},{4,6},{5,7},{6,4},{7,5},{8,10},{9,11},{10,... | collective-permute-start | bytes 3145736 | tf_op jit(solution)/shard_map/ppermute | solution.py:614
  384.4 37.8 %copy-start.9 = (bf16[2048]{0:T(1024)(128)(2,1)S(1)}, bf16[2048]{0:T(1024)(128)(2,1)}, u32[]{:S(2)}) copy-start(bf16[2048]{0:T(1024)(128)(2,1)} %param.26) | copy-start | bytes 12292
  384.4 37.8 %copy-start.14 = (f32[32]{0:T(128)S(1)}, f32[32]{0:T(128)}, u32[]{:S(2)}) copy-start(f32[32]{0:T(128)} %param.25) | copy-start | bytes 388
  467.3 117.2 %collective-permute-start.10 = (bf16[512,2048]{1,0:T(8,128)(2,1)}, bf16[512,2048]{1,0:T(8,128)(2,1)S(1)}, u32[]{:S(2)}, u32[]{:S(2)}) collective-permute-start(bf16[512,2048]{1,0:T(8,128)(2,1)} %get-tuple-element.91), channel_id=1, source_target_pairs={{0,2},{1,3},{2,0},{3,1},{4,6},{5,7},{6,4},{7,5},{8,10},{9,11},{10,... | collective-permute-start | bytes 6291464 | tf_op jit(solution)/shard_map/ppermute | solution.py:614
  468.1 91.8 %collective-permute-start.12 = (bf16[512,2048]{1,0:T(8,128)(2,1)}, bf16[512,2048]{1,0:T(8,128)(2,1)}, u32[]{:S(2)}, u32[]{:S(2)}) collective-permute-start(bf16[512,2048]{1,0:T(8,128)(2,1)} %get-tuple-element.92), channel_id=1, source_target_pairs={{0,2},{1,3},{2,0},{3,1},{4,6},{5,7},{6,4},{7,5},{8,10},{9,11},{10,... | collective-permute-start | bytes 6291464 | tf_op jit(solution)/shard_map/ppermute | solution.py:614
  584.5 157.1 %collective-permute-start.13 = (f32[512,4096]{1,0:T(8,128)}, f32[512,4096]{1,0:T(8,128)}, u32[]{:S(2)}, u32[]{:S(2)}) collective-permute-start(f32[512,4096]{1,0:T(8,128)} %out_proj.5), channel_id=1, source_target_pairs={{0,1},{1,0},{2,3},{3,2},{4,5},{5,4},{6,7},{7,6},{8,9},{9,8},{10,11... | collective-permute-start | bytes 25165832 | tf_op jit(solution)/shard_map/ppermute | solution.py:614
  610.2 159.1 %collective-permute-start.11 = (f32[512,4096]{1,0:T(8,128)}, f32[512,4096]{1,0:T(8,128)}, u32[]{:S(2)}, u32[]{:S(2)}) collective-permute-start(f32[512,4096]{1,0:T(8,128)} %out_proj.4), channel_id=1, source_target_pairs={{0,1},{1,0},{2,3},{3,2},{4,5},{5,4},{6,7},{7,6},{8,9},{9,8},{10,11... | collective-permute-start | bytes 25165832 | tf_op jit(solution)/shard_map/ppermute | solution.py:614
  648.8 92.8 %collective-permute-start.7 = (bf16[1024,2048]{1,0:T(8,128)(2,1)}, bf16[1024,2048]{1,0:T(8,128)(2,1)S(1)}, u32[]{:S(2)}, u32[]{:S(2)}) collective-permute-start(bf16[1024,2048]{1,0:T(8,128)(2,1)} %get-tuple-element.82), channel_id=1, source_target_pairs={{0,2},{1,3},{2,0},{3,1},{4,6},{5,7},{6,4},{7,5},{8,10},{9,11},{10,... | collective-permute-start | bytes 12582920 | tf_op jit(solution)/shard_map/ppermute | solution.py:614
  (8 other events, 10.2 us)
Sparse Core Ops, SparseCore 0:
  148.3 123.0 all-gather.2
  422.4 121.5 all-gather.4

commit v6 on v5

--- a/solution.py
+++ b/solution.py
@@ -174,7 +174,7 @@
                 def _():
                     for c in copies(k):
                         c.wait()
-            bbuf[:, 0:NB] = jnp.dot(xbuf[m], wb_ref[...], preferred_element_type=f32).astype(bf16).astype(f32)
+            bbuf[:, :NB] = jnp.dot(xbuf[m], wb_ref[...], preferred_element_type=f32).astype(bf16).astype(f32)
             bbuf[:, NB:NB + HEADS] = mac(xbuf[m], wdt_ref[...], 1, 1).astype(bf16).astype(f32)
             x_dot(m)
             setup(m, m // per, lax.rem(m, per))
@@ -244,9 +244,9 @@
     )(pre, *srcs, *[aux] * nx, w2, wb, wdt, *consts, *([] if cin is None else [cin]), *into)
 
 
-def mixz_kernel(pre, *refs, ns, first):
+def mixz_kernel(pre, *refs, ns, first, n_out):
     xs_, auxs = refs[:ns], refs[ns:2 * ns]
-    (xa_ref, bg_ref, cg_ref, dc_ref, wz_ref, cin_ref, hp_ref, yn_ref, cout_ref, xv, av, zbuf, ybuf, xw, state) = refs[2 * ns:]
+    (xa_ref, bg_ref, cg_ref, dc_ref, wz_ref, cin_ref, hp_ref, *yn_refs, cout_ref, xv, av, zbuf, ybuf, xw, state, ynbuf) = refs[2 * ns:]
     g, i, tile = pl.program_id(0), pl.program_id(1), pl.program_id(2)
     n_tiles = pl.num_programs(2)
 
@@ -255,6 +255,7 @@
         state[...] = cin_ref[0]
 
     at = i * n_tiles + tile
+    yn = yn_refs[0] if n_out == 1 else ynbuf
     for k in range(ns):
         @pl.when((at >= first[k]) & (at < first[k + 1]))
         def _():
@@ -296,7 +297,7 @@
             dtp = pair_bcast(dc, HEADS // 2 + p)
             last = cump[T - 1:T, :]
             xw[:, cs] = (xaf * (jnp.exp2(last - cump) * dtp * k_end)).astype(bf16)
-            y = y + ybuf[:, cs] * (jnp.exp2(cump) * k_in) + hp_ref[0:1, cs] * xaf
+            y = y + ybuf[:, cs] * (jnp.exp2(cump) * k_in) + hp_ref[:1, cs] * xaf
             v = y * silu(zbuf[rs, cs])
             ybuf[:, cs] = v
             sq = sq + v * v
@@ -305,15 +306,21 @@
         r = jnp.broadcast_to(lax.rsqrt(ms + NORM_EPS), (T, T))
         for p in range(GW // T):
             cs = slice(p * T, (p + 1) * T)
-            yn_ref[rs, cs] = (ybuf[:, cs] * r * hp_ref[1:2, cs]).astype(bf16)
+            yn[rs, cs] = (ybuf[:, cs] * r * hp_ref[1:2, cs]).astype(bf16)
         state[...] = state[...] + mac(bg, xw[...], 0, 0)
 
+    if n_out > 1:
+        for k in range(n_out):
+            @pl.when(tile // (n_tiles // n_out) == k)
+            def _():
+                yn_refs[k][...] = ynbuf[...]
+
     @pl.when(tile == n_tiles - 1)
     def _():
         cout_ref[0] = state[...]
 
 
-def mixz_call(pre, aux, amaps, xs, arrs, w2, cin, hp, *, nx, per, ofs, cofs):
+def mixz_call(pre, aux, amaps, xs, arrs, w2, cin, hp, *, nx, per, ofs, cofs, n_out=1):
     ns = len(xs)
     first = [0]
     for v in xs:
@@ -328,14 +335,17 @@
     in_specs += [pl.BlockSpec((MT // T, SUB, T), lambda g, i, t, b, k=k: (amaps[k](b) + piece(k)(i, t), 0, 0)) for k in range(ns)]
     same = lambda g: g
     in_specs += [rows(GW, same), rows(T, same), rows(T, lambda g: 2 + g), rows(T, lambda g: 0), cols(D), state(cofs), cols(8)]
+    po = per // n_out
+    outs = [rows(GW, same, 0)] if n_out == 1 else [
+        pl.BlockSpec((MT, GW), lambda g, i, t, b, k=k: (jnp.clip(t - k * po, 0, po - 1), g)) for k in range(n_out)]
     gs = pltpu.PrefetchScalarGridSpec(
-        num_scalar_prefetch=1, grid=(2, nx, per), in_specs=in_specs, out_specs=[rows(GW, same, 0), state(0)],
+        num_scalar_prefetch=1, grid=(2, nx, per), in_specs=in_specs, out_specs=outs + [state(0)],
         scratch_shapes=[pltpu.VMEM((MT, D), bf16), pltpu.VMEM((MT // T, SUB, T), f32), pltpu.VMEM((MT, GW), f32), pltpu.VMEM((T, GW), f32),
-                        pltpu.VMEM((T, GW), bf16), pltpu.VMEM((T, GW), f32)],
+                        pltpu.VMEM((T, GW), bf16), pltpu.VMEM((T, GW), f32), pltpu.VMEM((MT if n_out > 1 else HALO, GW), bf16)],
     )
     return pl.pallas_call(
-        functools.partial(mixz_kernel, ns=ns, first=first), grid_spec=gs,
-        out_shape=[jax.ShapeDtypeStruct((n, XW), bf16), jax.ShapeDtypeStruct((nx, T, XW), f32)],
+        functools.partial(mixz_kernel, ns=ns, first=first, n_out=n_out), grid_spec=gs,
+        out_shape=[jax.ShapeDtypeStruct((n // n_out, XW), bf16)] * n_out + [jax.ShapeDtypeStruct((nx, T, XW), f32)],
         compiler_params=pltpu.CompilerParams(dimension_semantics=("arbitrary",) * 3, vmem_limit_bytes=60 * MIB),
         cost_estimate=pl.CostEstimate(flops=n * 20_000_000, bytes_accessed=n * 14000, transcendentals=n * 10000),
         name="mixz",
@@ -476,7 +486,7 @@
     )(seg.reshape(rows // T, T), x, x, w)
 
 
-CW = 256
+CW = 128
 
 
 def chain_kernel(n_blocks, e01_ref, e2_ref, e3_ref, out_hbm, ebuf, sbuf, obuf, out_ref, lsem, osem, send_sem, recv_sem):
@@ -573,7 +583,7 @@
 def out_kernel(y_ref, yr_ref, w_ref, wr0_ref, wr1_ref, *refs):
     h = XW // 2
     acc = (jnp.dot(y_ref[...], w_ref[...], preferred_element_type=f32)
-           + jnp.dot(yr_ref[:, 0:h], wr0_ref[...], preferred_element_type=f32)
+           + jnp.dot(yr_ref[:, :h], wr0_ref[...], preferred_element_type=f32)
            + jnp.dot(yr_ref[:, h:], wr1_ref[...], preferred_element_type=f32))
     if len(refs) > 1:
         x_ref, other_ref = refs[:2]
@@ -677,20 +687,18 @@
             return mixz_call(pre, aux, amaps, xs, arrs, w2, start, hp2, **kw)
 
         at = lambda s, k=0: (lambda b: b[s] * per + k)
-        yn, c = mix([at(3)], x_fwd[:1], rem3, starts, nx=1, per=kper, ofs=0, cofs=3)
+        yn, c = mix([at(3), at(3, 2), at(3, 3)], x_fwd, rem3, starts, nx=1, per=per, ofs=0, cofs=3)
         y_in = [send(yn, CHIP_SWAP)]
-        yn, c = mix([at(3, 2), at(3, 3)], x_fwd[1:], rem3, c, nx=1, per=kper, ofs=kper, cofs=0)
-        y_in.append(send(yn, CHIP_SWAP))
-        yn, c = mix([at(2), at(2, 2), at(2, 3)], x_dir, rem2, after(starts, c), nx=1, per=per, ofs=0, cofs=2)
-        y_in.append(send(yn, CHIP_SWAP))
+        *yn, c = mix([at(2), at(2, 2), at(2, 3)], x_dir, rem2, after(starts, c), nx=1, per=per, ofs=0, cofs=2, n_out=NCH)
+        y_in += [send(v, CHIP_SWAP) for v in yn]
         y_own, _ = mix([at(0), at(1)], [x_loc, x_par], own, after(starts, c), nx=2, per=per, ofs=0, cofs=0)
         other = []
         for k in range(NCH):
-            part = out_call(1, k, y_own, y_in[k], 0, w_out, w_rem)
+            part = out_call(1, k, y_own, y_in[0], k, w_out, w_rem)
             other.append(send(part, CORE_SWAP))
         y = None
         for k in range(NCH):
-            y = out_call(0, k, y_own, y_in[2], k, w_out, w_rem, x_loc, other[k], y)
+            y = out_call(0, k, y_own, y_in[k + 1], 0, w_out, w_rem, x_loc, other[k], y)
         return y
 
     return jax.shard_map(body, mesh=mesh, in_specs=(token_spec, seg_spec) + weight_specs, out_specs=token_spec, check_vma=False)

time: 809 us -> 773 us (0.956)
  the two profiles are of different devices: /device:TPU:26 before, /device:TPU:0 now
where the time goes in v6:
time: 773 us; the launch traced here: 761 us
  Pallas kernels  503 us (65%)
  waiting for transfers between devices  194 us (25%)
  local copies, waits for them, and re-layouts  38 us (5%)
  between operations  13.9 us (2%)
  starting transfers between devices  9.25 us (1%)
    pallas_call x6, Pallas kernels, front_call(): pl.pallas_call(functools.partial(front_kernel, nx=nx, per=per, where=wher...  216 us
    ppermute x14, waiting for transfers between devices, send(): return lax.ppermute(v, 'tp', perm)  193 us
    pallas_call x3, Pallas kernels, mixz_call(): pl.pallas_call(functools.partial(mixz_kernel, ns=ns, first=first, n_out=n...  146 us
    pallas_call x4, Pallas kernels, out_call(): pl.pallas_call(out_kernel, grid=(D // NT,), in_specs=specs, out_specs=pl....  100 us
    unnamed x36, local copies, waits for them, and re-layouts  37.8 us
    pallas_call x1, Pallas kernels, chain_call(): pl.pallas_call(functools.partial(chain_kernel, n_blocks), in_specs=[hbm]...  29 us
  transfers between devices with their start and end apart: 16, of which 6 were waited for; matrix products, arithmetic and copies ran while one was open for 4% of the time, Pallas kernels for 58%

profile of v6, /device:TPU:0, one launch (start us, length us, event | category | flops | bytes accessed | tf_op | source)
XLA Modules:
  0.0 761.3 jit_solution(15986772528674087826)
XLA Ops:
  7.2 11.7 %ahead.1 = (f32[32,8,128]{2,1,0:T(8,128)S(1)}, bf16[5,16,4096]{2,1,0:T(8,128)(2,1)S(1)}, bf16[512,4096]{1,0:T(8,128)(2,1)S(1)}, bf16[256,4096]{1,0:T(8,128)(2,1)...) custom-call(s32[8,128]{1,0:T(8,128)S(1)} %bitcast.19, ...), custom_call_target="tpu_custom_call" | custom-call | tf_op jit(solution)/shard_map/ahead/pallas_call | solution.py:476
  19.6 2.0 copy-done.2
  26.4 23.2 %copy.25 = bf16[512,8,2,2048]{3,1,2,0:T(8,128)(2,1)} copy(bf16[512,8,2,2048]{3,2,1,0:T(2,128)(2,1)} %bitcast.39) | data formatting | bytes 67108864
  49.6 5.0 copy.26
  57.2 90.9 %front.6 = (bf16[2048,2048]{1,0:T(8,128)(2,1)}, bf16[2048,512]{1,0:T(8,128)(2,1)}, f32[2048,128]{1,0:T(8,128)}, f32[2,136,2048]{2,1,0:T(8,128)}) custom-call(s32[4]{0:T(128)} %pad_add_fusion.pre, bf16[80,4096]{1,0:T(8,128)(2,1)} %bitcast.20, bf16[1024,4096]{1,0:T(8,128)(2,1)} %refs_0_.5, bf16[80,4096]{1,0:T(8,128)(2,1)} %bitcast.21, ...), custom_call_target="tpu_custom_call" | custom-call | flops 51200000000 | bytes 20480000 | tf_op jit(solution)/shard_map/front/pallas_call | solution.py:236
  149.1 91.9 %collective-permute-done.2.refs_1_.refs_0_ = bf16[512,4096]{1,0:T(8,128)(2,1)} collective-permute-done((bf16[512,4096]{1,0:T(8,128)(2,1)}, bf16[512,4096]{1,0:T(8,128)(2,1)}, u32[]{:S(2)}, u32[]{:S(2)}) %collective-permute-start.2) | collective-permute-done | bytes 4194336 | tf_op jit(solution)/shard_map/ppermute | solution.py:624
  243.0 28.8 %front.7 = (bf16[1024,2048]{1,0:T(8,128)(2,1)}, bf16[1024,512]{1,0:T(8,128)(2,1)}, f32[1024,128]{1,0:T(8,128)}, f32[1,136,2048]{2,1,0:T(8,128)}) custom-call(s32[4]{0:T(128)} %pad_add_fusion.pre, bf16[80,4096]{1,0:T(8,128)(2,1)} %bitcast.22, bf16[512,4096]{1,0:T(8,128)(2,1)} %collective-permute-done.2.refs_1_.refs_0_, f32[32,8,128]{2,1,0:T(8,128)} %copy-done, ...), custom_call_target="tpu_custom_call" | custom-call | flops 12800000000 | bytes 5120000 | tf_op jit(solution)/shard_map/front/pallas_call | solution.py:236
  271.9 28.8 %front.8 = (bf16[1024,2048]{1,0:T(8,128)(2,1)}, bf16[1024,512]{1,0:T(8,128)(2,1)}, f32[1024,128]{1,0:T(8,128)}, f32[1,136,2048]{2,1,0:T(8,128)}) custom-call(s32[4]{0:T(128)} %pad_add_fusion.pre, bf16[80,4096]{1,0:T(8,128)(2,1)} %bitcast.23, bf16[512,4096]{1,0:T(8,128)(2,1)} %collective-permute-done.3.refs_1_.refs_0_, f32[32,8,128]{2,1,0:T(8,128)} %copy-done, ...), custom_call_target="tpu_custom_call" | custom-call | flops 12800000000 | bytes 5120000 | tf_op jit(solution)/shard_map/front/pallas_call | solution.py:236
  300.8 19.0 %front.9 = (bf16[1024,2048]{1,0:T(8,128)(2,1)}, bf16[1024,512]{1,0:T(8,128)(2,1)}, f32[1024,128]{1,0:T(8,128)}, f32[1,136,2048]{2,1,0:T(8,128)}) custom-call(s32[4]{0:T(128)} %pad_add_fusion.pre, bf16[512,4096]{1,0:T(8,128)(2,1)} %collective-permute-done.2.refs_1_.refs_0_, ...), custom_call_target="tpu_custom_call", output_to_operand_aliasing={{0}: (11, {}), {1}: (12, {}), {2}: (13, {})} | custom-call | flops 6400000000 | bytes 2560000 | tf_op jit(solution)/shard_map/front/pallas_call | solution.py:236
  319.9 14.5 %collective-permute-done.4.refs_1_.refs_2_ = bf16[256,4096]{1,0:T(8,128)(2,1)} collective-permute-done((bf16[256,4096]{1,0:T(8,128)(2,1)}, bf16[256,4096]{1,0:T(8,128)(2,1)}, u32[]{:S(2)}, u32[]{:S(2)}) %collective-permute-start.4) | collective-permute-done | bytes 2097184 | tf_op jit(solution)/shard_map/ppermute | solution.py:624
  335.5 18.7 %front.10 = (bf16[1024,2048]{1,0:T(8,128)(2,1)}, bf16[1024,512]{1,0:T(8,128)(2,1)}, f32[1024,128]{1,0:T(8,128)}, f32[1,136,2048]{2,1,0:T(8,128)}) custom-call(s32[4]{0:T(128)} %pad_add_fusion.pre, bf16[256,4096]{1,0:T(8,128)(2,1)} %collective-permute-done.1.refs_1_.refs_0_, ...), custom_call_target="tpu_custom_call", output_to_operand_aliasing={{0}: (11, {}), {1}: (12, {}), {2}: (13, {})} | custom-call | flops 6400000000 | bytes 2560000 | tf_op jit(solution)/shard_map/front/pallas_call | solution.py:236
  354.2 29.4 %front.11 = (bf16[1024,2048]{1,0:T(8,128)(2,1)}, bf16[1024,512]{1,0:T(8,128)(2,1)}, f32[1024,128]{1,0:T(8,128)}, f32[1,136,2048]{2,1,0:T(8,128)}) custom-call(s32[4]{0:T(128)} %pad_add_fusion.pre, bf16[512,4096]{1,0:T(8,128)(2,1)} %collective-permute-done.3.refs_1_.refs_0_, ...), custom_call_target="tpu_custom_call", output_to_operand_aliasing={{0}: (12, {}), {1}: (13, {}), {2}: (14, {})} | custom-call | flops 12800000000 | bytes 5120000 | tf_op jit(solution)/shard_map/front/pallas_call | solution.py:236
  383.7 29.0 %chain.1.refs_9_.refs_11_ = f32[4,128,2048]{2,1,0:T(8,128)} custom-call(f32[2,136,2048]{2,1,0:T(8,128)} %get-tuple-element.54.e01_ref, f32[1,136,2048]{2,1,0:T(8,128)} %get-tuple-element.71.e2_ref, f32[1,136,2048]{2,1,0:T(8,128)} %get-tuple-element.76.e3_ref), custom_call_target="tpu_custom_call" | custom-call | tf_op jit(solution)/shard_map/chain/pallas_call | solution.py:567
  413.5 38.3 %mixz.5 = (bf16[1024,2048]{1,0:T(8,128)(2,1)}, f32[1,128,2048]{2,1,0:T(8,128)}) custom-call(s32[4]{0:T(128)} %pad_add_fusion.pre, bf16[512,4096]{1,0:T(8,128)(2,1)} %collective-permute-done.3.refs_1_.refs_0_, bf16[256,4096]{1,0:T(8,128)(2,1)} %collective-permute-done.5.refs_1_, bf16[256,4096]{1,0:T(8,128)(2,1)} %collective-permute-done.6.refs_2_, ...), custom_call_target="tpu_custom_call" | custom-call | flops 20480000000 | bytes 14336000 | tf_op jit(solution)/shard_map/mixz/pallas_call | solution.py:346
  452.9 68.8 %mixz.3 = (bf16[2048,2048]{1,0:T(8,128)(2,1)}, f32[2,128,2048]{2,1,0:T(8,128)}) custom-call(s32[4]{0:T(128)} %pad_add_fusion.pre, bf16[1024,4096]{1,0:T(8,128)(2,1)} %refs_0_.5, bf16[1024,4096]{1,0:T(8,128)(2,1)} %collective-permute-done.refs_3_.refs_1_, f32[32,8,128]{2,1,0:T(8,128)} %copy-done, f32[32,8,128]{2,1,0:T(8,128)} %copy-done, ...), custom_call_target="tpu_custom_call" | custom-call | flops 40960000000 | bytes 28672000 | tf_op jit(solution)/shard_map/mixz/pallas_call | solution.py:346
  521.7 22.9 %collective-permute-done.10.yr_ref = bf16[1024,2048]{1,0:T(8,128)(2,1)} collective-permute-done((bf16[1024,2048]{1,0:T(8,128)(2,1)}, bf16[1024,2048]{1,0:T(8,128)(2,1)}, u32[]{:S(2)}, u32[]{:S(2)}) %collective-permute-start.10) | collective-permute-done | bytes 4194336 | tf_op jit(solution)/shard_map/ppermute | solution.py:624
  546.1 24.3 %out_proj.5 = f32[512,4096]{1,0:T(8,128)} custom-call(bf16[2048,2048]{1,0:T(8,128)(2,1)} %get-tuple-element.77.y_ref, bf16[1024,2048]{1,0:T(8,128)(2,1)} %collective-permute-done.10.yr_ref, bf16[2048,4096]{1,0:T(8,128)(2,1)} %w_ref.7, bf16[1024,4096]{1,0:T(8,128)(2,1)} %all-gather.3.cloned.1.call-done.wr0_ref, ...), custom_call_target="tpu_custom_call" | custom-call | flops 16896000000 | bytes 51200000 | tf_op jit(solution)/shard_map/out_proj/pallas_call | solution.py:611
  570.4 24.4 %out_proj.4 = f32[512,4096]{1,0:T(8,128)} custom-call(bf16[2048,2048]{1,0:T(8,128)(2,1)} %get-tuple-element.77.y_ref, bf16[1024,2048]{1,0:T(8,128)(2,1)} %collective-permute-done.10.yr_ref, bf16[2048,4096]{1,0:T(8,128)(2,1)} %w_ref.7, bf16[1024,4096]{1,0:T(8,128)(2,1)} %all-gather.3.cloned.1.call-done.wr0_ref, ...), custom_call_target="tpu_custom_call" | custom-call | flops 16896000000 | bytes 51200000 | tf_op jit(solution)/shard_map/out_proj/pallas_call | solution.py:611
  595.3 39.0 %mixz.4 = (bf16[512,2048]{1,0:T(8,128)(2,1)}, bf16[512,2048]{1,0:T(8,128)(2,1)}, f32[1,128,2048]{2,1,0:T(8,128)}) custom-call(s32[4]{0:T(128)} %pad_add_fusion.pre, bf16[512,4096]{1,0:T(8,128)(2,1)} %collective-permute-done.2.refs_1_.refs_0_, bf16[256,4096]{1,0:T(8,128)(2,1)} %collective-permute-done.1.refs_1_.refs_0_, ...), custom_call_target="tpu_custom_call" | custom-call | flops 20480000000 | bytes 14336000 | tf_op jit(solution)/shard_map/mixz/pallas_call | solution.py:346
  634.3 1.5 collective-permute-start.12
  636.4 46.7 %collective-permute-done.12.yr_ref = bf16[512,2048]{1,0:T(8,128)(2,1)S(1)} collective-permute-done((bf16[512,2048]{1,0:T(8,128)(2,1)}, bf16[512,2048]{1,0:T(8,128)(2,1)S(1)}, u32[]{:S(2)}, u32[]{:S(2)}) %collective-permute-start.12) | collective-permute-done | bytes 2097184 | tf_op jit(solution)/shard_map/ppermute | solution.py:624
  684.5 25.8 %out_proj.6.refs_2_ = bf16[1024,4096]{1,0:T(8,128)(2,1)} custom-call(bf16[2048,2048]{1,0:T(8,128)(2,1)} %get-tuple-element.77.y_ref, bf16[512,2048]{1,0:T(8,128)(2,1)} %copy-done.7, bf16[2048,4096]{1,0:T(8,128)(2,1)} %w_ref.7, bf16[1024,4096]{1,0:T(8,128)(2,1)} %all-gather.3.cloned.1.call-done.wr0_ref, ...), custom_call_target="tpu_custom_call" | custom-call | flops 16896000000 | bytes 51200000 | tf_op jit(solution)/shard_map/out_proj/pallas_call | solution.py:611
  710.2 16.8 %collective-permute-done.7.yr_ref = bf16[512,2048]{1,0:T(8,128)(2,1)S(1)} collective-permute-done((bf16[512,2048]{1,0:T(8,128)(2,1)}, bf16[512,2048]{1,0:T(8,128)(2,1)S(1)}, u32[]{:S(2)}, u32[]{:S(2)}) %collective-permute-start.7) | collective-permute-done | bytes 2097184 | tf_op jit(solution)/shard_map/ppermute | solution.py:624
  728.4 25.8 %out_proj.7 = bf16[1024,4096]{1,0:T(8,128)(2,1)} custom-call(bf16[2048,2048]{1,0:T(8,128)(2,1)} %get-tuple-element.77.y_ref, bf16[512,2048]{1,0:T(8,128)(2,1)} %copy-done.6, bf16[2048,4096]{1,0:T(8,128)(2,1)} %w_ref.7, bf16[1024,4096]{1,0:T(8,128)(2,1)} %all-gather.3.cloned.1.call-done.wr0_ref, ...), custom_call_target="tpu_custom_call", output_to_operand_aliasing={{}: (7, {})} | custom-call | flops 16896000000 | bytes 51200000 | tf_op jit(solution)/shard_map/out_proj/pallas_call | solution.py:611
  (70 shorter events, 20.1 us)
Async XLA Ops:
  6.5 538.1 %all-gather.3.cloned.1.call-start = ((), (), s32[]{:S(2)}) async-start(), calls=%async_computation | async-start | bytes 9437184 | tf_op jit(solution)/shard_map/all_gather | solution.py:651
  25.1 32.1 %collective-permute-start = (bf16[1024,4096]{1,0:T(8,128)(2,1)}, bf16[1024,4096]{1,0:T(8,128)(2,1)}, u32[]{:S(2)}, u32[]{:S(2)}) collective-permute-start(bf16[1024,4096]{1,0:T(8,128)(2,1)} %refs_0_.5), channel_id=1, source_target_pairs={{0,1},{1,0},{2,3},{3,2},{4,5},{5,4},{6,7},{7,6},{8,9},{9,8},{10,11... | collective-permute-start | bytes 25165832 | tf_op jit(solution)/shard_map/ppermute | solution.py:624
  25.1 123.0 %collective-permute-start.8 = (bf16[128,4096]{1,0:T(8,128)(2,1)S(1)}, bf16[128,4096]{1,0:T(8,128)(2,1)}, u32[]{:S(2)}, u32[]{:S(2)}) collective-permute-start(bf16[128,4096]{1,0:T(8,128)(2,1)S(1)} %get-tuple-element.82), channel_id=1, source_target_pairs={{0,2},{1,3},{2,0},{3,1},{4,6},{5,7},{6,4},{7,5},{8,10},{9,11},{10,... | collective-permute-start | bytes 3145736 | tf_op jit(solution)/shard_map/ppermute | solution.py:624
  49.6 5.1 copy-start.9
  49.6 5.1 copy-start.11
  49.6 5.1 copy-start.12
  49.6 5.7 copy-start.13
  49.6 5.7 copy-start.14
  49.6 6.9 copy-start.8
  148.1 398.0 %all-gather.5.cloned.1.call-start = ((), (), s32[]{:S(2)}) async-start(), calls=%async_computation.1 | async-start | bytes 9437184 | tf_op jit(solution)/shard_map/all_gather | solution.py:651
  148.3 92.7 %collective-permute-start.2 = (bf16[512,4096]{1,0:T(8,128)(2,1)}, bf16[512,4096]{1,0:T(8,128)(2,1)}, u32[]{:S(2)}, u32[]{:S(2)}) collective-permute-start(bf16[512,4096]{1,0:T(8,128)(2,1)} %copy-done.2), channel_id=1, source_target_pairs={{0,2},{1,3},{2,0},{3,1},{4,6},{5,7},{6,4},{7,5},{8,10},{9,11},{10,... | collective-permute-start | bytes 12582920 | tf_op jit(solution)/shard_map/ppermute | solution.py:624
  241.0 30.9 %collective-permute-start.3 = (bf16[512,4096]{1,0:T(8,128)(2,1)}, bf16[512,4096]{1,0:T(8,128)(2,1)}, u32[]{:S(2)}, u32[]{:S(2)}) collective-permute-start(bf16[512,4096]{1,0:T(8,128)(2,1)} %collective-permute-done.2.refs_1_.refs_0_), channel_id=1, source_target_pairs={{0,1},{1,0},{2,3},{3,2},{4,5},{5,4},{6,7},{7,6},{8,9},{9,8},{10,11... | collective-permute-start | bytes 12582920 | tf_op jit(solution)/shard_map/ppermute | solution.py:624
  241.0 59.7 %collective-permute-start.1 = (bf16[256,4096]{1,0:T(8,128)(2,1)}, bf16[256,4096]{1,0:T(8,128)(2,1)}, u32[]{:S(2)}, u32[]{:S(2)}) collective-permute-start(bf16[256,4096]{1,0:T(8,128)(2,1)} %copy-done.4), channel_id=1, source_target_pairs={{0,2},{1,3},{2,0},{3,1},{4,6},{5,7},{6,4},{7,5},{8,10},{9,11},{10,... | collective-permute-start | bytes 6291464 | tf_op jit(solution)/shard_map/ppermute | solution.py:624
  242.2 92.2 %collective-permute-start.4 = (bf16[256,4096]{1,0:T(8,128)(2,1)}, bf16[256,4096]{1,0:T(8,128)(2,1)}, u32[]{:S(2)}, u32[]{:S(2)}) collective-permute-start(bf16[256,4096]{1,0:T(8,128)(2,1)} %copy-done.3), channel_id=1, source_target_pairs={{0,2},{1,3},{2,0},{3,1},{4,6},{5,7},{6,4},{7,5},{8,10},{9,11},{10,... | collective-permute-start | bytes 6291464 | tf_op jit(solution)/shard_map/ppermute | solution.py:624
  300.8 53.4 %collective-permute-start.5 = (bf16[256,4096]{1,0:T(8,128)(2,1)}, bf16[256,4096]{1,0:T(8,128)(2,1)}, u32[]{:S(2)}, u32[]{:S(2)}) collective-permute-start(bf16[256,4096]{1,0:T(8,128)(2,1)} %collective-permute-done.1.refs_1_.refs_0_), channel_id=1, source_target_pairs={{0,1},{1,0},{2,3},{3,2},{4,5},{5,4},{6,7},{7,6},{8,9},{9,8},{10,11... | collective-permute-start | bytes 6291464 | tf_op jit(solution)/shard_map/ppermute | solution.py:624
  334.3 19.9 %collective-permute-start.6 = (bf16[256,4096]{1,0:T(8,128)(2,1)}, bf16[256,4096]{1,0:T(8,128)(2,1)}, u32[]{:S(2)}, u32[]{:S(2)}) collective-permute-start(bf16[256,4096]{1,0:T(8,128)(2,1)} %collective-permute-done.4.refs_1_.refs_2_), channel_id=1, source_target_pairs={{0,1},{1,0},{2,3},{3,2},{4,5},{5,4},{6,7},{7,6},{8,9},{9,8},{10,11... | collective-permute-start | bytes 6291464 | tf_op jit(solution)/shard_map/ppermute | solution.py:624
  334.3 78.3 %collective-permute-start.9 = (bf16[128,4096]{1,0:T(8,128)(2,1)}, bf16[128,4096]{1,0:T(8,128)(2,1)}, u32[]{:S(2)}, u32[]{:S(2)}) collective-permute-start(bf16[128,4096]{1,0:T(8,128)(2,1)} %get-tuple-element.84), channel_id=1, source_target_pairs={{0,2},{1,3},{2,0},{3,1},{4,6},{5,7},{6,4},{7,5},{8,10},{9,11},{10,... | collective-permute-start | bytes 3145736 | tf_op jit(solution)/shard_map/ppermute | solution.py:624
  383.6 29.0 %copy-start.15 = (f32[32]{0:T(128)S(1)}, f32[32]{0:T(128)}, u32[]{:S(2)}) copy-start(f32[32]{0:T(128)} %param.25) | copy-start | bytes 388
  383.6 29.2 %copy-start.10 = (bf16[2048]{0:T(1024)(128)(2,1)S(1)}, bf16[2048]{0:T(1024)(128)(2,1)}, u32[]{:S(2)}) copy-start(bf16[2048]{0:T(1024)(128)(2,1)} %param.26) | copy-start | bytes 12292
  451.8 92.9 %collective-permute-start.10 = (bf16[1024,2048]{1,0:T(8,128)(2,1)}, bf16[1024,2048]{1,0:T(8,128)(2,1)}, u32[]{:S(2)}, u32[]{:S(2)}) collective-permute-start(bf16[1024,2048]{1,0:T(8,128)(2,1)} %get-tuple-element.89), channel_id=1, source_target_pairs={{0,2},{1,3},{2,0},{3,1},{4,6},{5,7},{6,4},{7,5},{8,10},{9,11},{10,... | collective-permute-start | bytes 12582920 | tf_op jit(solution)/shard_map/ppermute | solution.py:624
  570.4 112.7 %collective-permute-start.13 = (f32[512,4096]{1,0:T(8,128)}, f32[512,4096]{1,0:T(8,128)}, u32[]{:S(2)}, u32[]{:S(2)}) collective-permute-start(f32[512,4096]{1,0:T(8,128)} %out_proj.5), channel_id=1, source_target_pairs={{0,1},{1,0},{2,3},{3,2},{4,5},{5,4},{6,7},{7,6},{8,9},{9,8},{10,11... | collective-permute-start | bytes 25165832 | tf_op jit(solution)/shard_map/ppermute | solution.py:624
  594.8 132.3 %collective-permute-start.11 = (f32[512,4096]{1,0:T(8,128)}, f32[512,4096]{1,0:T(8,128)}, u32[]{:S(2)}, u32[]{:S(2)}) collective-permute-start(f32[512,4096]{1,0:T(8,128)} %out_proj.4), channel_id=1, source_target_pairs={{0,1},{1,0},{2,3},{3,2},{4,5},{5,4},{6,7},{7,6},{8,9},{9,8},{10,11... | collective-permute-start | bytes 25165832 | tf_op jit(solution)/shard_map/ppermute | solution.py:624
  634.3 48.8 %collective-permute-start.12 = (bf16[512,2048]{1,0:T(8,128)(2,1)}, bf16[512,2048]{1,0:T(8,128)(2,1)S(1)}, u32[]{:S(2)}, u32[]{:S(2)}) collective-permute-start(bf16[512,2048]{1,0:T(8,128)(2,1)} %get-tuple-element.90), channel_id=1, source_target_pairs={{0,2},{1,3},{2,0},{3,1},{4,6},{5,7},{6,4},{7,5},{8,10},{9,11},{10,... | collective-permute-start | bytes 6291464 | tf_op jit(solution)/shard_map/ppermute | solution.py:624
  635.8 91.2 %collective-permute-start.7 = (bf16[512,2048]{1,0:T(8,128)(2,1)}, bf16[512,2048]{1,0:T(8,128)(2,1)S(1)}, u32[]{:S(2)}, u32[]{:S(2)}) collective-permute-start(bf16[512,2048]{1,0:T(8,128)(2,1)} %get-tuple-element.81), channel_id=1, source_target_pairs={{0,2},{1,3},{2,0},{3,1},{4,6},{5,7},{6,4},{7,5},{8,10},{9,11},{10,... | collective-permute-start | bytes 6291464 | tf_op jit(solution)/shard_map/ppermute | solution.py:624
  (8 other events, 9.6 us)
Sparse Core Ops, SparseCore 0:
  148.2 127.5 all-gather.2
  412.8 133.2 all-gather.4
